TPU v7x, 16 devices: a whole 2x2x2 slice. The times are simulated.
16 devices in a mesh: dp: 2 (over z), tp: 8 (over y, x, core).
Axes of the slice: x: 2, y: 2, z: 2, core: 2. Of those that a mesh axis runs over, the one named last changes fastest.
Arguments:
- x_norm: bfloat16 [2048, 4096], P(('dp', 'tp')), parts along dimension 0
- w_gate: bfloat16 [4096, 11008], P(None, 'tp')
- w_up: bfloat16 [4096, 11008], P(None, 'tp')
- w_down: bfloat16 [11008, 4096], P('tp')
- u_gate: bfloat16 [2048, 11008], P('dp', 'tp'), parts along dimension 0
- u_up: bfloat16 [2048, 11008], P('dp', 'tp'), parts along dimension 0
- grad_out: bfloat16 [2048, 4096], P(('dp', 'tp')), parts along dimension 0
Outputs:
- output 1: bfloat16 [2048, 4096], P(('dp', 'tp')), parts along dimension 0
- output 2: float32 [8192, 11008], P('dp', 'tp'), parts along dimension 0
- output 3: float32 [8192, 11008], P('dp', 'tp'), parts along dimension 0
- output 4: float32 [22016, 4096], P(('dp', 'tp')), parts along dimension 0
There are 2 independent parts. A program takes and returns all parts, laid end to end along the dimension named above; an argument that names none is the same for every part.
All inputs are finite; a program needn't handle non-finite values.
Results may differ from a plain program's by a relative error of at most 0.0116485.
Values are sent between devices in bfloat16 or wider.
A program may use at most 1 GiB of HBM per device.

v0:
```python
import jax
import jax.numpy as jnp
from jax import lax
from jax.sharding import PartitionSpec as P

CONTRACT_ROWS = (((0,), (0,)), ((), ()))
CONTRACT_COLS = (((1,), (1,)), ((), ()))


def solution(mesh):
    def local_backward(x_loc, wg_loc, wu_loc, wd_loc, ug_loc, uu_loc, dy_loc):
        x_all = lax.all_gather(x_loc, 'tp', axis=0, tiled=True)
        dy_all = lax.all_gather(dy_loc, 'tp', axis=0, tiled=True)
        gate_pre = ug_loc.astype(jnp.float32)
        up_pre = uu_loc.astype(jnp.float32)
        sig_gate = jax.nn.sigmoid(gate_pre)
        gate_act = gate_pre * sig_gate
        z_act = (gate_act * up_pre).astype(jnp.bfloat16)
        grad_down = lax.dot_general(z_act, dy_all, CONTRACT_ROWS, preferred_element_type=jnp.float32)
        grad_hid = lax.dot_general(dy_all, wd_loc, CONTRACT_COLS, preferred_element_type=jnp.float32)
        grad_up = (grad_hid * gate_act).astype(jnp.bfloat16)
        grad_gate = (grad_hid * up_pre * sig_gate * (1.0 + gate_pre * (1.0 - sig_gate))).astype(jnp.bfloat16)
        part_x = (lax.dot_general(grad_gate, wg_loc, CONTRACT_COLS, preferred_element_type=jnp.float32)
                  + lax.dot_general(grad_up, wu_loc, CONTRACT_COLS, preferred_element_type=jnp.float32))
        grad_x = lax.psum_scatter(part_x.astype(jnp.bfloat16), 'tp', scatter_dimension=0, tiled=True)
        grad_wg = lax.dot_general(x_all, grad_gate, CONTRACT_ROWS, preferred_element_type=jnp.float32)
        grad_wu = lax.dot_general(x_all, grad_up, CONTRACT_ROWS, preferred_element_type=jnp.float32)
        return grad_x, grad_wg, grad_wu, grad_down

    tok_spec = P(('dp', 'tp'), None)
    col_spec = P(None, 'tp')
    act_spec = P('dp', 'tp')
    return jax.shard_map(local_backward, mesh=mesh,
                         in_specs=(tok_spec, col_spec, col_spec, P('tp', None), act_spec, act_spec, tok_spec),
                         out_specs=(tok_spec, act_spec, act_spec, tok_spec),
                         check_vma=False)
```

profile of v0, /device:TPU:0, one launch (start us, length us, event | category | flops | bytes accessed | tf_op | source)
XLA Modules:
  0.0 198.5 jit_solution(1926365489491928529)
XLA Ops:
  7.2 0.0 all-gather.3.cloned.1.call-start
  7.2 0.7 all-gather.3.cloned.1.call-update
  7.9 0.0 all-gather.5.cloned.1.call-start
  7.9 0.7 all-gather.5.cloned.1.call-update
  8.6 0.0 reduce-scatter.2.cloned.1.call-start
  8.7 54.1 %all-gather.3.cloned.1.call-done = bf16[1024,4096]{1,0:T(8,128)(2,1)} async-done(((bf16[128,4096]{1,0:T(8,128)(2,1)}), bf16[1024,4096]{1,0:T(8,128)(2,1)}) %all-gather.3.cloned.1.call-update) | async-done | bytes 8388624 | tf_op jit(solution)/shard_map/all_gather | solution.py:13
  62.8 20.2 %fusion.2 = (bf16[1024,1376]{0,1:T(8,128)(2,1)S(1)}, f32[1024,1376]{0,1:T(8,128)}) fusion(bf16[1024,1376]{0,1:T(8,128)(2,1)} %param.12, bf16[1024,1376]{0,1:T(8,128)(2,1)} %param.11, bf16[1024,4096]{1,0:T(8,128)(2,1)} %all-gather.3.cloned.1.call-done, bf16[1376,4096]{1,0:T(8,128)(2,1)} %param.10), kind=kOutput, calls=%fused_computation.10 | convolution fusion | flops 11559632896 | bytes 33751040 | tf_op jit(solution)/shard_map/dot_general | solution.py:20
  83.0 0.0 copy-start.3
  83.0 0.0 copy-start.1
  83.0 20.8 %fusion.11 = f32[1024,4096]{1,0:T(8,128)} fusion(bf16[1024,1376]{0,1:T(8,128)(2,1)S(1)} %get-tuple-element.4, bf16[4096,1376]{0,1:T(8,128)(2,1)} %param.8), kind=kOutput, calls=%fused_computation.19 | convolution fusion | flops 11542724608 | bytes 30867456 | tf_op jit(solution)/shard_map/dot_general | solution.py:23
  103.8 0.0 copy-done.3
  103.8 0.0 copy-done.1
  103.8 23.0 %add_convert_fusion = bf16[1024,4096]{1,0:T(8,128)(2,1)} fusion(f32[1024,4096]{1,0:T(8,128)} %fusion.11, bf16[4096,1376]{0,1:T(8,128)(2,1)} %param.9, f32[1024,1376]{0,1:T(8,128)} %get-tuple-element.5, bf16[1024,1376]{0,1:T(8,128)(2,1)S(1)} %copy-done.1), kind=kOutput, calls=%fused_computation.2 | convolution fusion | flops 11560976384 | bytes 44892160 | tf_op jit(solution)/shard_map/dot_general | solution.py:24
  126.8 0.0 reduce-scatter.2.cloned.1.call-update
  126.8 0.0 copy-start
  126.8 0.0 all-gather.5.cloned.1.call-done
  126.8 0.0 copy-start.2
  126.8 0.0 slice-start
  126.9 19.6 %convolution_bitcast_fusion.1 = f32[4096,1376]{0,1:T(8,128)} fusion(bf16[1024,1376]{0,1:T(8,128)(2,1)} %copy-done.3, bf16[1024,4096]{1,0:T(8,128)(2,1)} %all-gather.5.cloned.1.call-done), kind=kOutput, calls=%fused_computation.1 | convolution fusion | flops 11542724608 | bytes 33751040 | tf_op jit(solution)/shard_map/dot_general | solution.py:26
  146.5 0.0 copy-done
  146.5 0.0 copy-done.2
  146.5 0.0 slice-start.1
  146.5 20.0 %fusion.8 = f32[1376,4096]{1,0:T(8,128)} fusion(bf16[1024,4096]{1,0:T(8,128)(2,1)} %all-gather.3.cloned.1.call-done, bf16[1024,1376]{0,1:T(8,128)(2,1)S(1)} %copy-done, bf16[1024,1376]{0,1:T(8,128)(2,1)S(1)} %copy-done.2), kind=kOutput, calls=%fused_computation.17 | convolution fusion | flops 11553996800 | bytes 36569088 | tf_op jit(solution)/shard_map/dot_general | solution.py:19
  166.5 0.0 slice-done
  166.5 0.0 slice-done.1
  166.5 18.7 %convolution_bitcast_fusion = f32[4096,1376]{0,1:T(8,128)} fusion(bf16[1024,4096]{1,0:T(8,128)(2,1)S(1)} %bitcast.14, f32[1024,1376]{0,1:T(8,128)} %get-tuple-element.5, bf16[1024,1376]{0,1:T(8,128)(2,1)} %param.11), kind=kOutput, calls=%fused_computation | convolution fusion | flops 11552587776 | bytes 39387136 | tf_op jit(solution)/shard_map/dot_general | solution.py:27
  185.2 6.7 %reduce-scatter.2.cloned.1.call-done = bf16[128,4096]{1,0:T(8,128)(2,1)} async-done(((bf16[1024,4096]{1,0:T(8,128)(2,1)}), bf16[128,4096]{1,0:T(8,128)(2,1)}) %reduce-scatter.2.cloned.1.call-update) | async-done | bytes 1048592 | tf_op jit(solution)/shard_map/reduce_scatter | solution.py:25
  (1 shorter events, 0.0 us)
Async XLA Ops:
  7.2 55.7 %all-gather.3.cloned.1.call-start = ((), (), s32[]{:S(2)}) async-start(), calls=%async_computation.1 | async-start | bytes 9437184 | tf_op jit(solution)/shard_map/all_gather | solution.py:13
  7.9 118.9 %all-gather.5.cloned.1.call-start = ((), (), s32[]{:S(2)}) async-start(), calls=%async_computation.3 | async-start | bytes 9437184 | tf_op jit(solution)/shard_map/all_gather | solution.py:12
  8.6 183.3 %reduce-scatter.2.cloned.1.call-start = ((), (), s32[]{:S(2)}) async-start(), calls=%async_computation.2 | async-start | bytes 9437184 | tf_op jit(solution)/shard_map/reduce_scatter | solution.py:25
  83.0 20.8 %copy-start.3 = (bf16[1024,1376]{0,1:T(8,128)(2,1)}, bf16[1024,1376]{0,1:T(8,128)(2,1)S(1)}, u32[]{:S(2)}) copy-start(bf16[1024,1376]{0,1:T(8,128)(2,1)S(1)} %get-tuple-element.4) | copy-start | bytes 8454148
  83.0 20.8 %copy-start.1 = (bf16[1024,1376]{0,1:T(8,128)(2,1)S(1)}, bf16[1024,1376]{0,1:T(8,128)(2,1)}, u32[]{:S(2)}) copy-start(bf16[1024,1376]{0,1:T(8,128)(2,1)} %param.11) | copy-start | bytes 8454148
  126.8 19.7 %copy-start = (bf16[1024,1376]{0,1:T(8,128)(2,1)S(1)}, bf16[1024,1376]{0,1:T(8,128)(2,1)}, u32[]{:S(2)}) copy-start(bf16[1024,1376]{0,1:T(8,128)(2,1)} %param.12) | copy-start | bytes 8454148
  126.8 19.6 %copy-start.2 = (bf16[1024,1376]{0,1:T(8,128)(2,1)S(1)}, bf16[1024,1376]{0,1:T(8,128)(2,1)}, u32[]{:S(2)}) copy-start(bf16[1024,1376]{0,1:T(8,128)(2,1)} %param.11) | copy-start | bytes 8454148
  126.8 39.6 %slice-start = ((s8[8388608]{0:T(1024)(128)(4,1)}), s8[4194304]{0:T(1024)(128)(4,1)S(1)}, s32[]{:S(2)}) async-start(s8[8388608]{0:T(1024)(128)(4,1)} %bitcast.13), calls=%async_computation.4 | async-start | bytes 8388608
  146.5 20.0 %slice-start.1 = ((s8[8388608]{0:T(1024)(128)(4,1)}), s8[4194304]{0:T(1024)(128)(4,1)S(1)}, s32[]{:S(2)}) async-start(s8[8388608]{0:T(1024)(128)(4,1)} %bitcast.13), calls=%async_computation.5 | async-start | bytes 8388608
Sparse Core Ops, SparseCore 0:
  9.8 52.9 all-gather.2
  64.7 50.1 all-gather.4
  126.9 64.9 reduce-scatter.1
where the time goes:
time: 199 us; the launch traced here: 198 us
  matrix products  122 us (61%)
  waiting for transfers between devices  62.3 us (31%)
  between operations  13.8 us (7%)
    all_gather x1, waiting for transfers between devices, local_backward(): dy_all = lax.all_gather(dy_loc, 'tp', axis=0, tiled=True)  54.1 us
    dot_general x1, matrix products, local_backward(): lax.dot_general(grad_up, wu_loc, CONTRACT_COLS, preferred_element_type=jn...  23 us
    dot_general x1, matrix products, local_backward(): lax.dot_general(grad_gate, wg_loc, CONTRACT_COLS, preferred_element_type=...  20.8 us
    dot_general x1, matrix products, local_backward(): lax.dot_general(dy_all, wd_loc, CONTRACT_COLS, preferred_element_type=jnp...  20.2 us
    dot_general x1, matrix products, local_backward(): lax.dot_general(z_act, dy_all, CONTRACT_ROWS, preferred_element_type=jnp....  20 us
    dot_general x1, matrix products, local_backward(): lax.dot_general(x_all, grad_gate, CONTRACT_ROWS, preferred_element_type=j...  19.6 us
    dot_general x1, matrix products, local_backward(): lax.dot_general(x_all, grad_up, CONTRACT_ROWS, preferred_element_type=jnp...  18.7 us
    reduce_scatter x1, waiting for transfers between devices, local_backward(): lax.psum_scatter(part_x.astype(jnp.bfloat16), 'tp', scatter_dimension=0,...  6.74 us
  transfers between devices with their start and end apart: 3, of which 2 were waited for; matrix products, arithmetic and copies ran while one was open for 62% of the time, Pallas kernels for 0%

commit v1 on v0

v1 whole, which is shorter than its diff:
```python
import functools

import jax
import jax.numpy as jnp
from jax import lax
from jax.experimental import pallas as pl
from jax.experimental.pallas import tpu as pltpu
from jax.sharding import PartitionSpec as P

MESH = pl.DeviceIdType.MESH
BF16 = jnp.bfloat16
F32 = jnp.float32
NH = 8
NT = (((1,), (1,)), ((), ()))


def _lanes(n):
    return (n + 127) // 128 * 128


def _comm_kernel(x_ref, dy_ref, wd_ref, wg_ref, wu_ref, ug_ref, uu_ref,
                 dx_ref, zt_ref, dgt_ref, dut_ref, dya_ref, xa_ref,
                 dyv, gv, av, spv, utv, duv, wbuf, ugv, uuv, r0v, r1v, r2v, dxv, xov,
                 ys, yr, xs, xr, rs, rr, yl, xl, wl, ul, ol, dl):
    tok, hid = dy_ref.shape
    ff = wd_ref.shape[0]
    fp = _lanes(ff)
    nfull, rest = ff // 128, ff % 128
    hc = hid // NH
    tall = 8 * tok

    t = lax.axis_index("tp")
    ty, tx, tc = t // 4, (t // 2) % 2, t % 2
    tq = t // 2
    xn = t + 2 - 4 * tx
    yn = t + 4 - 8 * ty
    dg = xn + yn - t
    pn = t + 1 - 2 * tc

    def n1(k):
        return xn + (yn - xn) * (k % 2)

    def n2(k):
        return yn + (xn - yn) * (k % 2)

    def cols(k):
        return pl.ds(pl.multiple_of(k * hc, hc), hc)

    def blk(ref, owner, k):
        return ref.at[owner // 2, owner % 2, :, cols(k)]

    def rcopy(src, dst, ss, rs_, dev):
        return pltpu.make_async_remote_copy(src_ref=src, dst_ref=dst, send_sem=ss, recv_sem=rs_,
                                            device_id={"tp": dev}, device_id_type=MESH)

    def ag(buf, ss, sr, k, j, owner, dev):
        return rcopy(blk(buf, owner, k), blk(buf, owner, k), ss.at[k, j], sr.at[k, j], dev)

    def ag_own(buf, ss, sr, k):
        ag(buf, ss, sr, k, 0, t, n1(k)).start()
        ag(buf, ss, sr, k, 1, t, n2(k)).start()
        ag(buf, ss, sr, k, 3, t, pn).start()

    def ag_mid(buf, ss, sr, k):
        ag(buf, ss, sr, k, 0, n1(k), n1(k)).wait_recv()
        ag(buf, ss, sr, k, 2, n1(k), n2(k)).start()
        ag(buf, ss, sr, k, 4, n1(k), pn).start()

    def ag_last(buf, ss, sr, k):
        ag(buf, ss, sr, k, 1, n2(k), n2(k)).wait_recv()
        ag(buf, ss, sr, k, 5, n2(k), pn).start()
        ag(buf, ss, sr, k, 2, dg, n2(k)).wait_recv()
        ag(buf, ss, sr, k, 6, dg, pn).start()

    def ag_end(buf, ss, sr, k):
        pc = 1 - 2 * tc
        ag(buf, ss, sr, k, 3, t + pc, pn).wait_recv()
        ag(buf, ss, sr, k, 4, n1(k) + pc, pn).wait_recv()
        ag(buf, ss, sr, k, 5, n2(k) + pc, pn).wait_recv()
        ag(buf, ss, sr, k, 6, dg + pc, pn).wait_recv()

    def ag_sent(buf, ss, sr, k):
        ag(buf, ss, sr, k, 0, t, n1(k)).wait_send()
        ag(buf, ss, sr, k, 1, t, n2(k)).wait_send()
        ag(buf, ss, sr, k, 2, n1(k), n2(k)).wait_send()
        ag(buf, ss, sr, k, 3, t, pn).wait_send()
        ag(buf, ss, sr, k, 4, n1(k), pn).wait_send()
        ag(buf, ss, sr, k, 5, n2(k), pn).wait_send()
        ag(buf, ss, sr, k, 6, dg, pn).wait_send()

    def y_local(k):
        return pltpu.make_async_copy(dy_ref.at[:, cols(k)], blk(dyv, t, k), yl.at[k])

    def x_local(k):
        return pltpu.make_async_copy(x_ref.at[:, cols(k)], xov.at[:, cols(k)], xl.at[k])

    def x_put(k):
        return pltpu.make_async_copy(xov.at[:, cols(k)], blk(xa_ref, t, k), xl.at[k])

    def wd_load(k):
        return pltpu.make_async_copy(wd_ref.at[:, cols(k)], wbuf.at[0, k % 2, pl.ds(0, ff), :], wl.at[0, k % 2])

    def w_load(k, j):
        src = (wg_ref, wu_ref)[j]
        return pltpu.make_async_copy(src.at[:, cols(k)], wbuf.at[(k + 1) % 2, j, pl.ds(0, ff), :],
                                     wl.at[(k + 1) % 2, j])

    def dy_out(k):
        return pltpu.make_async_copy(dyv.at[:, :, :, cols(k)], dya_ref.at[:, :, :, cols(k)], dl.at[k])

    ug_in = pltpu.make_async_copy(ug_ref, ugv, ul.at[0])
    uu_in = pltpu.make_async_copy(uu_ref, uuv, ul.at[1])
    for k in range(NH):
        y_local(k).start()
    wd_load(0).start()
    wd_load(1).start()
    ug_in.start()
    uu_in.start()
    for k in range(NH):
        x_local(k).start()

    barrier = pltpu.get_barrier_semaphore()
    for dev in (xn, yn, pn):
        pl.semaphore_signal(barrier, inc=1, device_id={"tp": dev}, device_id_type=MESH)
    pl.semaphore_wait(barrier, 3)

    for k in range(2):
        y_local(k).wait()
        ag_own(dyv, ys, yr, k)

    for a in range(2):
        for b in range(2):
            wbuf[a, b, ff:, :] = jnp.zeros((fp - ff, hc), BF16)
    gv[...] = jnp.zeros_like(gv)
    ug_in.wait()
    uu_in.wait()

    def u_block(r0, n):
        rows = pl.ds(r0, n)
        ug = ugv[rows, :].astype(F32)
        ub = uuv[rows, :]
        uu = ub.astype(F32)
        s = jax.nn.sigmoid(ug)
        a = ug * s
        sp = s * (1.0 + ug * (1.0 - s))
        ugv[rows, :] = (a * uu).astype(BF16)
        if n < 128:
            pad = jnp.zeros((128 - n, tall), F32)
            a = jnp.concatenate([a, pad], axis=0)
            sp = jnp.concatenate([sp, pad], axis=0)
            uu = jnp.concatenate([uu, pad], axis=0)
        lanes = pl.ds(r0, 128)
        av[:, lanes] = a.T
        spv[:, lanes] = sp.T
        utv[:, lanes] = uu.T.astype(BF16)

    def phase1(i, carry):
        @pl.when(i < NH - 2)
        def _():
            y_local(i + 2).wait()
            ag_own(dyv, ys, yr, i + 2)

        @pl.when(i < NH)
        def _():
            ag_mid(dyv, ys, yr, i)

        @pl.when(i < nfull)
        def _():
            u_block(pl.multiple_of(i * 128, 128), 128)

        @pl.when((i >= 1) & (i <= NH))
        def _():
            ag_last(dyv, ys, yr, i - 1)

        @pl.when(i >= 2)
        def _():
            k = i - 2
            ag_end(dyv, ys, yr, k)
            dy_out(k).start()
            wd_load(k).wait()
            dyc = dyv[:, :, :, cols(k)].reshape(tall, hc)
            for n in range(0, fp, 256):
                w = min(256, fp - n)
                gv[:, n:n + w] += lax.dot_general(dyc, wbuf[0, k % 2, n:n + w, :], NT, preferred_element_type=F32)

            @pl.when(k + 2 < NH)
            def _():
                wd_load(k + 2).start()

        return carry

    w_load(0, 0).start()
    w_load(0, 1).start()
    lax.fori_loop(0, NH + 2, phase1, 0)
    w_load(1, 0).start()
    w_load(1, 1).start()
    for k in range(NH):
        x_local(k).wait()
        x_put(k).start()
    if rest:
        u_block(nfull * 128, rest)
    zt_out = pltpu.make_async_copy(ugv, zt_ref, ol.at[0])
    zt_out.start()
    for k in range(NH):
        x_put(k).wait()
    for k in range(2):
        ag_own(xa_ref, xs, xr, k)

    def gates(i, carry):
        rows = pl.ds(pl.multiple_of(i * 128, 128), 128)
        g = gv[rows, :]
        duv[rows, :fp] = (g * utv[rows, :].astype(F32) * spv[rows, :]).astype(BF16)
        duv[rows, fp:] = (g * av[rows, :]).astype(BF16)
        return carry

    lax.fori_loop(0, tall // 128, gates, 0)

    def sent(k, carry):
        ag_sent(dyv, ys, yr, k)
        dy_out(k).wait()
        return carry

    lax.fori_loop(0, NH, sent, 0)
    zt_out.wait()

    def rs0(k, c):
        return rcopy(dyv.at[:, c, :, cols(k)], r0v.at[k], rs.at[k, 0], rr.at[k, 0], pn)

    def rs1(k, j, owner):
        return rcopy(blk(dyv, owner, k), r1v.at[k, j], rs.at[k, 1 + j], rr.at[k, 1 + j], n1(k))

    def rs2(k):
        return rcopy(blk(dyv, n2(k), k), r2v.at[k], rs.at[k, 3], rr.at[k, 3], n2(k))

    def add(owner, k, other):
        b = blk(dyv, owner, k)
        b[...] = (b[...].astype(F32) + other.astype(F32)).astype(BF16)

    def t_block(r0, n):
        lanes = pl.ds(r0, 128)
        rows = pl.ds(r0, n)
        ugv[rows, :] = duv[:, lanes].T[:n]
        uuv[rows, :] = duv[:, pl.ds(fp + r0, 128)].T[:n]

    def phase2(i, carry):
        @pl.when(i < NH - 2)
        def _():
            ag_own(xa_ref, xs, xr, i + 2)

        @pl.when(i < NH)
        def _():
            ag_mid(xa_ref, xs, xr, i)
            w_load(i, 0).wait()
            w_load(i, 1).wait()
            slot = (i + 1) % 2
            for n in range(0, hc, 256):
                p = lax.dot_general(duv[:, :fp], wbuf[slot, 0, :, n:n + 256], (((1,), (0,)), ((), ())),
                                    preferred_element_type=F32)
                p = p + lax.dot_general(duv[:, fp:], wbuf[slot, 1, :, n:n + 256], (((1,), (0,)), ((), ())),
                                        preferred_element_type=F32)
                dyv[:, :, :, pl.ds(pl.multiple_of(i * hc + n, 256), 256)] = p.astype(BF16).reshape(4, 2, tok, 256)

            @pl.when(i + 2 < NH)
            def _():
                w_load(i + 2, 0).start()
                w_load(i + 2, 1).start()

        @pl.when(i < nfull)
        def _():
            t_block(pl.multiple_of(i * 128, 128), 128)

        @pl.when(i < NH)
        def _():
            rs0(i, 1 - tc).start()

        @pl.when((i >= 1) & (i <= NH))
        def _():
            k = i - 1
            ag_last(xa_ref, xs, xr, k)
            rs0(k, tc).wait_recv()
            for q in range(4):
                add(2 * q + tc, k, r0v[k, q])
            rs1(k, 0, n1(k)).start()
            rs1(k, 1, dg).start()

        @pl.when((i >= 2) & (i <= NH + 1))
        def _():
            k = i - 2
            rs1(k, 0, t).wait_recv()
            rs1(k, 1, n2(k)).wait_recv()
            add(n2(k), k, r1v[k, 1])
            add(t, k, r1v[k, 0])
            rs2(k).start()

        @pl.when(i >= 3)
        def _():
            k = i - 3
            rs2(k).wait_recv()
            dxv[:, cols(k)] = (blk(dyv, t, k)[...].astype(F32) + r2v[k].astype(F32)).astype(BF16)

        return carry

    lax.fori_loop(0, NH + 3, phase2, 0)
    if rest:
        t_block(nfull * 128, rest)
    outs = [pltpu.make_async_copy(ugv, dgt_ref, ol.at[0]), pltpu.make_async_copy(uuv, dut_ref, ol.at[1]),
            pltpu.make_async_copy(dxv, dx_ref, ol.at[2])]
    for o in outs:
        o.start()

    def drain(k, carry):
        ag_end(xa_ref, xs, xr, k)
        ag_sent(xa_ref, xs, xr, k)
        rs0(k, 1 - tc).wait_send()
        rs1(k, 0, n1(k)).wait_send()
        rs1(k, 1, dg).wait_send()
        rs2(k).wait_send()
        return carry

    lax.fori_loop(0, NH, drain, 0)
    for o in outs:
        o.wait()


def _weight_kernel(zt_ref, dgt_ref, dut_ref, dy_ref, x_ref, dd_ref, dg_ref, du_ref):
    j = pl.program_id(0)
    n = pl.num_programs(0) // 3

    @pl.when(j < n)
    def _():
        dd_ref[...] = jnp.dot(zt_ref[...], dy_ref[...], preferred_element_type=F32)

    @pl.when((j >= n) & ((j - n) % 2 == 0))
    def _():
        dg_ref[...] = jnp.dot(dgt_ref[...], x_ref[...], preferred_element_type=F32)

    @pl.when((j >= n) & ((j - n) % 2 == 1))
    def _():
        du_ref[...] = jnp.dot(dut_ref[...], x_ref[...], preferred_element_type=F32)


def solution(mesh):
    def local_backward(x, wg, wu, wd, ug, uu, dy):
        tok, hid = dy.shape
        ff = wd.shape[0]
        fp = _lanes(ff)
        tall = 8 * tok
        hc = hid // NH
        any_ = pl.BlockSpec(memory_space=pl.ANY)
        sem = pltpu.SemaphoreType.DMA
        full = jax.ShapeDtypeStruct((4, 2, tok, hid), BF16)
        act = jax.ShapeDtypeStruct((ff, tall), BF16)
        dx, zt, dgt, dut, dya, xa = pl.pallas_call(
            _comm_kernel,
            out_shape=(jax.ShapeDtypeStruct((tok, hid), BF16), act, act, act, full, full),
            in_specs=[any_] * 7,
            out_specs=(any_,) * 6,
            scratch_shapes=[
                pltpu.VMEM((4, 2, tok, hid), BF16),
                pltpu.VMEM((tall, fp), F32),
                pltpu.VMEM((tall, fp), F32),
                pltpu.VMEM((tall, fp), F32),
                pltpu.VMEM((tall, fp), BF16),
                pltpu.VMEM((tall, 2 * fp), BF16),
                pltpu.VMEM((2, 2, fp, hc), BF16),
                pltpu.VMEM((ff, tall), BF16),
                pltpu.VMEM((ff, tall), BF16),
                pltpu.VMEM((NH, 4, tok, hc), BF16),
                pltpu.VMEM((NH, 2, tok, hc), BF16),
                pltpu.VMEM((NH, tok, hc), BF16),
                pltpu.VMEM((tok, hid), BF16),
                pltpu.VMEM((tok, hid), BF16),
                sem((NH, 7)), sem((NH, 7)), sem((NH, 7)), sem((NH, 7)), sem((NH, 4)), sem((NH, 4)),
                sem((NH,)), sem((NH,)), sem((2, 2)), sem((2,)), sem((3,)), sem((NH,)),
            ],
            compiler_params=pltpu.CompilerParams(collective_id=0, has_side_effects=True, vmem_limit_bytes=67043328),
            name="gather_reduce",
        )(x, dy, wd, wg.T, wu.T, ug.T, uu.T)

        nb = 512
        n = hid // nb
        res = pl.BlockSpec((ff, tall), lambda j: (0, 0))
        grad = jax.ShapeDtypeStruct((ff, hid), F32)
        dwd, dwg, dwu = pl.pallas_call(
            _weight_kernel,
            grid=(3 * n,),
            out_shape=(grad, grad, grad),
            in_specs=[res, res, res,
                      pl.BlockSpec((tall, nb), lambda j: (0, jnp.minimum(j, n - 1))),
                      pl.BlockSpec((tall, nb), lambda j: (0, jnp.maximum(j - n, 0) // 2))],
            out_specs=(pl.BlockSpec((ff, nb), lambda j: (0, jnp.minimum(j, n - 1))),
                       pl.BlockSpec((ff, nb), lambda j: (0, jnp.maximum(j - n, 0) // 2)),
                       pl.BlockSpec((ff, nb), lambda j: (0, jnp.maximum(j - n - 1, 0) // 2))),
            compiler_params=pltpu.CompilerParams(vmem_limit_bytes=63 * 2 ** 20),
            cost_estimate=pl.CostEstimate(flops=6 * ff * tall * hid, bytes_accessed=12 * ff * hid, transcendentals=0),
            name="weight_grads",
        )(zt, dgt, dut, dya.reshape(tall, hid), xa.reshape(tall, hid))
        return dx, dwg.T, dwu.T, dwd

    tok_spec = P(('dp', 'tp'), None)
    col_spec = P(None, 'tp')
    act_spec = P('dp', 'tp')
    return jax.shard_map(local_backward, mesh=mesh,
                         in_specs=(tok_spec, col_spec, col_spec, P('tp', None), act_spec, act_spec, tok_spec),
                         out_specs=(tok_spec, act_spec, act_spec, tok_spec),
                         check_vma=False)
```

time: 199 us -> 183 us (0.920)
  Pallas kernels: 0 us -> 179 us
  matrix products: 122 us -> 0 us
  waiting for transfers between devices: 62.3 us -> 0 us
  between operations: 13.8 us -> 0.64 us
  local copies, waits for them, and re-layouts: 0.03 us -> 2.29 us
    pallas_call x0 -> x2, Pallas kernels: none -> 179 us  [the longest x1 127 us: local_backward(): pl.pallas_call(_comm_kernel, out_shape=(jax.ShapeDtypeStruct((tok, hid),...]
    dot_general x6 -> x0, matrix products: 122 us -> none  [the longest x1 23 us: local_backward(): lax.dot_general(grad_up, wu_loc, CONTRACT_COLS, preferred_element_type=jn...]
    all_gather x2 -> x0, waiting for transfers between devices: 54.1 us -> none  [the longest x1 54.1 us: local_backward(): dy_all = lax.all_gather(dy_loc, 'tp', axis=0, tiled=True)]
    reduce_scatter x1 -> x0, waiting for transfers between devices: 6.74 us -> none  [local_backward(): lax.psum_scatter(part_x.astype(jnp.bfloat16), 'tp', scatter_dimension=0,...]
    unnamed x12 -> x1, local copies, waits for them, and re-layouts: 0.03 us -> 2.29 us
  transfers between devices with their start and end apart: 3 -> 0, of which waited for: 2 -> 0; matrix products, arithmetic and copies ran while one was open for 62% -> 0% of each run, Pallas kernels for 0% -> 0%
where the time goes in v1:
time: 183 us; the launch traced here: 182 us
  Pallas kernels  179 us (98%)
  local copies, waits for them, and re-layouts  2.29 us (1%)
    pallas_call x1, Pallas kernels, local_backward(): pl.pallas_call(_comm_kernel, out_shape=(jax.ShapeDtypeStruct((tok, hid),...  127 us
    pallas_call x1, Pallas kernels, local_backward(): pl.pallas_call(_weight_kernel, grid=(3 * n,), out_shape=(grad, grad, grad...  51.6 us

profile of v1, /device:TPU:0, one launch (start us, length us, event | category | flops | bytes accessed | tf_op | source)
XLA Modules:
  0.0 181.9 jit_solution(12739478848990307926)
XLA Ops:
  0.6 127.3 %gather_reduce.1 = (bf16[128,4096]{1,0:T(8,128)(2,1)}, bf16[1376,1024]{1,0:T(8,128)(2,1)}, bf16[1376,1024]{1,0:T(8,128)(2,1)}, bf16[1376,1024]{1,0:T(8,128)(2,1)...) custom-call(bf16[128,4096]{1,0:T(8,128)(2,1)} %x_ref.1, bf16[128,4096]{1,0:T(8,128)(2,1)} %dy_ref.1, ...), custom_call_target="tpu_custom_call" | custom-call | tf_op jit(solution)/shard_map/gather_reduce/pallas_call | solution.py:353
  128.0 51.6 %weight_grads.1 = (f32[1376,4096]{1,0:T(8,128)}, f32[1376,4096]{1,0:T(8,128)}, f32[1376,4096]{1,0:T(8,128)}) custom-call(bf16[1376,1024]{1,0:T(8,128)(2,1)} %get-tuple-element.14.zt_ref, bf16[1376,1024]{1,0:T(8,128)(2,1)} %get-tuple-element.15.dgt_ref, bf16[1376,1024]{1,0:T(8,128)(2,1)} %get-tuple-element.16.dut_ref, bf16[1024,4096]{1,0:T(8,128)(2,1)} %bitcast.12, ...), custom_call_target="tpu_custom_call" | custom-call | flops 34628173824 | bytes 67633152 | tf_op jit(solution)/shard_map/weight_grads/pallas_call | solution.py:384
  179.6 2.3 %copy.12 = bf16[128,4096]{1,0:T(8,128)(2,1)} copy(bf16[128,4096]{1,0:T(8,128)(2,1)} %get-tuple-element.26) | data formatting | bytes 2097152

commit v2 on v1

--- a/solution.py
+++ b/solution.py
@@ -19,19 +19,19 @@
 
 
 def _comm_kernel(x_ref, dy_ref, wd_ref, wg_ref, wu_ref, ug_ref, uu_ref,
-                 dx_ref, zt_ref, dgt_ref, dut_ref, dya_ref, xa_ref,
-                 dyv, gv, av, spv, utv, duv, wbuf, ugv, uuv, r0v, r1v, r2v, dxv, xov,
-                 ys, yr, xs, xr, rs, rr, yl, xl, wl, ul, ol, dl):
+                 sa_ref, ka_ref, sb_ref, kb_ref, zt_ref, dgt_ref, dut_ref, dya_ref, xa_ref,
+                 dyv, gv, av, spv, utv, duv, wbuf, ugv, uuv, r0v, xov,
+                 ys, yr, xs, xr, rs, rr, yl, xl, wl, ul, ol, dl, po):
     tok, hid = dy_ref.shape
     ff = wd_ref.shape[0]
     fp = _lanes(ff)
     nfull, rest = ff // 128, ff % 128
     hc = hid // NH
     tall = 8 * tok
+    half = NH // 2
 
     t = lax.axis_index("tp")
     ty, tx, tc = t // 4, (t // 2) % 2, t % 2
-    tq = t // 2
     xn = t + 2 - 4 * tx
     yn = t + 4 - 8 * ty
     dg = xn + yn - t
@@ -60,6 +60,14 @@
         ag(buf, ss, sr, k, 0, t, n1(k)).start()
         ag(buf, ss, sr, k, 1, t, n2(k)).start()
         ag(buf, ss, sr, k, 3, t, pn).start()
+
+    def x_own(k, j, dev):
+        return rcopy(xov.at[:, cols(k)], blk(xa_ref, t, k), xs.at[k, j], xr.at[k, j], dev)
+
+    def x_send(k):
+        x_own(k, 0, n1(k)).start()
+        x_own(k, 1, n2(k)).start()
+        x_own(k, 3, pn).start()
 
     def ag_mid(buf, ss, sr, k):
         ag(buf, ss, sr, k, 0, n1(k), n1(k)).wait_recv()
@@ -164,6 +172,12 @@
         def _():
             ag_mid(dyv, ys, yr, i)
 
+        for first, ks in ((NH - 1, range(0, 2)), (NH, range(2, 5)), (NH + 1, range(5, NH))):
+            @pl.when(i == first)
+            def _():
+                for k in ks:
+                    x_send(k)
+
         @pl.when(i < nfull)
         def _():
             u_block(pl.multiple_of(i * 128, 128), 128)
@@ -191,21 +205,16 @@
 
     w_load(0, 0).start()
     w_load(0, 1).start()
+    for k in range(NH):
+        x_local(k).wait()
+        x_put(k).start()
     lax.fori_loop(0, NH + 2, phase1, 0)
     w_load(1, 0).start()
     w_load(1, 1).start()
-    for k in range(NH):
-        x_local(k).wait()
-        x_put(k).start()
     if rest:
         u_block(nfull * 128, rest)
     zt_out = pltpu.make_async_copy(ugv, zt_ref, ol.at[0])
     zt_out.start()
-    for k in range(NH):
-        x_put(k).wait()
-    for k in range(2):
-        ag_own(xa_ref, xs, xr, k)
-
     def gates(i, carry):
         rows = pl.ds(pl.multiple_of(i * 128, 128), 128)
         g = gv[rows, :]
@@ -224,13 +233,13 @@
     zt_out.wait()
 
     def rs0(k, c):
-        return rcopy(dyv.at[:, c, :, cols(k)], r0v.at[k], rs.at[k, 0], rr.at[k, 0], pn)
-
-    def rs1(k, j, owner):
-        return rcopy(blk(dyv, owner, k), r1v.at[k, j], rs.at[k, 1 + j], rr.at[k, 1 + j], n1(k))
-
-    def rs2(k):
-        return rcopy(blk(dyv, n2(k), k), r2v.at[k], rs.at[k, 3], rr.at[k, 3], n2(k))
+        return rcopy(dyv.at[:, c, :, cols(k)], r0v.at[k], rs.at[k], rr.at[k], pn)
+
+    def sums_out(k, left):
+        kk = k if left else k - half
+        send, keep, far, near = (sa_ref, ka_ref, xn, yn) if left else (sb_ref, kb_ref, yn, xn)
+        return [pltpu.make_async_copy(blk(dyv, owner, k), ref.at[b, :, cols(kk)], po.at[k, 2 * a + b])
+                for a, ref, owners in ((0, send, (far, dg)), (1, keep, (t, near))) for b, owner in enumerate(owners)]
 
     def add(owner, k, other):
         b = blk(dyv, owner, k)
@@ -243,10 +252,6 @@
         uuv[rows, :] = duv[:, pl.ds(fp + r0, 128)].T[:n]
 
     def phase2(i, carry):
-        @pl.when(i < NH - 2)
-        def _():
-            ag_own(xa_ref, xs, xr, i + 2)
-
         @pl.when(i < NH)
         def _():
             ag_mid(xa_ref, xs, xr, i)
@@ -265,9 +270,10 @@
                 w_load(i + 2, 0).start()
                 w_load(i + 2, 1).start()
 
-        @pl.when(i < nfull)
-        def _():
-            t_block(pl.multiple_of(i * 128, 128), 128)
+        for b in (2 * i, 2 * i + 1):
+            @pl.when(b < nfull)
+            def _():
+                t_block(pl.multiple_of(b * 128, 128), 128)
 
         @pl.when(i < NH)
         def _():
@@ -280,41 +286,48 @@
             rs0(k, tc).wait_recv()
             for q in range(4):
                 add(2 * q + tc, k, r0v[k, q])
-            rs1(k, 0, n1(k)).start()
-            rs1(k, 1, dg).start()
-
-        @pl.when((i >= 2) & (i <= NH + 1))
-        def _():
-            k = i - 2
-            rs1(k, 0, t).wait_recv()
-            rs1(k, 1, n2(k)).wait_recv()
-            add(n2(k), k, r1v[k, 1])
-            add(t, k, r1v[k, 0])
-            rs2(k).start()
-
-        @pl.when(i >= 3)
-        def _():
-            k = i - 3
-            rs2(k).wait_recv()
-            dxv[:, cols(k)] = (blk(dyv, t, k)[...].astype(F32) + r2v[k].astype(F32)).astype(BF16)
+
+            @pl.when(k < half)
+            def _():
+                for o in sums_out(k, True):
+                    o.start()
+
+            @pl.when(k >= half)
+            def _():
+                for o in sums_out(k, False):
+                    o.start()
 
         return carry
 
-    lax.fori_loop(0, NH + 3, phase2, 0)
+    lax.fori_loop(0, NH + 1, phase2, 0)
     if rest:
         t_block(nfull * 128, rest)
-    outs = [pltpu.make_async_copy(ugv, dgt_ref, ol.at[0]), pltpu.make_async_copy(uuv, dut_ref, ol.at[1]),
-            pltpu.make_async_copy(dxv, dx_ref, ol.at[2])]
+    outs = [pltpu.make_async_copy(ugv, dgt_ref, ol.at[0]), pltpu.make_async_copy(uuv, dut_ref, ol.at[1])]
     for o in outs:
         o.start()
 
     def drain(k, carry):
         ag_end(xa_ref, xs, xr, k)
-        ag_sent(xa_ref, xs, xr, k)
+        x_put(k).wait()
+        x_own(k, 0, n1(k)).wait_send()
+        x_own(k, 1, n2(k)).wait_send()
+        ag(xa_ref, xs, xr, k, 2, n1(k), n2(k)).wait_send()
+        x_own(k, 3, pn).wait_send()
+        ag(xa_ref, xs, xr, k, 4, n1(k), pn).wait_send()
+        ag(xa_ref, xs, xr, k, 5, n2(k), pn).wait_send()
+        ag(xa_ref, xs, xr, k, 6, dg, pn).wait_send()
         rs0(k, 1 - tc).wait_send()
-        rs1(k, 0, n1(k)).wait_send()
-        rs1(k, 1, dg).wait_send()
-        rs2(k).wait_send()
+
+        @pl.when(k < half)
+        def _():
+            for o in sums_out(k, True):
+                o.wait()
+
+        @pl.when(k >= half)
+        def _():
+            for o in sums_out(k, False):
+                o.wait()
+
         return carry
 
     lax.fori_loop(0, NH, drain, 0)
@@ -322,21 +335,87 @@
         o.wait()
 
 
-def _weight_kernel(zt_ref, dgt_ref, dut_ref, dy_ref, x_ref, dd_ref, dg_ref, du_ref):
+def _row_chunks(ff):
+    n = ff // 16
+    size = -(-n // 4)
+    return [16 * min(size, n - i) for i in range(0, n, size)]
+
+
+def _weight_kernel(*refs, n):
+    m = len(refs) // 3
+    lhs, rhs, out = refs[:m], refs[m:2 * m], refs[2 * m:]
+    ff, tall = lhs[0].shape
+    nb = out[0].shape[1]
+    sizes = _row_chunks(ff)
     j = pl.program_id(0)
-    n = pl.num_programs(0) // 3
-
-    @pl.when(j < n)
-    def _():
-        dd_ref[...] = jnp.dot(zt_ref[...], dy_ref[...], preferred_element_type=F32)
-
-    @pl.when((j >= n) & ((j - n) % 2 == 0))
-    def _():
-        dg_ref[...] = jnp.dot(dgt_ref[...], x_ref[...], preferred_element_type=F32)
-
-    @pl.when((j >= n) & ((j - n) % 2 == 1))
-    def _():
-        du_ref[...] = jnp.dot(dut_ref[...], x_ref[...], preferred_element_type=F32)
+
+    def product(a, b, o, accs):
+        steps = []
+        for pair in range(nb // 512):
+            row = 0
+            for c, size in enumerate(sizes):
+                for kt in range(tall // 256):
+                    steps.append((pair, c, row, size, kt))
+                row += size
+
+        def push(s):
+            pair, _, _, _, kt = steps[s]
+            for q in range(2):
+                lo = pair * 512 + q * 256
+                pltpu.matmul_push_rhs(b[kt * 256:kt * 256 + 256, lo:lo + 256], s % 2, q)
+
+        def pop(pair, c, row, size):
+            for q in range(2):
+                lo = pair * 512 + q * 256
+                o[row:row + size, lo:lo + 256] = pltpu.matmul_pop(accs[q][c])
+
+        push(0)
+        late = None
+        for s, (pair, c, row, size, kt) in enumerate(steps):
+            if s + 1 < len(steps):
+                push(s + 1)
+            block = a[row:row + size, kt * 256:kt * 256 + 256]
+            for q in range(2):
+                pltpu.matmul_acc_lhs(accs[q][c], block, load_staged_rhs=s % 2)
+            if kt == 0 and late is not None:
+                pop(*late)
+            if kt == tall // 256 - 1:
+                late = (pair, c, row, size)
+        pop(*late)
+
+    def body(*flat):
+        half = len(flat) // 2
+        accs = []
+        for part in (flat[:half], flat[half:]):
+            accs.append([part[2] if i == len(sizes) - 1 else part[i % 2] for i in range(len(sizes))])
+        for i in range(m):
+            @pl.when((j >= i * n) & (j < (i + 1) * n))
+            def _():
+                product(lhs[i], rhs[i], out[i], accs)
+
+    pl.run_scoped(body, *[pltpu.ACC(q)((size, 256), F32) for q in range(2) for size in (sizes[0], sizes[0], sizes[-1])])
+
+
+def _weight_grads(lhs, rhs, name):
+    m = len(lhs)
+    ff, tall = lhs[0].shape
+    hid = rhs[0].shape[1]
+    nb = 1024
+    n = hid // nb
+
+    def col(i):
+        return lambda j: (0, jnp.clip(j - i * n, 0, n - 1))
+
+    return pl.pallas_call(
+        functools.partial(_weight_kernel, n=n),
+        grid=(m * n,),
+        out_shape=(jax.ShapeDtypeStruct((ff, hid), F32),) * m,
+        in_specs=[pl.BlockSpec((ff, tall), lambda j: (0, 0))] * m + [pl.BlockSpec((tall, nb), col(i)) for i in range(m)],
+        out_specs=tuple(pl.BlockSpec((ff, nb), col(i)) for i in range(m)),
+        compiler_params=pltpu.CompilerParams(vmem_limit_bytes=63 * 2 ** 20),
+        cost_estimate=pl.CostEstimate(flops=2 * m * ff * tall * hid, bytes_accessed=m * 4 * ff * hid, transcendentals=0),
+        name=name,
+    )(*lhs, *rhs)
 
 
 def solution(mesh):
@@ -350,11 +429,12 @@
         sem = pltpu.SemaphoreType.DMA
         full = jax.ShapeDtypeStruct((4, 2, tok, hid), BF16)
         act = jax.ShapeDtypeStruct((ff, tall), BF16)
-        dx, zt, dgt, dut, dya, xa = pl.pallas_call(
+        half = jax.ShapeDtypeStruct((2, tok, hid // 2), BF16)
+        sa, ka, sb, kb, zt, dgt, dut, dya, xa = pl.pallas_call(
             _comm_kernel,
-            out_shape=(jax.ShapeDtypeStruct((tok, hid), BF16), act, act, act, full, full),
+            out_shape=(half, half, half, half, act, act, act, full, full),
             in_specs=[any_] * 7,
-            out_specs=(any_,) * 6,
+            out_specs=(any_,) * 9,
             scratch_shapes=[
                 pltpu.VMEM((4, 2, tok, hid), BF16),
                 pltpu.VMEM((tall, fp), F32),
@@ -366,35 +446,34 @@
                 pltpu.VMEM((ff, tall), BF16),
                 pltpu.VMEM((ff, tall), BF16),
                 pltpu.VMEM((NH, 4, tok, hc), BF16),
-                pltpu.VMEM((NH, 2, tok, hc), BF16),
-                pltpu.VMEM((NH, tok, hc), BF16),
                 pltpu.VMEM((tok, hid), BF16),
-                pltpu.VMEM((tok, hid), BF16),
-                sem((NH, 7)), sem((NH, 7)), sem((NH, 7)), sem((NH, 7)), sem((NH, 4)), sem((NH, 4)),
-                sem((NH,)), sem((NH,)), sem((2, 2)), sem((2,)), sem((3,)), sem((NH,)),
+                sem((NH, 7)), sem((NH, 7)), sem((NH, 7)), sem((NH, 7)), sem((NH,)), sem((NH,)),
+                sem((NH,)), sem((NH,)), sem((2, 2)), sem((2,)), sem((2,)), sem((NH,)), sem((NH, 4)),
             ],
             compiler_params=pltpu.CompilerParams(collective_id=0, has_side_effects=True, vmem_limit_bytes=67043328),
-            name="gather_reduce",
+            name="gather_partial",
         )(x, dy, wd, wg.T, wu.T, ug.T, uu.T)
-
-        nb = 512
-        n = hid // nb
-        res = pl.BlockSpec((ff, tall), lambda j: (0, 0))
-        grad = jax.ShapeDtypeStruct((ff, hid), F32)
-        dwd, dwg, dwu = pl.pallas_call(
-            _weight_kernel,
-            grid=(3 * n,),
-            out_shape=(grad, grad, grad),
-            in_specs=[res, res, res,
-                      pl.BlockSpec((tall, nb), lambda j: (0, jnp.minimum(j, n - 1))),
-                      pl.BlockSpec((tall, nb), lambda j: (0, jnp.maximum(j - n, 0) // 2))],
-            out_specs=(pl.BlockSpec((ff, nb), lambda j: (0, jnp.minimum(j, n - 1))),
-                       pl.BlockSpec((ff, nb), lambda j: (0, jnp.maximum(j - n, 0) // 2)),
-                       pl.BlockSpec((ff, nb), lambda j: (0, jnp.maximum(j - n - 1, 0) // 2))),
-            compiler_params=pltpu.CompilerParams(vmem_limit_bytes=63 * 2 ** 20),
-            cost_estimate=pl.CostEstimate(flops=6 * ff * tall * hid, bytes_accessed=12 * ff * hid, transcendentals=0),
-            name="weight_grads",
-        )(zt, dgt, dut, dya.reshape(tall, hid), xa.reshape(tall, hid))
+        dya = dya.reshape(tall, hid)
+        xa = xa.reshape(tall, hid)
+
+        def to_x(v):
+            return lax.ppermute(v, 'tp', [(i, i ^ 2) for i in range(8)])
+
+        def to_y(v):
+            return lax.ppermute(v, 'tp', [(i, i ^ 4) for i in range(8)])
+
+        def plus(*terms):
+            return sum(v.astype(F32) for v in terms).astype(BF16)
+
+        ra, rb = to_x(sa), to_y(sb)
+        dwd, dwg = _weight_grads((zt, dgt), (dya, xa), "grads_down_gate")
+        ra, rb, dwd, dwg = lax.optimization_barrier((ra, rb, dwd, dwg))
+        ma, mb = plus(ka[1], ra[1]), plus(kb[1], rb[1])
+        ma, mb, dut = lax.optimization_barrier((ma, mb, dut))
+        fa, fb = to_y(ma), to_x(mb)
+        dwu, = _weight_grads((dut,), (xa,), "grads_up")
+        fa, fb, dwu = lax.optimization_barrier((fa, fb, dwu))
+        dx = jnp.concatenate([plus(ka[0], ra[0], fa), plus(kb[0], rb[0], fb)], axis=1)
         return dx, dwg.T, dwu.T, dwd
 
     tok_spec = P(('dp', 'tp'), None)

time: 183 us -> 159 us (0.87)
  Pallas kernels: 179 us -> 147 us
  other arithmetic: 0 us -> 6.85 us
  starting transfers between devices: 0 us -> 4.13 us
  local copies, waits for them, and re-layouts: 2.29 us -> 0 us
    pallas_call x2 -> x3, Pallas kernels: 179 us -> 147 us  [the longest x1 96.1 us: local_backward(): pl.pallas_call(_comm_kernel, out_shape=(half, half, half, half, act, act,...]
    convert_element_type x0 -> x3, other arithmetic: none -> 5.81 us  [plus(): return sum((v.astype(F32) for v in terms)).astype(BF16)]
    ppermute x0 -> x4, starting transfers between devices: none -> 4.13 us  [the longest x2 2.07 us: to_y(): return lax.ppermute(v, 'tp', [(i, i ^ 4) for i in range(8)])]
    unnamed x1 -> x0, local copies, waits for them, and re-layouts: 2.29 us -> none
  transfers between devices with their start and end apart: 0 -> 4, of which waited for: 0 -> 0; matrix products, arithmetic and copies ran while one was open for 0% -> 0% of each run, Pallas kernels for 0% -> 32%
where the time goes in v2:
time: 159 us
  Pallas kernels  147 us (92%)
  other arithmetic  6.85 us (4%)
  starting transfers between devices  4.13 us (3%)
    pallas_call x1, Pallas kernels, local_backward(): pl.pallas_call(_comm_kernel, out_shape=(half, half, half, half, act, act,...  96.1 us
    pallas_call x2, Pallas kernels, _weight_grads(): pl.pallas_call(functools.partial(_weight_kernel, n=n), grid=(m * n,), out...  50.8 us
    convert_element_type x3, other arithmetic, plus(): return sum((v.astype(F32) for v in terms)).astype(BF16)  5.81 us
  transfers between devices with their start and end apart: 4, of which 0 were waited for; matrix products, arithmetic and copies ran while one was open for 0% of the time, Pallas kernels for 32%

profile of v2, /device:TPU:0, one launch (start us, length us, event | category | flops | bytes accessed | tf_op | source)
XLA Modules:
  0.0 158.5 jit_solution(15199374084175337816)
XLA Ops:
  0.6 96.1 %gather_partial.1 = (bf16[2,128,2048]{2,1,0:T(8,128)(2,1)}, bf16[2,128,2048]{2,1,0:T(8,128)(2,1)}, bf16[2,128,2048]{2,1,0:T(8,128)(2,1)}, bf16[2,128,2048]{2,1,0...) custom-call(bf16[128,4096]{1,0:T(8,128)(2,1)} %x_ref.1, ...), custom_call_target="tpu_custom_call" | custom-call | tf_op jit(solution)/shard_map/gather_partial/pallas_call | solution.py:433
  96.7 1.2 collective-permute-start
  97.9 0.9 collective-permute-start.1
  98.7 33.4 %grads_down_gate.1 = (f32[1376,4096]{1,0:T(8,128)}, f32[1376,4096]{1,0:T(8,128)}) custom-call(bf16[1376,1024]{1,0:T(8,128)(2,1)} %get-tuple-element.28.refs_0_, bf16[1376,1024]{1,0:T(8,128)(2,1)} %get-tuple-element.29.refs_1_, bf16[1024,4096]{1,0:T(8,128)(2,1)} %bitcast.26, bf16[1024,4096]{1,0:T(8,128)(2,1)} %bitcast.24), custom_call_target="tpu_custom_call" | custom-call | flops 23085449216 | bytes 45088768 | tf_op jit(solution)/shard_map/grads_down_gate/pallas_call | solution.py:409
  132.1 0.0 collective-permute-done
  132.1 0.0 collective-permute-done.1
  132.1 2.1 %fusion.2 = bf16[128,2048]{1,0:T(8,128)(2,1)} fusion(bf16[2,128,2048]{2,1,0:T(8,128)(2,1)} %collective-permute-done, bf16[2,128,2048]{2,1,0:T(8,128)(2,1)} %get-tuple-element.25), kind=kLoop, calls=%fused_computation.7 | loop fusion | flops 1048576 | bytes 1572864 | tf_op jit(solution)/shard_map/convert_element_type | solution.py:466
  134.3 1.3 fusion.3
  135.6 1.2 collective-permute-start.2
  136.8 0.9 collective-permute-start.3
  137.7 17.4 %grads_up.1 = f32[1376,4096]{1,0:T(8,128)} custom-call(bf16[1376,1024]{1,0:T(8,128)(2,1)} %get-tuple-element.40.refs_0_, bf16[1024,4096]{1,0:T(8,128)(2,1)} %bitcast.25), custom_call_target="tpu_custom_call" | custom-call | flops 11542724608 | bytes 22544384 | tf_op jit(solution)/shard_map/grads_up/pallas_call | solution.py:409
  155.1 0.0 collective-permute-done.2
  155.1 0.0 collective-permute-done.3
  155.1 2.4 %fusion = (bf16[128,2048]{1,0:T(8,128)(2,1)S(1)}, bf16[128,2048]{1,0:T(8,128)(2,1)S(1)}) fusion(bf16[128,2048]{1,0:T(8,128)(2,1)} %collective-permute-done.3, bf16[2,128,2048]{2,1,0:T(8,128)(2,1)} %collective-permute-done.1, bf16[2,128,2048]{2,1,0:T(8,128)(2,1)} %get-tuple-element.35, bf16[128,2048]{1,0:T(8,128)(2,1)} %collective-permute-done.2, ...), kind=kLoop, calls=%fused_computation.2 | loop fusion | flops 3145728 | bytes 4194304 | tf_op jit(solution)/shard_map/convert_element_type | solution.py:466
  157.5 1.0 pad_maximum_fusion
Async XLA Ops:
  96.7 35.4 %collective-permute-start = (bf16[2,128,2048]{2,1,0:T(8,128)(2,1)}, bf16[2,128,2048]{2,1,0:T(8,128)(2,1)}, u32[]{:S(2)}, u32[]{:S(2)}) collective-permute-start(bf16[2,128,2048]{2,1,0:T(8,128)(2,1)} %get-tuple-element.26), channel_id=1, source_target_pairs={{0,2},{1,3},{2,0},{3,1},{4,6},{5,7},{6,4},{7,5},{8,10},{9,11},{10,... | collective-permute-start | bytes 3145736 | tf_op jit(solution)/shard_map/ppermute | solution.py:460
  97.9 34.3 %collective-permute-start.1 = (bf16[2,128,2048]{2,1,0:T(8,128)(2,1)}, bf16[2,128,2048]{2,1,0:T(8,128)(2,1)}, u32[]{:S(2)}, u32[]{:S(2)}) collective-permute-start(bf16[2,128,2048]{2,1,0:T(8,128)(2,1)} %get-tuple-element.27), channel_id=1, source_target_pairs={{0,4},{1,5},{2,6},{3,7},{4,0},{5,1},{6,2},{7,3},{8,12},{9,13},{10,... | collective-permute-start | bytes 3145736 | tf_op jit(solution)/shard_map/ppermute | solution.py:463
  135.6 19.5 %collective-permute-start.2 = (bf16[128,2048]{1,0:T(8,128)(2,1)}, bf16[128,2048]{1,0:T(8,128)(2,1)}, u32[]{:S(2)}, u32[]{:S(2)}) collective-permute-start(bf16[128,2048]{1,0:T(8,128)(2,1)} %fusion.2), channel_id=1, source_target_pairs={{0,4},{1,5},{2,6},{3,7},{4,0},{5,1},{6,2},{7,3},{8,12},{9,13},{10,... | collective-permute-start | bytes 1572872 | tf_op jit(solution)/shard_map/ppermute | solution.py:463
  136.8 18.3 %collective-permute-start.3 = (bf16[128,2048]{1,0:T(8,128)(2,1)S(1)}, bf16[128,2048]{1,0:T(8,128)(2,1)}, u32[]{:S(2)}, u32[]{:S(2)}) collective-permute-start(bf16[128,2048]{1,0:T(8,128)(2,1)S(1)} %fusion.3), channel_id=1, source_target_pairs={{0,2},{1,3},{2,0},{3,1},{4,6},{5,7},{6,4},{7,5},{8,10},{9,11},{10,... | collective-permute-start | bytes 1572872 | tf_op jit(solution)/shard_map/ppermute | solution.py:460

commit v3 on v2

--- a/solution.py
+++ b/solution.py
@@ -10,6 +10,7 @@
 MESH = pl.DeviceIdType.MESH
 BF16 = jnp.bfloat16
 F32 = jnp.float32
+AHEAD = 3
 NH = 8
 NT = (((1,), (1,)), ((), ()))
 
@@ -132,7 +133,7 @@
         pl.semaphore_signal(barrier, inc=1, device_id={"tp": dev}, device_id_type=MESH)
     pl.semaphore_wait(barrier, 3)
 
-    for k in range(2):
+    for k in range(AHEAD):
         y_local(k).wait()
         ag_own(dyv, ys, yr, k)
 
@@ -163,16 +164,16 @@
         utv[:, lanes] = uu.T.astype(BF16)
 
     def phase1(i, carry):
-        @pl.when(i < NH - 2)
-        def _():
-            y_local(i + 2).wait()
-            ag_own(dyv, ys, yr, i + 2)
+        @pl.when(i < NH - AHEAD)
+        def _():
+            y_local(i + AHEAD).wait()
+            ag_own(dyv, ys, yr, i + AHEAD)
 
         @pl.when(i < NH)
         def _():
             ag_mid(dyv, ys, yr, i)
 
-        for first, ks in ((NH - 1, range(0, 2)), (NH, range(2, 5)), (NH + 1, range(5, NH))):
+        for first, ks in ((NH - 1, range(0, 2)), (NH, range(2, 4)), (NH + 1, range(4, 6)), (NH + 2, range(6, NH))):
             @pl.when(i == first)
             def _():
                 for k in ks:
@@ -182,13 +183,13 @@
         def _():
             u_block(pl.multiple_of(i * 128, 128), 128)
 
-        @pl.when((i >= 1) & (i <= NH))
-        def _():
-            ag_last(dyv, ys, yr, i - 1)
-
-        @pl.when(i >= 2)
-        def _():
-            k = i - 2
+        @pl.when((i >= 2) & (i <= NH + 1))
+        def _():
+            ag_last(dyv, ys, yr, i - 2)
+
+        @pl.when(i >= 3)
+        def _():
+            k = i - 3
             ag_end(dyv, ys, yr, k)
             dy_out(k).start()
             wd_load(k).wait()
@@ -208,7 +209,7 @@
     for k in range(NH):
         x_local(k).wait()
         x_put(k).start()
-    lax.fori_loop(0, NH + 2, phase1, 0)
+    lax.fori_loop(0, NH + 3, phase1, 0)
     w_load(1, 0).start()
     w_load(1, 1).start()
     if rest:
@@ -251,13 +252,23 @@
         ugv[rows, :] = duv[:, lanes].T[:n]
         uuv[rows, :] = duv[:, pl.ds(fp + r0, 128)].T[:n]
 
+    per = -(-nfull // NH)
+
     def phase2(i, carry):
+        for first, ks in ((NH - 2, range(0, 3)), (NH - 1, range(3, 6)), (NH, range(6, NH))):
+            @pl.when(i == first)
+            def _():
+                for k in ks:
+                    ag_last(xa_ref, xs, xr, k)
+
         @pl.when(i < NH)
         def _():
             ag_mid(xa_ref, xs, xr, i)
             w_load(i, 0).wait()
             w_load(i, 1).wait()
             slot = (i + 1) % 2
+            for b in range(per):
+                t_block(pl.multiple_of(jnp.minimum(per * i + b, nfull - 1) * 128, 128), 128)
             for n in range(0, hc, 256):
                 p = lax.dot_general(duv[:, :fp], wbuf[slot, 0, :, n:n + 256], (((1,), (0,)), ((), ())),
                                     preferred_element_type=F32)
@@ -270,11 +281,6 @@
                 w_load(i + 2, 0).start()
                 w_load(i + 2, 1).start()
 
-        for b in (2 * i, 2 * i + 1):
-            @pl.when(b < nfull)
-            def _():
-                t_block(pl.multiple_of(b * 128, 128), 128)
-
         @pl.when(i < NH)
         def _():
             rs0(i, 1 - tc).start()
@@ -282,7 +288,6 @@
         @pl.when((i >= 1) & (i <= NH))
         def _():
             k = i - 1
-            ag_last(xa_ref, xs, xr, k)
             rs0(k, tc).wait_recv()
             for q in range(4):
                 add(2 * q + tc, k, r0v[k, q])
@@ -333,6 +338,21 @@
     lax.fori_loop(0, NH, drain, 0)
     for o in outs:
         o.wait()
+
+
+def _plus(*terms):
+    return sum(v.astype(F32) for v in terms).astype(BF16)
+
+
+def _pass_kernel(ka_ref, ra_ref, kb_ref, rb_ref, ma_ref, mb_ref):
+    ma_ref[...] = _plus(ka_ref[0], ra_ref[0])
+    mb_ref[...] = _plus(kb_ref[0], rb_ref[0])
+
+
+def _join_kernel(ka_ref, ra_ref, fa_ref, kb_ref, rb_ref, fb_ref, dx_ref):
+    h = fa_ref.shape[1]
+    dx_ref[:, :h] = _plus(ka_ref[0], ra_ref[0], fa_ref[...])
+    dx_ref[:, h:] = _plus(kb_ref[0], rb_ref[0], fb_ref[...])
 
 
 def _row_chunks(ff):
@@ -462,18 +482,23 @@
         def to_y(v):
             return lax.ppermute(v, 'tp', [(i, i ^ 4) for i in range(8)])
 
-        def plus(*terms):
-            return sum(v.astype(F32) for v in terms).astype(BF16)
-
         ra, rb = to_x(sa), to_y(sb)
         dwd, dwg = _weight_grads((zt, dgt), (dya, xa), "grads_down_gate")
         ra, rb, dwd, dwg = lax.optimization_barrier((ra, rb, dwd, dwg))
-        ma, mb = plus(ka[1], ra[1]), plus(kb[1], rb[1])
+        rows = tok // 2
+        flat = pl.BlockSpec((rows, hid // 2), lambda j: (j, 0))
+        pair = jax.ShapeDtypeStruct((tok, hid // 2), BF16)
+        second = pl.BlockSpec((1, rows, hid // 2), lambda j: (1, j, 0))
+        ma, mb = pl.pallas_call(_pass_kernel, out_shape=(pair, pair), in_specs=[second] * 4, out_specs=(flat, flat), grid=(2,),
+                                name="pass_on")(ka, ra, kb, rb)
         ma, mb, dut = lax.optimization_barrier((ma, mb, dut))
         fa, fb = to_y(ma), to_x(mb)
         dwu, = _weight_grads((dut,), (xa,), "grads_up")
         fa, fb, dwu = lax.optimization_barrier((fa, fb, dwu))
-        dx = jnp.concatenate([plus(ka[0], ra[0], fa), plus(kb[0], rb[0], fb)], axis=1)
+        first = pl.BlockSpec((1, rows, hid // 2), lambda j: (0, j, 0))
+        dx = pl.pallas_call(_join_kernel, out_shape=jax.ShapeDtypeStruct((tok, hid), BF16),
+                            in_specs=[first, first, flat, first, first, flat],
+                            out_specs=pl.BlockSpec((rows, hid), lambda j: (j, 0)), grid=(2,), name="join")(ka, ra, fa, kb, rb, fb)
         return dx, dwg.T, dwu.T, dwd
 
     tok_spec = P(('dp', 'tp'), None)

time: 159 us -> 148 us (0.931)
  other arithmetic: 6.85 us -> 0 us
  Pallas kernels: 147 us -> 142 us
    pallas_call x1, Pallas kernels: 96.1 us -> 86.4 us  [local_backward(): pl.pallas_call(_comm_kernel, out_shape=(half, half, half, half, act, act,...]
    convert_element_type x3 -> x0, other arithmetic: 5.81 us -> none  [plus(): return sum((v.astype(F32) for v in terms)).astype(BF16)]
    pallas_call x0 -> x2, Pallas kernels: none -> 5.18 us  [the longest x1 2.81 us: local_backward(): pl.pallas_call(_join_kernel, out_shape=jax.ShapeDtypeStruct((tok, hid), B...]
  transfers between devices with their start and end apart: 4 -> 4, of which waited for: 0 -> 0; matrix products, arithmetic and copies ran while one was open for 0% -> 0% of each run, Pallas kernels for 32% -> 34%
where the time goes in v3:
time: 148 us
  Pallas kernels  142 us (96%)
  starting transfers between devices  4.08 us (3%)
    pallas_call x1, Pallas kernels, local_backward(): pl.pallas_call(_comm_kernel, out_shape=(half, half, half, half, act, act,...  86.4 us
    pallas_call x2, Pallas kernels, _weight_grads(): pl.pallas_call(functools.partial(_weight_kernel, n=n), grid=(m * n,), out...  50.8 us
  transfers between devices with their start and end apart: 4, of which 0 were waited for; matrix products, arithmetic and copies ran while one was open for 0% of the time, Pallas kernels for 34%

profile of v3, /device:TPU:0, one launch (start us, length us, event | category | flops | bytes accessed | tf_op | source)
XLA Modules:
  0.0 148.0 jit_solution(15584404557219180366)
XLA Ops:
  0.6 86.4 %gather_partial.1 = (bf16[2,128,2048]{2,1,0:T(8,128)(2,1)}, bf16[2,128,2048]{2,1,0:T(8,128)(2,1)}, bf16[2,128,2048]{2,1,0:T(8,128)(2,1)}, bf16[2,128,2048]{2,1,0...) custom-call(bf16[128,4096]{1,0:T(8,128)(2,1)} %x_ref.1, ...), custom_call_target="tpu_custom_call" | custom-call | tf_op jit(solution)/shard_map/gather_partial/pallas_call | solution.py:453
  87.0 1.0 collective-permute-start
  88.0 1.1 collective-permute-start.1
  89.1 33.4 %grads_down_gate.1 = (f32[1376,4096]{1,0:T(8,128)}, f32[1376,4096]{1,0:T(8,128)}) custom-call(bf16[1376,1024]{1,0:T(8,128)(2,1)} %get-tuple-element.30.refs_0_, bf16[1376,1024]{1,0:T(8,128)(2,1)} %get-tuple-element.31.refs_1_, bf16[1024,4096]{1,0:T(8,128)(2,1)} %bitcast.14, bf16[1024,4096]{1,0:T(8,128)(2,1)} %bitcast.12), custom_call_target="tpu_custom_call" | custom-call | flops 23085449216 | bytes 45088768 | tf_op jit(solution)/shard_map/grads_down_gate/pallas_call | solution.py:429
  122.5 0.0 collective-permute-done.ra_ref
  122.5 0.0 collective-permute-done.1.rb_ref
  122.5 2.4 %pass_on.1 = (bf16[128,2048]{1,0:T(8,128)(2,1)}, bf16[128,2048]{1,0:T(8,128)(2,1)}) custom-call(bf16[2,128,2048]{2,1,0:T(8,128)(2,1)} %get-tuple-element.27.ka_ref, bf16[2,128,2048]{2,1,0:T(8,128)(2,1)} %collective-permute-done.ra_ref, bf16[2,128,2048]{2,1,0:T(8,128)(2,1)} %get-tuple-element.37.kb_ref, bf16[2,128,2048]{2,1,0:T(8,128)(2,1)} %collective-permute-done.1.rb_ref), custom_call_target="tpu_custom_call" | custom-call | tf_op jit(solution)/shard_map/pass_on/pallas_call | solution.py:492
  124.9 0.9 collective-permute-start.2
  125.8 1.1 collective-permute-start.3
  126.9 17.4 %grads_up.1 = f32[1376,4096]{1,0:T(8,128)} custom-call(bf16[1376,1024]{1,0:T(8,128)(2,1)} %get-tuple-element.44.refs_0_, bf16[1024,4096]{1,0:T(8,128)(2,1)} %bitcast.13), custom_call_target="tpu_custom_call" | custom-call | flops 11542724608 | bytes 22544384 | tf_op jit(solution)/shard_map/grads_up/pallas_call | solution.py:429
  144.3 0.0 collective-permute-done.2.fa_ref
  144.4 0.0 copy-start
  144.4 0.0 collective-permute-done.3.fb_ref
  144.4 0.8 copy-done
  145.1 2.8 %join.1 = bf16[128,4096]{1,0:T(8,128)(2,1)} custom-call(bf16[2,128,2048]{2,1,0:T(8,128)(2,1)} %get-tuple-element.27.ka_ref, bf16[2,128,2048]{2,1,0:T(8,128)(2,1)} %collective-permute-done.ra_ref, bf16[128,2048]{1,0:T(8,128)(2,1)} %copy-done, bf16[2,128,2048]{2,1,0:T(8,128)(2,1)} %get-tuple-element.37.kb_ref, ...), custom_call_target="tpu_custom_call" | custom-call | tf_op jit(solution)/shard_map/join/pallas_call | solution.py:499
Async XLA Ops:
  87.0 35.5 %collective-permute-start = (bf16[2,128,2048]{2,1,0:T(8,128)(2,1)}, bf16[2,128,2048]{2,1,0:T(8,128)(2,1)}, u32[]{:S(2)}, u32[]{:S(2)}) collective-permute-start(bf16[2,128,2048]{2,1,0:T(8,128)(2,1)} %get-tuple-element.28), channel_id=1, source_target_pairs={{0,2},{1,3},{2,0},{3,1},{4,6},{5,7},{6,4},{7,5},{8,10},{9,11},{10,... | collective-permute-start | bytes 3145736 | tf_op jit(solution)/shard_map/ppermute | solution.py:480
  88.0 34.5 %collective-permute-start.1 = (bf16[2,128,2048]{2,1,0:T(8,128)(2,1)}, bf16[2,128,2048]{2,1,0:T(8,128)(2,1)}, u32[]{:S(2)}, u32[]{:S(2)}) collective-permute-start(bf16[2,128,2048]{2,1,0:T(8,128)(2,1)} %get-tuple-element.29), channel_id=1, source_target_pairs={{0,4},{1,5},{2,6},{3,7},{4,0},{5,1},{6,2},{7,3},{8,12},{9,13},{10,... | collective-permute-start | bytes 3145736 | tf_op jit(solution)/shard_map/ppermute | solution.py:483
  124.9 19.5 %collective-permute-start.2 = (bf16[128,2048]{1,0:T(8,128)(2,1)}, bf16[128,2048]{1,0:T(8,128)(2,1)S(1)}, u32[]{:S(2)}, u32[]{:S(2)}) collective-permute-start(bf16[128,2048]{1,0:T(8,128)(2,1)} %get-tuple-element.42), channel_id=1, source_target_pairs={{0,4},{1,5},{2,6},{3,7},{4,0},{5,1},{6,2},{7,3},{8,12},{9,13},{10,... | collective-permute-start | bytes 1572872 | tf_op jit(solution)/shard_map/ppermute | solution.py:483
  125.8 18.5 %collective-permute-start.3 = (bf16[128,2048]{1,0:T(8,128)(2,1)}, bf16[128,2048]{1,0:T(8,128)(2,1)}, u32[]{:S(2)}, u32[]{:S(2)}) collective-permute-start(bf16[128,2048]{1,0:T(8,128)(2,1)} %get-tuple-element.43), channel_id=1, source_target_pairs={{0,2},{1,3},{2,0},{3,1},{4,6},{5,7},{6,4},{7,5},{8,10},{9,11},{10,... | collective-permute-start | bytes 1572872 | tf_op jit(solution)/shard_map/ppermute | solution.py:480
  144.4 0.8 copy-start

commit v4 on v3

--- a/solution.py
+++ b/solution.py
@@ -10,8 +10,9 @@
 MESH = pl.DeviceIdType.MESH
 BF16 = jnp.bfloat16
 F32 = jnp.float32
-AHEAD = 3
 NH = 8
+NY = 16
+AHEAD, LAG, TAKE = 4, 4, 6
 NT = (((1,), (1,)), ((), ()))
 
 
@@ -20,9 +21,9 @@
 
 
 def _comm_kernel(x_ref, dy_ref, wd_ref, wg_ref, wu_ref, ug_ref, uu_ref,
-                 sa_ref, ka_ref, sb_ref, kb_ref, zt_ref, dgt_ref, dut_ref, dya_ref, xa_ref,
-                 dyv, gv, av, spv, utv, duv, wbuf, ugv, uuv, r0v, xov,
-                 ys, yr, xs, xr, rs, rr, yl, xl, wl, ul, ol, dl, po):
+                 so_ref, sx_ref, sy_ref, sd_ref, zt_ref, dgt_ref, dut_ref, dya_ref, xa_ref,
+                 dyv, gv, av, spv, utv, duv, wbuf, ugv, uuv, r0v, r1v, xov,
+                 ys, yr, xs, xr, rs, rr, r1s, r1r, yl, xl, wl, ul, ol, dl, po):
     tok, hid = dy_ref.shape
     ff = wd_ref.shape[0]
     fp = _lanes(ff)
@@ -44,18 +45,22 @@
     def n2(k):
         return yn + (xn - yn) * (k % 2)
 
-    def cols(k):
-        return pl.ds(pl.multiple_of(k * hc, hc), hc)
-
-    def blk(ref, owner, k):
-        return ref.at[owner // 2, owner % 2, :, cols(k)]
+    hy = hid // NY
+    per_h = NY // NH
+
+    def cols(k, w=hc):
+        return pl.ds(pl.multiple_of(k * w, w), w)
+
+    def blk(ref, owner, k, w=hc):
+        return ref.at[owner // 2, owner % 2, :, cols(k, w)]
 
     def rcopy(src, dst, ss, rs_, dev):
         return pltpu.make_async_remote_copy(src_ref=src, dst_ref=dst, send_sem=ss, recv_sem=rs_,
                                             device_id={"tp": dev}, device_id_type=MESH)
 
     def ag(buf, ss, sr, k, j, owner, dev):
-        return rcopy(blk(buf, owner, k), blk(buf, owner, k), ss.at[k, j], sr.at[k, j], dev)
+        w = hid // ss.shape[0]
+        return rcopy(blk(buf, owner, k, w), blk(buf, owner, k, w), ss.at[k, j], sr.at[k, j], dev)
 
     def ag_own(buf, ss, sr, k):
         ag(buf, ss, sr, k, 0, t, n1(k)).start()
@@ -98,7 +103,7 @@
         ag(buf, ss, sr, k, 6, dg, pn).wait_send()
 
     def y_local(k):
-        return pltpu.make_async_copy(dy_ref.at[:, cols(k)], blk(dyv, t, k), yl.at[k])
+        return pltpu.make_async_copy(dy_ref.at[:, cols(k, hy)], blk(dyv, t, k, hy), yl.at[k])
 
     def x_local(k):
         return pltpu.make_async_copy(x_ref.at[:, cols(k)], xov.at[:, cols(k)], xl.at[k])
@@ -119,7 +124,7 @@
 
     ug_in = pltpu.make_async_copy(ug_ref, ugv, ul.at[0])
     uu_in = pltpu.make_async_copy(uu_ref, uuv, ul.at[1])
-    for k in range(NH):
+    for k in range(NY):
         y_local(k).start()
     wd_load(0).start()
     wd_load(1).start()
@@ -164,33 +169,39 @@
         utv[:, lanes] = uu.T.astype(BF16)
 
     def phase1(i, carry):
-        @pl.when(i < NH - AHEAD)
+        @pl.when(i < NY - AHEAD)
         def _():
             y_local(i + AHEAD).wait()
             ag_own(dyv, ys, yr, i + AHEAD)
 
-        @pl.when(i < NH)
+        @pl.when(i < NY)
         def _():
             ag_mid(dyv, ys, yr, i)
 
-        for first, ks in ((NH - 1, range(0, 2)), (NH, range(2, 4)), (NH + 1, range(4, 6)), (NH + 2, range(6, NH))):
-            @pl.when(i == first)
-            def _():
-                for k in ks:
-                    x_send(k)
+        @pl.when(i >= NY + TAKE - NH)
+        def _():
+            x_send(i - (NY + TAKE - NH))
 
         @pl.when(i < nfull)
         def _():
             u_block(pl.multiple_of(i * 128, 128), 128)
 
-        @pl.when((i >= 2) & (i <= NH + 1))
-        def _():
-            ag_last(dyv, ys, yr, i - 2)
-
-        @pl.when(i >= 3)
-        def _():
-            k = i - 3
-            ag_end(dyv, ys, yr, k)
+        if rest:
+            @pl.when(i == nfull)
+            def _():
+                u_block(nfull * 128, rest)
+
+        @pl.when((i >= LAG) & (i < NY + LAG))
+        def _():
+            ag_last(dyv, ys, yr, i - LAG)
+
+        @pl.when(i >= TAKE)
+        def _():
+            ag_end(dyv, ys, yr, i - TAKE)
+
+        @pl.when((i >= TAKE) & ((i - TAKE) % per_h == per_h - 1))
+        def _():
+            k = (i - TAKE) // per_h
             dy_out(k).start()
             wd_load(k).wait()
             dyc = dyv[:, :, :, cols(k)].reshape(tall, hc)
@@ -209,11 +220,9 @@
     for k in range(NH):
         x_local(k).wait()
         x_put(k).start()
-    lax.fori_loop(0, NH + 3, phase1, 0)
+    lax.fori_loop(0, NY + TAKE, phase1, 0)
     w_load(1, 0).start()
     w_load(1, 1).start()
-    if rest:
-        u_block(nfull * 128, rest)
     zt_out = pltpu.make_async_copy(ugv, zt_ref, ol.at[0])
     zt_out.start()
     def gates(i, carry):
@@ -227,20 +236,23 @@
 
     def sent(k, carry):
         ag_sent(dyv, ys, yr, k)
+        return carry
+
+    lax.fori_loop(0, NY, sent, 0)
+    for k in range(NH):
         dy_out(k).wait()
-        return carry
-
-    lax.fori_loop(0, NH, sent, 0)
     zt_out.wait()
 
     def rs0(k, c):
         return rcopy(dyv.at[:, c, :, cols(k)], r0v.at[k], rs.at[k], rr.at[k], pn)
 
-    def sums_out(k, left):
-        kk = k if left else k - half
-        send, keep, far, near = (sa_ref, ka_ref, xn, yn) if left else (sb_ref, kb_ref, yn, xn)
-        return [pltpu.make_async_copy(blk(dyv, owner, k), ref.at[b, :, cols(kk)], po.at[k, 2 * a + b])
-                for a, ref, owners in ((0, send, (far, dg)), (1, keep, (t, near))) for b, owner in enumerate(owners)]
+    def rs1(k):
+        return rcopy(blk(dyv, dg, k), r1v.at[k], r1s.at[k], r1r.at[k], n1(k))
+
+    def sums_out(k, diagonal):
+        outs = [(so_ref, t, k), (sx_ref, xn, k), (sy_ref, yn, k)] + ([(sd_ref, dg, k - half)] if diagonal else [])
+        return [pltpu.make_async_copy(blk(dyv, owner, k), ref.at[:, cols(c)], po.at[k, i])
+                for i, (ref, owner, c) in enumerate(outs)]
 
     def add(owner, k, other):
         b = blk(dyv, owner, k)
@@ -294,13 +306,20 @@
 
             @pl.when(k < half)
             def _():
+                rs1(k).start()
+
+            @pl.when(k >= half)
+            def _():
                 for o in sums_out(k, True):
                     o.start()
 
-            @pl.when(k >= half)
-            def _():
-                for o in sums_out(k, False):
-                    o.start()
+        @pl.when((i >= half) & (i < NH))
+        def _():
+            k = i - half
+            rs1(k).wait_recv()
+            add(n2(k), k, r1v[k])
+            for o in sums_out(k, False):
+                o.start()
 
         return carry
 
@@ -325,12 +344,13 @@
 
         @pl.when(k < half)
         def _():
+            rs1(k).wait_send()
+            for o in sums_out(k, False):
+                o.wait()
+
+        @pl.when(k >= half)
+        def _():
             for o in sums_out(k, True):
-                o.wait()
-
-        @pl.when(k >= half)
-        def _():
-            for o in sums_out(k, False):
                 o.wait()
 
         return carry
@@ -344,15 +364,10 @@
     return sum(v.astype(F32) for v in terms).astype(BF16)
 
 
-def _pass_kernel(ka_ref, ra_ref, kb_ref, rb_ref, ma_ref, mb_ref):
-    ma_ref[...] = _plus(ka_ref[0], ra_ref[0])
-    mb_ref[...] = _plus(kb_ref[0], rb_ref[0])
-
-
-def _join_kernel(ka_ref, ra_ref, fa_ref, kb_ref, rb_ref, fb_ref, dx_ref):
-    h = fa_ref.shape[1]
-    dx_ref[:, :h] = _plus(ka_ref[0], ra_ref[0], fa_ref[...])
-    dx_ref[:, h:] = _plus(kb_ref[0], rb_ref[0], fb_ref[...])
+def _join_kernel(so_ref, fx_ref, fy_ref, fd_ref, dx_ref):
+    h = fd_ref.shape[1]
+    dx_ref[:, :h] = _plus(so_ref[:, :h], fx_ref[:, :h], fy_ref[:, :h])
+    dx_ref[:, h:] = _plus(so_ref[:, h:], fx_ref[:, h:], fy_ref[:, h:], fd_ref[...])
 
 
 def _row_chunks(ff):
@@ -361,20 +376,42 @@
     return [16 * min(size, n - i) for i in range(0, n, size)]
 
 
-def _weight_kernel(*refs, n):
-    m = len(refs) // 3
-    lhs, rhs, out = refs[:m], refs[m:2 * m], refs[2 * m:]
-    ff, tall = lhs[0].shape
-    nb = out[0].shape[1]
+def _weight_kernel(zt_ref, dgt_ref, dut_ref, dy_ref, x_ref, dd_ref, dg_ref, du_ref,
+                   zv, dgv, duv, yv, xv, o0, o1, o2, ls, ysem, xsem, os):
+    ff, tall = zt_ref.shape
+    hid = dy_ref.shape[1]
+    nb = yv.shape[-1]
+    n = hid // nb
     sizes = _row_chunks(ff)
-    j = pl.program_id(0)
-
-    def product(a, b, o, accs):
+    depth = tall // 256
+
+    def load(src, dst, sem, j, p):
+        lo = pl.ds(pl.multiple_of(j * nb + p * 512, 512), 512)
+        return pltpu.make_async_copy(src.at[:, lo], dst.at[j % 2, :, p * 512:p * 512 + 512], sem.at[j % 2, p])
+
+    def loads(j):
+        return [load(src, dst, sem, j, p) for src, dst, sem in ((dy_ref, yv, ysem), (x_ref, xv, xsem))
+                for p in range(nb // 512)]
+
+    def put(i, j, rows, width, p):
+        stage, out = ((o0, dd_ref), (o1, dg_ref), (o2, du_ref))[i]
+        lo = pl.ds(pl.multiple_of(j * nb + p * 512, 512), width)
+        slot = j % stage.shape[0]
+        return pltpu.make_async_copy(stage.at[slot, rows, p * 512:p * 512 + width], out.at[rows, lo], os.at[i, slot])
+
+    def put_all(i, j):
+        return put(i, j, pl.ds(0, ff), nb, 0)
+
+    def product(i, j, accs, waits):
+        a = (zv, dgv, duv)[i]
+        b = (yv, xv, xv)[i].at[j % 2]
+        stage = (o0, o1, o2)[i]
+        slot = j % stage.shape[0]
         steps = []
         for pair in range(nb // 512):
             row = 0
             for c, size in enumerate(sizes):
-                for kt in range(tall // 256):
+                for kt in range(depth):
                     steps.append((pair, c, row, size, kt))
                 row += size
 
@@ -387,55 +424,93 @@
         def pop(pair, c, row, size):
             for q in range(2):
                 lo = pair * 512 + q * 256
-                o[row:row + size, lo:lo + 256] = pltpu.matmul_pop(accs[q][c])
-
-        push(0)
+                stage[slot, row:row + size, lo:lo + 256] = pltpu.matmul_pop(accs[q][c])
+            put(i, j, pl.ds(row, size), 512, pair).start()
+
         late = None
         for s, (pair, c, row, size, kt) in enumerate(steps):
-            if s + 1 < len(steps):
+            if s == 0 or (c == 0 and kt == 0 and waits):
+                for w in waits[pair] if waits else ():
+                    w.wait()
+                push(s)
+            if s + 1 < len(steps) and not (waits and steps[s + 1][1] == 0 and steps[s + 1][4] == 0):
                 push(s + 1)
             block = a[row:row + size, kt * 256:kt * 256 + 256]
             for q in range(2):
                 pltpu.matmul_acc_lhs(accs[q][c], block, load_staged_rhs=s % 2)
             if kt == 0 and late is not None:
                 pop(*late)
-            if kt == tall // 256 - 1:
+            if kt == depth - 1:
                 late = (pair, c, row, size)
         pop(*late)
 
+    zl, gl, ul = (pltpu.make_async_copy(src, dst, ls.at[i])
+                  for i, (src, dst) in enumerate(((zt_ref, zv), (dgt_ref, dgv), (dut_ref, duv))))
+    first = loads(0)
+    zl.start()
+    for c in first[:2]:
+        c.start()
+    gl.start()
+    for c in first[2:]:
+        c.start()
+    ul.start()
+    for c in loads(1):
+        c.start()
+
     def body(*flat):
-        half = len(flat) // 2
-        accs = []
-        for part in (flat[:half], flat[half:]):
-            accs.append([part[2] if i == len(sizes) - 1 else part[i % 2] for i in range(len(sizes))])
-        for i in range(m):
-            @pl.when((j >= i * n) & (j < (i + 1) * n))
-            def _():
-                product(lhs[i], rhs[i], out[i], accs)
+        h = len(flat) // 2
+        accs = [[part[2] if i == len(sizes) - 1 else part[i % 2] for i in range(len(sizes))]
+                for part in (flat[:h], flat[h:])]
+        product(0, 0, accs, [[zl, first[0]], [first[1]]])
+        product(1, 0, accs, [[gl, first[2]], [first[3]]])
+        product(2, 0, accs, [[ul], []])
+
+        def rest(j, carry):
+            for c in loads(j):
+                c.wait()
+
+            @pl.when(j + 1 < n)
+            def _():
+                for c in loads(j + 1):
+                    c.start()
+
+            put_all(0, j - 1).wait()
+            put_all(1, j - 1).wait()
+
+            @pl.when(j >= 2)
+            def _():
+                put_all(2, j - 2).wait()
+
+            for i in range(3):
+                product(i, j, accs, None)
+            return carry
+
+        lax.fori_loop(1, n, rest, 0)
 
     pl.run_scoped(body, *[pltpu.ACC(q)((size, 256), F32) for q in range(2) for size in (sizes[0], sizes[0], sizes[-1])])
-
-
-def _weight_grads(lhs, rhs, name):
-    m = len(lhs)
-    ff, tall = lhs[0].shape
-    hid = rhs[0].shape[1]
+    put_all(0, n - 1).wait()
+    put_all(1, n - 1).wait()
+    put_all(2, n - 2).wait()
+    put_all(2, n - 1).wait()
+
+
+def _weight_grads(zt, dgt, dut, dy, x):
+    ff, tall = zt.shape
+    hid = x.shape[1]
     nb = 1024
-    n = hid // nb
-
-    def col(i):
-        return lambda j: (0, jnp.clip(j - i * n, 0, n - 1))
-
+    sem = pltpu.SemaphoreType.DMA
+    any_ = pl.BlockSpec(memory_space=pl.ANY)
     return pl.pallas_call(
-        functools.partial(_weight_kernel, n=n),
-        grid=(m * n,),
-        out_shape=(jax.ShapeDtypeStruct((ff, hid), F32),) * m,
-        in_specs=[pl.BlockSpec((ff, tall), lambda j: (0, 0))] * m + [pl.BlockSpec((tall, nb), col(i)) for i in range(m)],
-        out_specs=tuple(pl.BlockSpec((ff, nb), col(i)) for i in range(m)),
+        _weight_kernel,
+        out_shape=(jax.ShapeDtypeStruct((ff, hid), F32),) * 3,
+        in_specs=[any_] * 5,
+        out_specs=(any_,) * 3,
+        scratch_shapes=[pltpu.VMEM((ff, tall), BF16)] * 3 + [pltpu.VMEM((2, tall, nb), BF16)] * 2
+        + [pltpu.VMEM((k, ff, nb), F32) for k in (1, 1, 2)] + [sem((3,)), sem((2, 2)), sem((2, 2)), sem((3, 2))],
         compiler_params=pltpu.CompilerParams(vmem_limit_bytes=63 * 2 ** 20),
-        cost_estimate=pl.CostEstimate(flops=2 * m * ff * tall * hid, bytes_accessed=m * 4 * ff * hid, transcendentals=0),
-        name=name,
-    )(*lhs, *rhs)
+        cost_estimate=pl.CostEstimate(flops=6 * ff * tall * hid, bytes_accessed=12 * ff * hid, transcendentals=0),
+        name="weight_grads",
+    )(zt, dgt, dut, dy, x)
 
 
 def solution(mesh):
@@ -449,10 +524,11 @@
         sem = pltpu.SemaphoreType.DMA
         full = jax.ShapeDtypeStruct((4, 2, tok, hid), BF16)
         act = jax.ShapeDtypeStruct((ff, tall), BF16)
-        half = jax.ShapeDtypeStruct((2, tok, hid // 2), BF16)
-        sa, ka, sb, kb, zt, dgt, dut, dya, xa = pl.pallas_call(
+        own = jax.ShapeDtypeStruct((tok, hid), BF16)
+        half = jax.ShapeDtypeStruct((tok, hid // 2), BF16)
+        so, sx, sy, sd, zt, dgt, dut, dya, xa = pl.pallas_call(
             _comm_kernel,
-            out_shape=(half, half, half, half, act, act, act, full, full),
+            out_shape=(own, own, own, half, act, act, act, full, full),
             in_specs=[any_] * 7,
             out_specs=(any_,) * 9,
             scratch_shapes=[
@@ -466,9 +542,10 @@
                 pltpu.VMEM((ff, tall), BF16),
                 pltpu.VMEM((ff, tall), BF16),
                 pltpu.VMEM((NH, 4, tok, hc), BF16),
+                pltpu.VMEM((NH // 2, tok, hc), BF16),
                 pltpu.VMEM((tok, hid), BF16),
-                sem((NH, 7)), sem((NH, 7)), sem((NH, 7)), sem((NH, 7)), sem((NH,)), sem((NH,)),
-                sem((NH,)), sem((NH,)), sem((2, 2)), sem((2,)), sem((2,)), sem((NH,)), sem((NH, 4)),
+                sem((NY, 7)), sem((NY, 7)), sem((NH, 7)), sem((NH, 7)), sem((NH,)), sem((NH,)),
+                sem((NH // 2,)), sem((NH // 2,)), sem((NY,)), sem((NH,)), sem((2, 2)), sem((2,)), sem((2,)), sem((NH,)), sem((NH, 4)),
             ],
             compiler_params=pltpu.CompilerParams(collective_id=0, has_side_effects=True, vmem_limit_bytes=67043328),
             name="gather_partial",
@@ -476,29 +553,17 @@
         dya = dya.reshape(tall, hid)
         xa = xa.reshape(tall, hid)
 
-        def to_x(v):
-            return lax.ppermute(v, 'tp', [(i, i ^ 2) for i in range(8)])
-
-        def to_y(v):
-            return lax.ppermute(v, 'tp', [(i, i ^ 4) for i in range(8)])
-
-        ra, rb = to_x(sa), to_y(sb)
-        dwd, dwg = _weight_grads((zt, dgt), (dya, xa), "grads_down_gate")
-        ra, rb, dwd, dwg = lax.optimization_barrier((ra, rb, dwd, dwg))
+        def to(v, flip):
+            return lax.ppermute(v, 'tp', [(i, i ^ flip) for i in range(8)])
+
+        fx, fy, fd = to(sx, 2), to(sy, 4), to(sd, 6)
+        dwd, dwg, dwu = _weight_grads(zt, dgt, dut, dya, xa)
+        fx, fy, fd, dwd, dwg, dwu = lax.optimization_barrier((fx, fy, fd, dwd, dwg, dwu))
         rows = tok // 2
-        flat = pl.BlockSpec((rows, hid // 2), lambda j: (j, 0))
-        pair = jax.ShapeDtypeStruct((tok, hid // 2), BF16)
-        second = pl.BlockSpec((1, rows, hid // 2), lambda j: (1, j, 0))
-        ma, mb = pl.pallas_call(_pass_kernel, out_shape=(pair, pair), in_specs=[second] * 4, out_specs=(flat, flat), grid=(2,),
-                                name="pass_on")(ka, ra, kb, rb)
-        ma, mb, dut = lax.optimization_barrier((ma, mb, dut))
-        fa, fb = to_y(ma), to_x(mb)
-        dwu, = _weight_grads((dut,), (xa,), "grads_up")
-        fa, fb, dwu = lax.optimization_barrier((fa, fb, dwu))
-        first = pl.BlockSpec((1, rows, hid // 2), lambda j: (0, j, 0))
-        dx = pl.pallas_call(_join_kernel, out_shape=jax.ShapeDtypeStruct((tok, hid), BF16),
-                            in_specs=[first, first, flat, first, first, flat],
-                            out_specs=pl.BlockSpec((rows, hid), lambda j: (j, 0)), grid=(2,), name="join")(ka, ra, fa, kb, rb, fb)
+        wide = pl.BlockSpec((rows, hid), lambda j: (j, 0))
+        dx = pl.pallas_call(_join_kernel, grid=(2,), out_shape=own, out_specs=wide,
+                            in_specs=[wide, wide, wide, pl.BlockSpec((rows, hid // 2), lambda j: (j, 0))],
+                            name="join")(so, fx, fy, fd)
         return dx, dwg.T, dwu.T, dwd
 
     tok_spec = P(('dp', 'tp'), None)

time: 148 us -> 134 us (0.905)
  Pallas kernels: 142 us -> 129 us
    pallas_call x5 -> x3, Pallas kernels: 142 us -> 129 us  [the longest x1 86.5 us: local_backward(): pl.pallas_call(_comm_kernel, out_shape=(own, own, own, half, act, act, ac...]
    ppermute x4 -> x3, starting transfers between devices: 4.08 us -> 3.52 us  [to(): return lax.ppermute(v, 'tp', [(i, i ^ flip) for i in range(8)])]
  transfers between devices with their start and end apart: 4 -> 3, of which waited for: 0 -> 0; matrix products, arithmetic and copies ran while one was open for 0% -> 0% of each run, Pallas kernels for 34% -> 30%
where the time goes in v4:
time: 134 us
  Pallas kernels  129 us (96%)
  starting transfers between devices  3.52 us (3%)
    pallas_call x1, Pallas kernels, local_backward(): pl.pallas_call(_comm_kernel, out_shape=(own, own, own, half, act, act, ac...  86.5 us
    pallas_call x1, Pallas kernels, _weight_grads(): pl.pallas_call(_weight_kernel, out_shape=(jax.ShapeDtypeStruct((ff, hid),...  39.9 us
    ppermute x3, starting transfers between devices, to(): return lax.ppermute(v, 'tp', [(i, i ^ flip) for i in range(8)])  3.52 us
    pallas_call x1, Pallas kernels, local_backward(): pl.pallas_call(_join_kernel, grid=(2,), out_shape=own, out_specs=wide, in...  2.99 us
  transfers between devices with their start and end apart: 3, of which 0 were waited for; matrix products, arithmetic and copies ran while one was open for 0% of the time, Pallas kernels for 30%

profile of v4, /device:TPU:0, one launch (start us, length us, event | category | flops | bytes accessed | tf_op | source)
XLA Modules:
  0.0 134.3 jit_solution(523084461449608330)
XLA Ops:
  0.6 86.5 %gather_partial.1 = (bf16[128,4096]{1,0:T(8,128)(2,1)}, bf16[128,4096]{1,0:T(8,128)(2,1)}, bf16[128,4096]{1,0:T(8,128)(2,1)}, bf16[128,2048]{1,0:T(8,128)(2,1)},...) custom-call(bf16[128,4096]{1,0:T(8,128)(2,1)} %x_ref.1, ...), custom_call_target="tpu_custom_call" | custom-call | tf_op jit(solution)/shard_map/gather_partial/pallas_call | solution.py:529
  87.1 1.5 %collective-permute-start.2 = (bf16[128,2048]{1,0:T(8,128)(2,1)}, bf16[128,2048]{1,0:T(8,128)(2,1)S(1)}, u32[]{:S(2)}, u32[]{:S(2)}) collective-permute-start(bf16[128,2048]{1,0:T(8,128)(2,1)} %get-tuple-element.25), channel_id=1, source_target_pairs={{0,6},{1,7},{2,4},{3,5},{4,2},{5,3},{6,0},{7,1},{8,14},{9,15},{10,... | collective-permute-start | bytes 1572872 | tf_op jit(solution)/shard_map/ppermute | solution.py:557
  88.6 1.1 collective-permute-start
  89.7 0.9 collective-permute-start.1
  90.6 39.9 %weight_grads.1 = (f32[1376,4096]{1,0:T(8,128)}, f32[1376,4096]{1,0:T(8,128)}, f32[1376,4096]{1,0:T(8,128)}) custom-call(bf16[1376,1024]{1,0:T(8,128)(2,1)} %get-tuple-element.26.zt_ref, bf16[1376,1024]{1,0:T(8,128)(2,1)} %get-tuple-element.27.dgt_ref, bf16[1376,1024]{1,0:T(8,128)(2,1)} %get-tuple-element.28.dut_ref, bf16[1024,4096]{1,0:T(8,128)(2,1)} %bitcast.12, ...), custom_call_target="tpu_custom_call" | custom-call | flops 34628173824 | bytes 67633152 | tf_op jit(solution)/shard_map/weight_grads/pallas_call | solution.py:503
  130.5 0.0 collective-permute-done.2.fd_ref
  130.5 0.0 copy-start
  130.5 0.0 collective-permute-done.fx_ref
  130.5 0.0 collective-permute-done.1.fy_ref
  130.5 0.8 copy-done
  131.3 3.0 %join.1 = bf16[128,4096]{1,0:T(8,128)(2,1)} custom-call(bf16[128,4096]{1,0:T(8,128)(2,1)} %get-tuple-element.22.so_ref, bf16[128,4096]{1,0:T(8,128)(2,1)} %collective-permute-done.fx_ref, bf16[128,4096]{1,0:T(8,128)(2,1)} %collective-permute-done.1.fy_ref, bf16[128,2048]{1,0:T(8,128)(2,1)} %copy-done), custom_call_target="tpu_custom_call" | custom-call | tf_op jit(solution)/shard_map/join/pallas_call | solution.py:564
Async XLA Ops:
  87.1 43.4 %collective-permute-start.2 = (bf16[128,2048]{1,0:T(8,128)(2,1)}, bf16[128,2048]{1,0:T(8,128)(2,1)S(1)}, u32[]{:S(2)}, u32[]{:S(2)}) collective-permute-start(bf16[128,2048]{1,0:T(8,128)(2,1)} %get-tuple-element.25), channel_id=1, source_target_pairs={{0,6},{1,7},{2,4},{3,5},{4,2},{5,3},{6,0},{7,1},{8,14},{9,15},{10,... | collective-permute-start | bytes 1572872 | tf_op jit(solution)/shard_map/ppermute | solution.py:557
  88.6 41.9 %collective-permute-start = (bf16[128,4096]{1,0:T(8,128)(2,1)}, bf16[128,4096]{1,0:T(8,128)(2,1)}, u32[]{:S(2)}, u32[]{:S(2)}) collective-permute-start(bf16[128,4096]{1,0:T(8,128)(2,1)} %get-tuple-element.23), channel_id=1, source_target_pairs={{0,2},{1,3},{2,0},{3,1},{4,6},{5,7},{6,4},{7,5},{8,10},{9,11},{10,... | collective-permute-start | bytes 3145736 | tf_op jit(solution)/shard_map/ppermute | solution.py:557
  89.7 40.8 %collective-permute-start.1 = (bf16[128,4096]{1,0:T(8,128)(2,1)}, bf16[128,4096]{1,0:T(8,128)(2,1)}, u32[]{:S(2)}, u32[]{:S(2)}) collective-permute-start(bf16[128,4096]{1,0:T(8,128)(2,1)} %get-tuple-element.24), channel_id=1, source_target_pairs={{0,4},{1,5},{2,6},{3,7},{4,0},{5,1},{6,2},{7,3},{8,12},{9,13},{10,... | collective-permute-start | bytes 3145736 | tf_op jit(solution)/shard_map/ppermute | solution.py:557
  130.5 0.8 copy-start

commit v5 on v4

v5 whole, which is shorter than its diff:
```python
import functools

import jax
import jax.numpy as jnp
from jax import lax
from jax.experimental import pallas as pl
from jax.experimental.pallas import tpu as pltpu
from jax.sharding import PartitionSpec as P

MESH = pl.DeviceIdType.MESH
BF16 = jnp.bfloat16
F32 = jnp.float32
NH = 8
DOWN = 4
NY = 16
AHEAD, LAG, TAKE = 4, 4, 6
NT = (((1,), (1,)), ((), ()))


def _lanes(n):
    return (n + 127) // 128 * 128


def _comm_kernel(x_ref, dy_ref, wd_ref, wg_ref, wu_ref, ug_ref, uu_ref,
                 so_ref, sx_ref, sy_ref, sd_ref, zt_ref, dgt_ref, dut_ref, dya_ref, xa_ref, dd_ref,
                 dyv, gv, av, spv, utv, duv, wbuf, ugv, uuv, r0v, r1v, xov, ddv,
                 ys, yr, xs, xr, rs, rr, r1r, yl, xl, wl, ul, ol, dl, po, pd):
    tok, hid = dy_ref.shape
    ff = wd_ref.shape[0]
    fp = _lanes(ff)
    nfull, rest = ff // 128, ff % 128
    hc = hid // NH
    tall = 8 * tok
    half = NH // 2

    t = lax.axis_index("tp")
    ty, tx, tc = t // 4, (t // 2) % 2, t % 2
    xn = t + 2 - 4 * tx
    yn = t + 4 - 8 * ty
    dg = xn + yn - t
    pn = t + 1 - 2 * tc

    def n1(k):
        return xn + (yn - xn) * (k % 2)

    def n2(k):
        return yn + (xn - yn) * (k % 2)

    hy = hid // NY
    per_h = NY // NH

    def cols(k, w=hc):
        return pl.ds(pl.multiple_of(k * w, w), w)

    def blk(ref, owner, k, w=hc):
        return ref.at[owner // 2, owner % 2, :, cols(k, w)]

    def rcopy(src, dst, ss, rs_, dev):
        return pltpu.make_async_remote_copy(src_ref=src, dst_ref=dst, send_sem=ss, recv_sem=rs_,
                                            device_id={"tp": dev}, device_id_type=MESH)

    def ag(buf, ss, sr, k, j, owner, dev):
        w = hid // sr.shape[0]
        return rcopy(blk(buf, owner, k, w), blk(buf, owner, k, w), ss.at[j], sr.at[k, (0, 1, 1, 2, 2, 2, 2)[j]], dev)

    def arrived(ref, sem):
        rcopy(ref, ref, sem, sem, t).wait_recv()

    def left(ref, sem):
        rcopy(ref, ref, sem, sem, t).wait_send()

    def ag_own(buf, ss, sr, k):
        ag(buf, ss, sr, k, 0, t, n1(k)).start()
        ag(buf, ss, sr, k, 1, t, n2(k)).start()
        ag(buf, ss, sr, k, 3, t, pn).start()

    def x_own(k, j, dev):
        return rcopy(xov.at[:, cols(k)], blk(xa_ref, t, k), xs.at[j], xr.at[k, (0, 1, 1, 2)[j]], dev)

    def x_send(k):
        x_own(k, 0, n1(k)).start()
        x_own(k, 1, n2(k)).start()
        x_own(k, 3, pn).start()

    def ag_mid(buf, ss, sr, k):
        ag(buf, ss, sr, k, 0, n1(k), n1(k)).wait_recv()
        ag(buf, ss, sr, k, 2, n1(k), n2(k)).start()
        ag(buf, ss, sr, k, 4, n1(k), pn).start()

    def ag_last(buf, ss, sr, k):
        w = hid // sr.shape[0]
        arrived(buf.at[pl.ds(0, 2), 0, :, cols(k, w)], sr.at[k, 1])
        ag(buf, ss, sr, k, 5, n2(k), pn).start()
        ag(buf, ss, sr, k, 6, dg, pn).start()

    def ag_end(buf, ss, sr, k):
        w = hid // sr.shape[0]
        arrived(buf.at[:, 0, :, cols(k, w)], sr.at[k, 2])

    def y_local(g):
        w = AHEAD * hy
        return pltpu.make_async_copy(dy_ref.at[:, cols(g, w)], blk(dyv, t, g, w), yl.at[g])

    x_local = pltpu.make_async_copy(x_ref, xov, xl.at[0])
    x_put = pltpu.make_async_copy(xov, xa_ref.at[t // 2, t % 2], xl.at[1])

    def down_out(k):
        return pltpu.make_async_copy(ddv.at[k % 2], dd_ref.at[:, cols(k)], pd.at[k % 2])

    def wd_load(k):
        return pltpu.make_async_copy(wd_ref.at[:, cols(k)], wbuf.at[0, pl.ds(pl.multiple_of(k % 2 * fp, fp), ff), :], wl.at[0, k % 2])

    def w_load(k, j):
        src = (wg_ref, wu_ref)[j]
        return pltpu.make_async_copy(src.at[:, cols(k)], wbuf.at[(k + 1) % 2, pl.ds(j * fp, ff), :],
                                     wl.at[(k + 1) % 2, j])

    def dy_out(k):
        return pltpu.make_async_copy(dyv.at[:, :, :, cols(k)], dya_ref.at[:, :, :, cols(k)], dl.at[0])

    ug_in = pltpu.make_async_copy(ug_ref, ugv.at[pl.ds(0, ff), :], ul.at[0])
    uu_in = pltpu.make_async_copy(uu_ref, uuv.at[pl.ds(0, ff), :], ul.at[1])
    for g in range(NY // AHEAD):
        y_local(g).start()
    wd_load(0).start()
    wd_load(1).start()
    ug_in.start()
    uu_in.start()
    x_local.start()

    barrier = pltpu.get_barrier_semaphore()
    for dev in (xn, yn, pn):
        pl.semaphore_signal(barrier, inc=1, device_id={"tp": dev}, device_id_type=MESH)
    pl.semaphore_wait(barrier, 3)

    y_local(0).wait()
    for k in range(AHEAD):
        ag_own(dyv, ys, yr, k)

    for a in range(2):
        for b in range(2):
            wbuf[a, b * fp + ff:b * fp + fp, :] = jnp.zeros((fp - ff, hc), BF16)
    gv[...] = jnp.zeros_like(gv)
    ug_in.wait()
    uu_in.wait()

    def u_block(r0, n):
        rows = pl.ds(r0, n)
        ug = ugv[rows, :].astype(F32)
        ub = uuv[rows, :]
        uu = ub.astype(F32)
        s = jax.nn.sigmoid(ug)
        a = ug * s
        sp = s * (1.0 + ug * (1.0 - s))
        ugv[rows, :] = (a * uu).astype(BF16)
        if n < 128:
            pad = jnp.zeros((128 - n, tall), F32)
            a = jnp.concatenate([a, pad], axis=0)
            sp = jnp.concatenate([sp, pad], axis=0)
            uu = jnp.concatenate([uu, pad], axis=0)
        lanes = pl.ds(r0, 128)
        av[:, lanes] = a.T
        spv[:, lanes] = sp.T
        utv[:, lanes] = uu.T.astype(BF16)

    down0 = -(-(fp // 128) // per_h) * per_h

    def phase1(i, carry):
        @pl.when((i < NY - AHEAD) & (i % AHEAD == 0))
        def _():
            y_local(i // AHEAD + 1).wait()

        @pl.when(i < NY - AHEAD)
        def _():
            ag_own(dyv, ys, yr, i + AHEAD)

        @pl.when(i < NY)
        def _():
            ag_mid(dyv, ys, yr, i)

        @pl.when(i >= NY + TAKE - NH)
        def _():
            x_send(i - (NY + TAKE - NH))

        @pl.when(i < nfull)
        def _():
            u_block(pl.multiple_of(i * 128, 128), 128)

        if rest:
            @pl.when(i == nfull)
            def _():
                u_block(nfull * 128, rest)

        @pl.when((i >= LAG) & (i < NY + LAG))
        def _():
            ag_last(dyv, ys, yr, i - LAG)

        @pl.when(i >= TAKE)
        def _():
            ag_end(dyv, ys, yr, i - TAKE)

        @pl.when((i >= TAKE) & ((i - TAKE) % per_h == per_h - 1))
        def _():
            k = (i - TAKE) // per_h
            dy_out(k).start()
            wd_load(k).wait()
            dyc = dyv[:, :, :, cols(k)].reshape(tall, hc)
            for n in range(0, fp, 256):
                w = min(256, fp - n)
                gv[:, n:n + w] += lax.dot_general(dyc, wbuf[0, pl.ds(pl.multiple_of(k % 2 * fp + n, 128), w), :], NT, preferred_element_type=F32)

            @pl.when(k + 2 < NH)
            def _():
                wd_load(k + 2).start()

        @pl.when((i >= down0) & ((i - down0) % per_h == 0) & (i < down0 + DOWN * per_h))
        def _():
            k = (i - down0) // per_h

            @pl.when(k >= 2)
            def _():
                down_out(k - 2).wait()

            dyc = dyv[:, :, :, cols(k)].reshape(tall, hc)
            ddv[k % 2] = jnp.dot(ugv[:ff, :], dyc, preferred_element_type=F32)
            down_out(k).start()

        return carry

    w_load(0, 0).start()
    w_load(0, 1).start()
    x_local.wait()
    x_put.start()
    lax.fori_loop(0, NY + TAKE, phase1, 0)
    w_load(1, 0).start()
    w_load(1, 1).start()
    zt_out = pltpu.make_async_copy(ugv.at[pl.ds(0, ff), :], zt_ref, ol.at[0])
    zt_out.start()
    def gates(i, carry):
        rows = pl.ds(pl.multiple_of(i * 128, 128), 128)
        g = gv[rows, :]
        duv[rows, :fp] = (g * utv[rows, :].astype(F32) * spv[rows, :]).astype(BF16)
        duv[rows, fp:] = (g * av[rows, :]).astype(BF16)
        return carry

    lax.fori_loop(0, tall // 128, gates, 0)

    for n in range(7):
        left(dyv.at[0, 0], ys.at[n])
    pltpu.make_async_copy(dyv, dya_ref, dl.at[0]).wait()
    zt_out.wait()
    for k in range(DOWN - 2, DOWN):
        down_out(k).wait()

    def rs0(k, c):
        return rcopy(dyv.at[:, c, :, cols(k)], r0v.at[k], rs.at[0], rr.at[k], pn)

    def rs1(k):
        return rcopy(blk(dyv, dg, k), r1v.at[k], rs.at[1], r1r.at[k], n1(k))

    def sums_out(k, diagonal):
        outs = [(so_ref, t, k), (sx_ref, xn, k), (sy_ref, yn, k)] + ([(sd_ref, dg, k - half)] if diagonal else [])
        return [pltpu.make_async_copy(blk(dyv, owner, k), ref.at[:, cols(c)], po.at[i])
                for i, (ref, owner, c) in enumerate(outs)]

    def add(owner, k, other):
        b = blk(dyv, owner, k)
        b[...] = (b[...].astype(F32) + other.astype(F32)).astype(BF16)

    def t_block(r0):
        rows = pl.ds(r0, 128)
        ugv[rows, :] = duv[:, rows].T
        uuv[rows, :] = duv[:, pl.ds(fp + r0, 128)].T

    blocks = fp // 128
    per = -(-blocks // NH)

    def phase2(i, carry):
        for first, ks in ((NH - 2, range(0, 3)), (NH - 1, range(3, 6)), (NH, range(6, NH))):
            @pl.when(i == first)
            def _():
                for k in ks:
                    ag_last(xa_ref, xs, xr, k)

        @pl.when(i < NH)
        def _():
            ag_mid(xa_ref, xs, xr, i)
            w_load(i, 0).wait()
            w_load(i, 1).wait()
            slot = (i + 1) % 2
            for b in range(per):
                t_block(pl.multiple_of(jnp.minimum(per * i + b, blocks - 1) * 128, 128))
            p = jnp.dot(duv[...], wbuf[slot], preferred_element_type=F32)
            dyv[:, :, :, cols(i)] = p.astype(BF16).reshape(4, 2, tok, hc)

            @pl.when(i + 2 < NH)
            def _():
                w_load(i + 2, 0).start()
                w_load(i + 2, 1).start()

        @pl.when(i < NH)
        def _():
            rs0(i, 1 - tc).start()

        @pl.when((i >= 1) & (i <= NH))
        def _():
            k = i - 1
            rs0(k, tc).wait_recv()
            for q in range(4):
                add(2 * q + tc, k, r0v[k, q])

            @pl.when(k < half)
            def _():
                rs1(k).start()

            @pl.when(k >= half)
            def _():
                for o in sums_out(k, True):
                    o.start()

        @pl.when((i >= half) & (i < NH))
        def _():
            k = i - half
            rs1(k).wait_recv()
            add(n2(k), k, r1v[k])
            for o in sums_out(k, False):
                o.start()

        return carry

    lax.fori_loop(0, NH + 1, phase2, 0)
    outs = [pltpu.make_async_copy(v.at[pl.ds(0, ff), :], ref, ol.at[i])
            for i, (v, ref) in enumerate(((ugv, dgt_ref), (uuv, dut_ref)))]
    for o in outs:
        o.start()

    def drain(k, carry):
        ag_end(xa_ref, xs, xr, k)
        return carry

    lax.fori_loop(0, NH, drain, 0)
    for n in range(7):
        left(xa_ref.at[0, 0], xs.at[n])
    left(dyv.at[:, 0], rs.at[0])
    left(dyv.at[0, 0, :, pl.ds(0, hid // 2)], rs.at[1])
    x_put.wait()
    for n, ref in enumerate((so_ref, sx_ref, sy_ref, sd_ref)):
        pltpu.make_async_copy(ref, ref, po.at[n]).wait()
    for o in outs:
        o.wait()


def _row_chunks(ff):
    n = ff // 16
    size = -(-n // 4)
    return [16 * min(size, n - i) for i in range(0, n, size)]


def _weight_kernel(zt_ref, dgt_ref, dut_ref, dy_ref, x_ref, part_ref, dd_ref, dg_ref, du_ref,
                   zv, dgv, duv, yv, xv, o0, o1, o2, cv, ls, ysem, xsem, os, ci, co):
    ff, tall = zt_ref.shape
    hid = dy_ref.shape[1]
    nb = yv.shape[-1]
    n = hid // nb
    sizes = _row_chunks(ff)
    depth = tall // 256

    def load(src, dst, sem, j, p):
        lo = pl.ds(j * nb + p * 512, 512)
        return pltpu.make_async_copy(src.at[:, lo], dst.at[j % 2, :, p * 512:p * 512 + 512], sem.at[j % 2, p])

    def put(i, j, rows, width, p):
        stage, out = ((o0, dd_ref), (o1, dg_ref), (o2, du_ref))[i]
        lo = pl.ds(j * nb + p * 512, width)
        slot = j % stage.shape[0]
        return pltpu.make_async_copy(stage.at[slot, rows, p * 512:p * 512 + width], out.at[rows, lo], os.at[i, slot])

    def put_all(i, j):
        return put(i, j, pl.ds(0, ff), nb, 0)

    def product(i, j, accs, waits):
        a = (zv, dgv, duv)[i]
        b = (yv, xv, xv)[i].at[j % 2]
        stage = (o0, o1, o2)[i]
        slot = j % stage.shape[0]
        steps = []
        for pair in range(nb // 512):
            row = 0
            for c, size in enumerate(sizes):
                for kt in range(depth):
                    steps.append((pair, c, row, size, kt))
                row += size

        def push(s):
            pair, _, _, _, kt = steps[s]
            for q in range(2):
                lo = pair * 512 + q * 256
                pltpu.matmul_push_rhs(b[kt * 256:kt * 256 + 256, lo:lo + 256], s % 2, q)

        def pop(pair, c, row, size):
            for q in range(2):
                lo = pair * 512 + q * 256
                stage[slot, row:row + size, lo:lo + 256] = pltpu.matmul_pop(accs[q][c])
            put(i, j, pl.ds(row, size), 512, pair).start()

        late = None
        for s, (pair, c, row, size, kt) in enumerate(steps):
            if s == 0 or (c == 0 and kt == 0 and waits):
                for w in waits[pair] if waits else ():
                    w.wait()
                push(s)
            if s + 1 < len(steps) and not (waits and steps[s + 1][1] == 0 and steps[s + 1][4] == 0):
                push(s + 1)
            block = a[row:row + size, kt * 256:kt * 256 + 256]
            for q in range(2):
                pltpu.matmul_acc_lhs(accs[q][c], block, load_staged_rhs=s % 2)
            if kt == 0 and late is not None:
                pop(*late)
            if kt == depth - 1:
                late = (pair, c, row, size)
        pop(*late)

    done = part_ref.shape[1]
    wide = cv.shape[2]
    pieces = done // wide

    def take(p):
        return pltpu.make_async_copy(part_ref.at[:, p * wide:p * wide + wide], cv.at[p % 2], ci.at[p % 2])

    def give(p):
        return pltpu.make_async_copy(cv.at[p % 2], dd_ref.at[:, p * wide:p * wide + wide], co.at[p % 2])

    def pass_on(p):
        if 1 <= p <= pieces:
            take(p - 1).wait()
            give(p - 1).start()
        if p < pieces:
            if p >= 2:
                give(p - 2).wait()
            take(p).start()

    zl, gl, ul = (pltpu.make_async_copy(src, dst, ls.at[i])
                  for i, (src, dst) in enumerate(((zt_ref, zv), (dgt_ref, dgv), (dut_ref, duv))))
    y_block = {j: [load(dy_ref, yv, ysem, j, h) for h in range(nb // 512)] for j in range(done // nb, n)}
    x_block = {j: [load(x_ref, xv, xsem, j, h) for h in range(nb // 512)] for j in range(2)}
    sent = {0: [], 1: [], 2: []}
    zl.start()
    for c in y_block[done // nb]:
        c.start()
    gl.start()
    for c in x_block[0]:
        c.start()
    ul.start()
    for j in range(done // nb + 1, n):
        for c in y_block[j]:
            c.start()
    for c in x_block[1]:
        c.start()

    def body(*flat):
        h = len(flat) // 2
        accs = [[part[2] if i == len(sizes) - 1 else part[i % 2] for i in range(len(sizes))]
                for part in (flat[:h], flat[h:])]
        todo = [(i, j) for j in range(n) for i in range(3) if i or j >= done // nb]
        down = [e for e in todo if not e[0]]
        order = []
        for j in range(n):
            order += down[j:j + 1] + [(1, j), (2, j)]
        for p, (i, j) in enumerate(order):
            if i == 1 and j and j + 1 < n:
                x_block[j + 1] = [load(x_ref, xv, xsem, j + 1, h) for h in range(nb // 512)]
            waits = []
            if p == 0:
                waits = [[zl, y_block[j][0]], [y_block[j][1]]]
            elif i == 0:
                waits = [y_block[j], []]
            elif (i, j) == (1, 0):
                waits = [[gl, x_block[0][0]], [x_block[0][1]]]
            elif (i, j) == (2, 0):
                waits = [[ul], []]
            elif i == 1:
                waits = [x_block[j], []]
            if i == 1 and j and j + 1 < n:
                for c in x_block[j + 1]:
                    c.start()
            before = sent[i]
            if len(before) >= (o0, o1, o2)[i].shape[0]:
                put_all(i, before[-(o0, o1, o2)[i].shape[0]]).wait()
            pass_on(p)
            product(i, j, accs, waits)
            before.append(j)

    pl.run_scoped(body, *[pltpu.ACC(q)((size, 256), F32) for q in range(2) for size in (sizes[0], sizes[0], sizes[-1])])
    for i, stage in enumerate((o0, o1, o2)):
        for j in sent[i][-stage.shape[0]:]:
            put_all(i, j).wait()
    for p in range(max(pieces - 2, 0), pieces):
        give(p).wait()


def _weight_grads(zt, dgt, dut, dy, x, part):
    ff, tall = zt.shape
    hid = x.shape[1]
    nb = 1024
    sem = pltpu.SemaphoreType.DMA
    any_ = pl.BlockSpec(memory_space=pl.ANY)
    return pl.pallas_call(
        _weight_kernel,
        out_shape=(jax.ShapeDtypeStruct((ff, hid), F32),) * 3,
        in_specs=[any_] * 6,
        out_specs=(any_,) * 3,
        scratch_shapes=[pltpu.VMEM((ff, tall), BF16)] * 3 + [pltpu.VMEM((2, tall, nb), BF16)] * 2
        + [pltpu.VMEM((k, ff, nb), F32) for k in (1, 2, 2)] + [pltpu.VMEM((2, ff, 256), F32)]
        + [sem((3,)), sem((2, 2)), sem((2, 2)), sem((3, 2)), sem((2,)), sem((2,))],
        compiler_params=pltpu.CompilerParams(vmem_limit_bytes=63 * 2 ** 20),
        cost_estimate=pl.CostEstimate(flops=6 * ff * tall * hid, bytes_accessed=12 * ff * hid, transcendentals=0),
        name="weight_grads",
    )(zt, dgt, dut, dy, x, part)


def solution(mesh):
    def local_backward(x, wg, wu, wd, ug, uu, dy):
        tok, hid = dy.shape
        ff = wd.shape[0]
        fp = _lanes(ff)
        tall = 8 * tok
        hc = hid // NH
        any_ = pl.BlockSpec(memory_space=pl.ANY)
        sem = pltpu.SemaphoreType.DMA
        full = jax.ShapeDtypeStruct((4, 2, tok, hid), BF16)
        act = jax.ShapeDtypeStruct((ff, tall), BF16)
        own = jax.ShapeDtypeStruct((tok, hid), BF16)
        half = jax.ShapeDtypeStruct((tok, hid // 2), BF16)
        so, sx, sy, sd, zt, dgt, dut, dya, xa, ddp = pl.pallas_call(
            _comm_kernel,
            out_shape=(own, own, own, half, act, act, act, full, full,
                       jax.ShapeDtypeStruct((ff, DOWN * hc), F32)),
            in_specs=[any_] * 7,
            out_specs=(any_,) * 10,
            scratch_shapes=[
                pltpu.VMEM((4, 2, tok, hid), BF16),
                pltpu.VMEM((tall, fp), F32),
                pltpu.VMEM((tall, fp), F32),
                pltpu.VMEM((tall, fp), F32),
                pltpu.VMEM((tall, fp), BF16),
                pltpu.VMEM((tall, 2 * fp), BF16),
                pltpu.VMEM((2, 2 * fp, hc), BF16),
                pltpu.VMEM((fp, tall), BF16),
                pltpu.VMEM((fp, tall), BF16),
                pltpu.VMEM((NH, 4, tok, hc), BF16),
                pltpu.VMEM((NH // 2, tok, hc), BF16),
                pltpu.VMEM((tok, hid), BF16),
                pltpu.VMEM((2, ff, hc), F32),
                sem((7,)), sem((NY, 3)), sem((7,)), sem((NH, 3)), sem((2,)), sem((NH,)), sem((NH // 2,)),
                sem((NY // AHEAD,)), sem((2,)), sem((2, 2)), sem((2,)), sem((2,)), sem((1,)), sem((4,)), sem((2,)),
            ],
            compiler_params=pltpu.CompilerParams(collective_id=0, has_side_effects=True, vmem_limit_bytes=67043328),
            name="gather_partial",
        )(x, dy, wd, wg.T, wu.T, ug.T, uu.T)
        dya = dya.reshape(tall, hid)
        xa = xa.reshape(tall, hid)

        def to(v, flip):
            return lax.ppermute(v, 'tp', [(i, i ^ flip) for i in range(8)])

        fx, fy, fd = to(sx, 2), to(sy, 4), to(sd, 6)
        dwd, dwg, dwu = _weight_grads(zt, dgt, dut, dya, xa, ddp)
        fx, fy, fd, dwd, dwg, dwu = lax.optimization_barrier((fx, fy, fd, dwd, dwg, dwu))
        right = jnp.pad(fd, ((0, 0), (hid // 2, 0)))
        dx = sum(v.astype(F32) for v in (so, fx, fy, right)).astype(BF16)
        return dx, dwg.T, dwu.T, dwd

    tok_spec = P(('dp', 'tp'), None)
    col_spec = P(None, 'tp')
    act_spec = P('dp', 'tp')
    return jax.shard_map(local_backward, mesh=mesh,
                         in_specs=(tok_spec, col_spec, col_spec, P('tp', None), act_spec, act_spec, tok_spec),
                         out_specs=(tok_spec, act_spec, act_spec, tok_spec),
                         check_vma=False)
```

time: 134 us -> 131 us (0.978)
  Pallas kernels: 129 us -> 123 us
  other arithmetic: 0 us -> 3.4 us
    convert_element_type x0 -> x1, other arithmetic: none -> 3.4 us  [local_backward(): dx = sum((v.astype(F32) for v in (so, fx, fy, right))).astype(BF16)]
    pallas_call x1 -> x0, Pallas kernels: 2.99 us -> none  [local_backward(): pl.pallas_call(_join_kernel, grid=(2,), out_shape=own, out_specs=wide, in...]
    pallas_call x1, Pallas kernels: 86.5 us -> 83.7 us  [local_backward(): pl.pallas_call(_comm_kernel, out_shape=(own, own, own, half, act, act, ac...]
where the time goes in v5:
time: 131 us
  Pallas kernels  123 us (94%)
  starting transfers between devices  3.52 us (3%)
  other arithmetic  3.4 us (3%)
    pallas_call x1, Pallas kernels, local_backward(): pl.pallas_call(_comm_kernel, out_shape=(own, own, own, half, act, act, ac...  83.7 us
    pallas_call x1, Pallas kernels, _weight_grads(): pl.pallas_call(_weight_kernel, out_shape=(jax.ShapeDtypeStruct((ff, hid),...  39.5 us
    ppermute x3, starting transfers between devices, to(): return lax.ppermute(v, 'tp', [(i, i ^ flip) for i in range(8)])  3.52 us
    convert_element_type x1, other arithmetic, local_backward(): dx = sum((v.astype(F32) for v in (so, fx, fy, right))).astype(BF16)  3.4 us
  transfers between devices with their start and end apart: 3, of which 0 were waited for; matrix products, arithmetic and copies ran while one was open for 0% of the time, Pallas kernels for 30%

profile of v5, /device:TPU:0, one launch (start us, length us, event | category | flops | bytes accessed | tf_op | source)
XLA Modules:
  0.0 130.8 jit_solution(17655120442473162303)
XLA Ops:
  0.6 83.7 %gather_partial.1 = (bf16[128,4096]{1,0:T(8,128)(2,1)}, bf16[128,4096]{1,0:T(8,128)(2,1)}, bf16[128,4096]{1,0:T(8,128)(2,1)}, bf16[128,2048]{1,0:T(8,128)(2,1)},...) custom-call(bf16[128,4096]{1,0:T(8,128)(2,1)} %x_ref.1, ...), custom_call_target="tpu_custom_call" | custom-call | tf_op jit(solution)/shard_map/gather_partial/pallas_call | solution.py:534
  84.3 2.1 %collective-permute-start.2 = (bf16[128,2048]{1,0:T(8,128)(2,1)}, bf16[128,2048]{1,0:T(8,128)(2,1)S(1)}, u32[]{:S(2)}, u32[]{:S(2)}) collective-permute-start(bf16[128,2048]{1,0:T(8,128)(2,1)} %get-tuple-element.26), channel_id=1, source_target_pairs={{0,6},{1,7},{2,4},{3,5},{4,2},{5,3},{6,0},{7,1},{8,14},{9,15},{10,... | collective-permute-start | bytes 1572872 | tf_op jit(solution)/shard_map/ppermute | solution.py:564
  86.5 0.9 collective-permute-start
  87.4 0.5 collective-permute-start.1
  87.9 39.5 %weight_grads.1 = (f32[1376,4096]{1,0:T(8,128)}, f32[1376,4096]{1,0:T(8,128)}, f32[1376,4096]{1,0:T(8,128)}) custom-call(bf16[1376,1024]{1,0:T(8,128)(2,1)} %get-tuple-element.27.zt_ref, bf16[1376,1024]{1,0:T(8,128)(2,1)} %get-tuple-element.28.dgt_ref, bf16[1376,1024]{1,0:T(8,128)(2,1)} %get-tuple-element.29.dut_ref, bf16[1024,4096]{1,0:T(8,128)(2,1)} %bitcast.12, ...), custom_call_target="tpu_custom_call" | custom-call | flops 34628173824 | bytes 67633152 | tf_op jit(solution)/shard_map/weight_grads/pallas_call | solution.py:507
  127.4 0.0 collective-permute-done.2
  127.4 0.0 collective-permute-done
  127.4 0.0 collective-permute-done.1
  127.4 3.4 %add_convert_fusion = bf16[128,4096]{1,0:T(8,128)(2,1)} fusion(bf16[128,4096]{1,0:T(8,128)(2,1)} %collective-permute-done.1, bf16[128,4096]{1,0:T(8,128)(2,1)} %collective-permute-done, bf16[128,4096]{1,0:T(8,128)(2,1)} %get-tuple-element.23, bf16[128,2048]{1,0:T(8,128)(2,1)S(1)} %collective-permute-done.2), kind=kLoop, calls=%fused_computation | loop fusion | flops 4194304 | bytes 4718592 | tf_op jit(solution)/shard_map/convert_element_type | solution.py:570
Async XLA Ops:
  84.3 43.1 %collective-permute-start.2 = (bf16[128,2048]{1,0:T(8,128)(2,1)}, bf16[128,2048]{1,0:T(8,128)(2,1)S(1)}, u32[]{:S(2)}, u32[]{:S(2)}) collective-permute-start(bf16[128,2048]{1,0:T(8,128)(2,1)} %get-tuple-element.26), channel_id=1, source_target_pairs={{0,6},{1,7},{2,4},{3,5},{4,2},{5,3},{6,0},{7,1},{8,14},{9,15},{10,... | collective-permute-start | bytes 1572872 | tf_op jit(solution)/shard_map/ppermute | solution.py:564
  86.5 40.9 %collective-permute-start = (bf16[128,4096]{1,0:T(8,128)(2,1)}, bf16[128,4096]{1,0:T(8,128)(2,1)}, u32[]{:S(2)}, u32[]{:S(2)}) collective-permute-start(bf16[128,4096]{1,0:T(8,128)(2,1)} %get-tuple-element.24), channel_id=1, source_target_pairs={{0,2},{1,3},{2,0},{3,1},{4,6},{5,7},{6,4},{7,5},{8,10},{9,11},{10,... | collective-permute-start | bytes 3145736 | tf_op jit(solution)/shard_map/ppermute | solution.py:564
  87.4 40.1 %collective-permute-start.1 = (bf16[128,4096]{1,0:T(8,128)(2,1)}, bf16[128,4096]{1,0:T(8,128)(2,1)}, u32[]{:S(2)}, u32[]{:S(2)}) collective-permute-start(bf16[128,4096]{1,0:T(8,128)(2,1)} %get-tuple-element.25), channel_id=1, source_target_pairs={{0,4},{1,5},{2,6},{3,7},{4,0},{5,1},{6,2},{7,3},{8,12},{9,13},{10,... | collective-permute-start | bytes 3145736 | tf_op jit(solution)/shard_map/ppermute | solution.py:564

commit v6 on v5

--- a/solution.py
+++ b/solution.py
@@ -11,7 +11,7 @@
 BF16 = jnp.bfloat16
 F32 = jnp.float32
 NH = 8
-DOWN = 4
+DOWN = 2
 NY = 16
 AHEAD, LAG, TAKE = 4, 4, 6
 NT = (((1,), (1,)), ((), ()))
@@ -276,7 +276,7 @@
     per = -(-blocks // NH)
 
     def phase2(i, carry):
-        for first, ks in ((NH - 2, range(0, 3)), (NH - 1, range(3, 6)), (NH, range(6, NH))):
+        for first, ks in ((NH - 3, range(0, 2)), (NH - 2, range(2, 4)), (NH - 1, range(4, 6)), (NH, range(6, NH))):
             @pl.when(i == first)
             def _():
                 for k in ks:
@@ -366,12 +366,18 @@
     depth = tall // 256
 
     def load(src, dst, sem, j, p):
-        lo = pl.ds(j * nb + p * 512, 512)
+        lo = pl.ds(pl.multiple_of(j * nb + p * 512, 512), 512)
         return pltpu.make_async_copy(src.at[:, lo], dst.at[j % 2, :, p * 512:p * 512 + 512], sem.at[j % 2, p])
+
+    def y_loads(j):
+        return [load(dy_ref, yv, ysem, j, p) for p in range(nb // 512)]
+
+    def x_loads(j):
+        return [load(x_ref, xv, xsem, j, p) for p in range(nb // 512)]
 
     def put(i, j, rows, width, p):
         stage, out = ((o0, dd_ref), (o1, dg_ref), (o2, du_ref))[i]
-        lo = pl.ds(j * nb + p * 512, width)
+        lo = pl.ds(pl.multiple_of(j * nb + p * 512, 512), width)
         slot = j % stage.shape[0]
         return pltpu.make_async_copy(stage.at[slot, rows, p * 512:p * 512 + width], out.at[rows, lo], os.at[i, slot])
 
@@ -420,81 +426,64 @@
                 late = (pair, c, row, size)
         pop(*late)
 
-    done = part_ref.shape[1]
-    wide = cv.shape[2]
-    pieces = done // wide
-
     def take(p):
-        return pltpu.make_async_copy(part_ref.at[:, p * wide:p * wide + wide], cv.at[p % 2], ci.at[p % 2])
+        return pltpu.make_async_copy(part_ref.at[:, p * 512:p * 512 + 512], cv.at[p], ci.at[p])
 
     def give(p):
-        return pltpu.make_async_copy(cv.at[p % 2], dd_ref.at[:, p * wide:p * wide + wide], co.at[p % 2])
-
-    def pass_on(p):
-        if 1 <= p <= pieces:
-            take(p - 1).wait()
-            give(p - 1).start()
-        if p < pieces:
-            if p >= 2:
-                give(p - 2).wait()
-            take(p).start()
+        return pltpu.make_async_copy(cv.at[p], dd_ref.at[:, p * 512:p * 512 + 512], co.at[p])
 
     zl, gl, ul = (pltpu.make_async_copy(src, dst, ls.at[i])
                   for i, (src, dst) in enumerate(((zt_ref, zv), (dgt_ref, dgv), (dut_ref, duv))))
-    y_block = {j: [load(dy_ref, yv, ysem, j, h) for h in range(nb // 512)] for j in range(done // nb, n)}
-    x_block = {j: [load(x_ref, xv, xsem, j, h) for h in range(nb // 512)] for j in range(2)}
-    sent = {0: [], 1: [], 2: []}
-    zl.start()
-    for c in y_block[done // nb]:
-        c.start()
+    parts = range(nb // 512)
+    first = x_loads(0)
     gl.start()
-    for c in x_block[0]:
+    for c in first:
         c.start()
     ul.start()
-    for j in range(done // nb + 1, n):
-        for c in y_block[j]:
-            c.start()
-    for c in x_block[1]:
+    zl.start()
+    for c in y_loads(1) + x_loads(1):
         c.start()
+    for p in parts:
+        take(p).start()
 
     def body(*flat):
         h = len(flat) // 2
         accs = [[part[2] if i == len(sizes) - 1 else part[i % 2] for i in range(len(sizes))]
                 for part in (flat[:h], flat[h:])]
-        todo = [(i, j) for j in range(n) for i in range(3) if i or j >= done // nb]
-        down = [e for e in todo if not e[0]]
-        order = []
-        for j in range(n):
-            order += down[j:j + 1] + [(1, j), (2, j)]
-        for p, (i, j) in enumerate(order):
-            if i == 1 and j and j + 1 < n:
-                x_block[j + 1] = [load(x_ref, xv, xsem, j + 1, h) for h in range(nb // 512)]
-            waits = []
-            if p == 0:
-                waits = [[zl, y_block[j][0]], [y_block[j][1]]]
-            elif i == 0:
-                waits = [y_block[j], []]
-            elif (i, j) == (1, 0):
-                waits = [[gl, x_block[0][0]], [x_block[0][1]]]
-            elif (i, j) == (2, 0):
-                waits = [[ul], []]
-            elif i == 1:
-                waits = [x_block[j], []]
-            if i == 1 and j and j + 1 < n:
-                for c in x_block[j + 1]:
+        product(1, 0, accs, [[gl, first[0]], first[1:]])
+        product(2, 0, accs, [[ul], []])
+        zl.wait()
+        for p in parts:
+            take(p).wait()
+            give(p).start()
+
+        def rest(j, carry):
+            for c in y_loads(j) + x_loads(j):
+                c.wait()
+
+            @pl.when(j + 1 < n)
+            def _():
+                for c in y_loads(j + 1) + x_loads(j + 1):
                     c.start()
-            before = sent[i]
-            if len(before) >= (o0, o1, o2)[i].shape[0]:
-                put_all(i, before[-(o0, o1, o2)[i].shape[0]]).wait()
-            pass_on(p)
-            product(i, j, accs, waits)
-            before.append(j)
+
+            @pl.when(j >= 2)
+            def _():
+                put_all(0, j - 1).wait()
+                put_all(2, j - 2).wait()
+
+            put_all(1, j - 1).wait()
+            for i in range(3):
+                product(i, j, accs, None)
+            return carry
+
+        lax.fori_loop(1, n, rest, 0)
 
     pl.run_scoped(body, *[pltpu.ACC(q)((size, 256), F32) for q in range(2) for size in (sizes[0], sizes[0], sizes[-1])])
-    for i, stage in enumerate((o0, o1, o2)):
-        for j in sent[i][-stage.shape[0]:]:
-            put_all(i, j).wait()
-    for p in range(max(pieces - 2, 0), pieces):
+    put_all(0, n - 1).wait()
+    put_all(1, n - 1).wait()
+    put_all(2, n - 2).wait()
+    put_all(2, n - 1).wait()
+    for p in parts:
         give(p).wait()
 
 
@@ -503,16 +492,16 @@
     hid = x.shape[1]
     nb = 1024
     sem = pltpu.SemaphoreType.DMA
-    any_ = pl.BlockSpec(memory_space=pl.ANY)
+    any_ = pl.BlockSpec(memory_space=pltpu.HBM)
     return pl.pallas_call(
         _weight_kernel,
         out_shape=(jax.ShapeDtypeStruct((ff, hid), F32),) * 3,
         in_specs=[any_] * 6,
         out_specs=(any_,) * 3,
         scratch_shapes=[pltpu.VMEM((ff, tall), BF16)] * 3 + [pltpu.VMEM((2, tall, nb), BF16)] * 2
-        + [pltpu.VMEM((k, ff, nb), F32) for k in (1, 2, 2)] + [pltpu.VMEM((2, ff, 256), F32)]
+        + [pltpu.VMEM((k, ff, nb), F32) for k in (1, 1, 2)] + [pltpu.VMEM((nb // 512, ff, 512), F32)]
         + [sem((3,)), sem((2, 2)), sem((2, 2)), sem((3, 2)), sem((2,)), sem((2,))],
-        compiler_params=pltpu.CompilerParams(vmem_limit_bytes=63 * 2 ** 20),
+        compiler_params=pltpu.CompilerParams(vmem_limit_bytes=54 * 2 ** 20),
         cost_estimate=pl.CostEstimate(flops=6 * ff * tall * hid, bytes_accessed=12 * ff * hid, transcendentals=0),
         name="weight_grads",
     )(zt, dgt, dut, dy, x, part)
@@ -564,6 +553,7 @@
             return lax.ppermute(v, 'tp', [(i, i ^ flip) for i in range(8)])
 
         fx, fy, fd = to(sx, 2), to(sy, 4), to(sd, 6)
+        zt, dgt, dut, ddp = (pltpu.with_memory_space_constraint(v, pltpu.HBM) for v in (zt, dgt, dut, ddp))
         dwd, dwg, dwu = _weight_grads(zt, dgt, dut, dya, xa, ddp)
         fx, fy, fd, dwd, dwg, dwu = lax.optimization_barrier((fx, fy, fd, dwd, dwg, dwu))
         right = jnp.pad(fd, ((0, 0), (hid // 2, 0)))

time: 131 us -> 129 us (0.985)
  other arithmetic: 3.4 us -> 1.54 us
    convert_element_type x1, other arithmetic: 3.4 us -> 1.54 us  [local_backward(): dx = sum((v.astype(F32) for v in (so, fx, fy, right))).astype(BF16)]
  transfers between devices with their start and end apart: 3 -> 3, of which waited for: 0 -> 0; matrix products, arithmetic and copies ran while one was open for 0% -> 0% of each run, Pallas kernels for 30% -> 31%
where the time goes in v6:
time: 129 us
  Pallas kernels  123 us (95%)
  starting transfers between devices  3.52 us (3%)
  other arithmetic  1.54 us (1%)
    pallas_call x1, Pallas kernels, local_backward(): pl.pallas_call(_comm_kernel, out_shape=(own, own, own, half, act, act, ac...  83.8 us
    pallas_call x1, Pallas kernels, _weight_grads(): pl.pallas_call(_weight_kernel, out_shape=(jax.ShapeDtypeStruct((ff, hid),...  39.7 us
    ppermute x3, starting transfers between devices, to(): return lax.ppermute(v, 'tp', [(i, i ^ flip) for i in range(8)])  3.52 us
  transfers between devices with their start and end apart: 3, of which 0 were waited for; matrix products, arithmetic and copies ran while one was open for 0% of the time, Pallas kernels for 31%

profile of v6, /device:TPU:0, one launch (start us, length us, event | category | flops | bytes accessed | tf_op | source)
XLA Modules:
  0.0 129.2 jit_solution(10918927371522626016)
XLA Ops:
  0.6 83.8 %gather_partial.1 = (bf16[128,4096]{1,0:T(8,128)(2,1)}, bf16[128,4096]{1,0:T(8,128)(2,1)}, bf16[128,4096]{1,0:T(8,128)(2,1)}, bf16[128,2048]{1,0:T(8,128)(2,1)},...) custom-call(bf16[128,4096]{1,0:T(8,128)(2,1)} %x_ref.1, ...), custom_call_target="tpu_custom_call" | custom-call | tf_op jit(solution)/shard_map/gather_partial/pallas_call | solution.py:523
  84.4 2.1 %collective-permute-start.2 = (bf16[128,2048]{1,0:T(8,128)(2,1)}, bf16[128,2048]{1,0:T(8,128)(2,1)S(1)}, u32[]{:S(2)}, u32[]{:S(2)}) collective-permute-start(bf16[128,2048]{1,0:T(8,128)(2,1)} %get-tuple-element.26), channel_id=1, source_target_pairs={{0,6},{1,7},{2,4},{3,5},{4,2},{5,3},{6,0},{7,1},{8,14},{9,15},{10,... | collective-permute-start | bytes 1572872 | tf_op jit(solution)/shard_map/ppermute | solution.py:553
  86.6 0.9 collective-permute-start
  87.5 0.5 collective-permute-start.1
  88.0 0.0 copy-start
  88.0 39.7 %weight_grads.1 = (f32[1376,4096]{1,0:T(8,128)}, f32[1376,4096]{1,0:T(8,128)}, f32[1376,4096]{1,0:T(8,128)}) custom-call(bf16[1376,1024]{1,0:T(8,128)(2,1)} %get-tuple-element.27.zt_ref, bf16[1376,1024]{1,0:T(8,128)(2,1)} %get-tuple-element.28.dgt_ref, bf16[1376,1024]{1,0:T(8,128)(2,1)} %get-tuple-element.29.dut_ref, bf16[1024,4096]{1,0:T(8,128)(2,1)} %bitcast.12, ...), custom_call_target="tpu_custom_call" | custom-call | flops 34628173824 | bytes 67633152 | tf_op jit(solution)/shard_map/weight_grads/pallas_call | solution.py:496
  127.6 0.0 collective-permute-done.2
  127.6 0.0 collective-permute-done
  127.6 0.0 collective-permute-done.1
  127.7 0.0 copy-done
  127.7 1.5 %add_convert_fusion = bf16[128,4096]{1,0:T(8,128)(2,1)} fusion(bf16[128,4096]{1,0:T(8,128)(2,1)S(1)} %collective-permute-done.1, bf16[128,4096]{1,0:T(8,128)(2,1)S(1)} %collective-permute-done, bf16[128,4096]{1,0:T(8,128)(2,1)S(1)} %copy-done, bf16[128,2048]{1,0:T(8,128)(2,1)S(1)} %collective-permute-done.2), kind=kLoop, calls=%fused_computation | loop fusion | flops 4194304 | bytes 4718592 | tf_op jit(solution)/shard_map/convert_element_type | solution.py:560
Async XLA Ops:
  84.4 43.2 %collective-permute-start.2 = (bf16[128,2048]{1,0:T(8,128)(2,1)}, bf16[128,2048]{1,0:T(8,128)(2,1)S(1)}, u32[]{:S(2)}, u32[]{:S(2)}) collective-permute-start(bf16[128,2048]{1,0:T(8,128)(2,1)} %get-tuple-element.26), channel_id=1, source_target_pairs={{0,6},{1,7},{2,4},{3,5},{4,2},{5,3},{6,0},{7,1},{8,14},{9,15},{10,... | collective-permute-start | bytes 1572872 | tf_op jit(solution)/shard_map/ppermute | solution.py:553
  86.6 41.1 %collective-permute-start = (bf16[128,4096]{1,0:T(8,128)(2,1)}, bf16[128,4096]{1,0:T(8,128)(2,1)S(1)}, u32[]{:S(2)}, u32[]{:S(2)}) collective-permute-start(bf16[128,4096]{1,0:T(8,128)(2,1)} %get-tuple-element.24), channel_id=1, source_target_pairs={{0,2},{1,3},{2,0},{3,1},{4,6},{5,7},{6,4},{7,5},{8,10},{9,11},{10,... | collective-permute-start | bytes 3145736 | tf_op jit(solution)/shard_map/ppermute | solution.py:553
  87.5 40.2 %collective-permute-start.1 = (bf16[128,4096]{1,0:T(8,128)(2,1)}, bf16[128,4096]{1,0:T(8,128)(2,1)S(1)}, u32[]{:S(2)}, u32[]{:S(2)}) collective-permute-start(bf16[128,4096]{1,0:T(8,128)(2,1)} %get-tuple-element.25), channel_id=1, source_target_pairs={{0,4},{1,5},{2,6},{3,7},{4,0},{5,1},{6,2},{7,3},{8,12},{9,13},{10,... | collective-permute-start | bytes 3145736 | tf_op jit(solution)/shard_map/ppermute | solution.py:553
  88.0 39.7 %copy-start = (bf16[128,4096]{1,0:T(8,128)(2,1)S(1)}, bf16[128,4096]{1,0:T(8,128)(2,1)}, u32[]{:S(2)}) copy-start(bf16[128,4096]{1,0:T(8,128)(2,1)} %get-tuple-element.23) | copy-start | bytes 3145732

commit v7 on v6

--- a/solution.py
+++ b/solution.py
@@ -276,15 +276,18 @@
     per = -(-blocks // NH)
 
     def phase2(i, carry):
-        for first, ks in ((NH - 3, range(0, 2)), (NH - 2, range(2, 4)), (NH - 1, range(4, 6)), (NH, range(6, NH))):
+        for first, ks in ((NH - 1, range(0, 3)), (NH, range(3, NH))):
             @pl.when(i == first)
             def _():
                 for k in ks:
                     ag_last(xa_ref, xs, xr, k)
 
+        @pl.when(i < NH - 1)
+        def _():
+            ag_mid(xa_ref, xs, xr, i + 1)
+
         @pl.when(i < NH)
         def _():
-            ag_mid(xa_ref, xs, xr, i)
             w_load(i, 0).wait()
             w_load(i, 1).wait()
             slot = (i + 1) % 2
@@ -318,9 +321,9 @@
                 for o in sums_out(k, True):
                     o.start()
 
-        @pl.when((i >= half) & (i < NH))
-        def _():
-            k = i - half
+        @pl.when(i >= NH + 1 - half)
+        def _():
+            k = i - (NH + 1 - half)
             rs1(k).wait_recv()
             add(n2(k), k, r1v[k])
             for o in sums_out(k, False):
@@ -328,6 +331,7 @@
 
         return carry
 
+    ag_mid(xa_ref, xs, xr, 0)
     lax.fori_loop(0, NH + 1, phase2, 0)
     outs = [pltpu.make_async_copy(v.at[pl.ds(0, ff), :], ref, ol.at[i])
             for i, (v, ref) in enumerate(((ugv, dgt_ref), (uuv, dut_ref)))]
@@ -443,8 +447,6 @@
     zl.start()
     for c in y_loads(1) + x_loads(1):
         c.start()
-    for p in parts:
-        take(p).start()
 
     def body(*flat):
         h = len(flat) // 2
@@ -453,9 +455,6 @@
         product(1, 0, accs, [[gl, first[0]], first[1:]])
         product(2, 0, accs, [[ul], []])
         zl.wait()
-        for p in parts:
-            take(p).wait()
-            give(p).start()
 
         def rest(j, carry):
             for c in y_loads(j) + x_loads(j):
@@ -465,6 +464,17 @@
             def _():
                 for c in y_loads(j + 1) + x_loads(j + 1):
                     c.start()
+
+            @pl.when(j == 1)
+            def _():
+                for p in parts:
+                    take(p).start()
+
+            @pl.when(j == 2)
+            def _():
+                for p in parts:
+                    take(p).wait()
+                    give(p).start()
 
             @pl.when(j >= 2)
             def _():

time: 129 us -> 125 us (0.969)
  Pallas kernels: 123 us -> 119 us
    pallas_call x1, Pallas kernels: 39.7 us -> 36.5 us  [_weight_grads(): pl.pallas_call(_weight_kernel, out_shape=(jax.ShapeDtypeStruct((ff, hid),...]
  transfers between devices with their start and end apart: 3 -> 3, of which waited for: 0 -> 0; matrix products, arithmetic and copies ran while one was open for 0% -> 0% of each run, Pallas kernels for 31% -> 29%
where the time goes in v7:
time: 125 us
  Pallas kernels  119 us (95%)
  starting transfers between devices  3.52 us (3%)
  other arithmetic  1.54 us (1%)
    pallas_call x1, Pallas kernels, local_backward(): pl.pallas_call(_comm_kernel, out_shape=(own, own, own, half, act, act, ac...  82.9 us
    pallas_call x1, Pallas kernels, _weight_grads(): pl.pallas_call(_weight_kernel, out_shape=(jax.ShapeDtypeStruct((ff, hid),...  36.5 us
    ppermute x3, starting transfers between devices, to(): return lax.ppermute(v, 'tp', [(i, i ^ flip) for i in range(8)])  3.52 us
  transfers between devices with their start and end apart: 3, of which 0 were waited for; matrix products, arithmetic and copies ran while one was open for 0% of the time, Pallas kernels for 29%

profile of v7, /device:TPU:0, one launch (start us, length us, event | category | flops | bytes accessed | tf_op | source)
XLA Modules:
  0.0 125.1 jit_solution(12931094497821012165)
XLA Ops:
  0.6 82.9 %gather_partial.1 = (bf16[128,4096]{1,0:T(8,128)(2,1)}, bf16[128,4096]{1,0:T(8,128)(2,1)}, bf16[128,4096]{1,0:T(8,128)(2,1)}, bf16[128,2048]{1,0:T(8,128)(2,1)},...) custom-call(bf16[128,4096]{1,0:T(8,128)(2,1)} %x_ref.1, ...), custom_call_target="tpu_custom_call" | custom-call | tf_op jit(solution)/shard_map/gather_partial/pallas_call | solution.py:533
  83.5 1.5 %collective-permute-start.2 = (bf16[128,2048]{1,0:T(8,128)(2,1)}, bf16[128,2048]{1,0:T(8,128)(2,1)S(1)}, u32[]{:S(2)}, u32[]{:S(2)}) collective-permute-start(bf16[128,2048]{1,0:T(8,128)(2,1)} %get-tuple-element.26), channel_id=1, source_target_pairs={{0,6},{1,7},{2,4},{3,5},{4,2},{5,3},{6,0},{7,1},{8,14},{9,15},{10,... | collective-permute-start | bytes 1572872 | tf_op jit(solution)/shard_map/ppermute | solution.py:563
  85.0 1.5 %collective-permute-start = (bf16[128,4096]{1,0:T(8,128)(2,1)}, bf16[128,4096]{1,0:T(8,128)(2,1)S(1)}, u32[]{:S(2)}, u32[]{:S(2)}) collective-permute-start(bf16[128,4096]{1,0:T(8,128)(2,1)} %get-tuple-element.24), channel_id=1, source_target_pairs={{0,2},{1,3},{2,0},{3,1},{4,6},{5,7},{6,4},{7,5},{8,10},{9,11},{10,... | collective-permute-start | bytes 3145736 | tf_op jit(solution)/shard_map/ppermute | solution.py:563
  86.5 0.5 collective-permute-start.1
  87.0 0.0 copy-start
  87.0 36.5 %weight_grads.1 = (f32[1376,4096]{1,0:T(8,128)}, f32[1376,4096]{1,0:T(8,128)}, f32[1376,4096]{1,0:T(8,128)}) custom-call(bf16[1376,1024]{1,0:T(8,128)(2,1)} %get-tuple-element.27.zt_ref, bf16[1376,1024]{1,0:T(8,128)(2,1)} %get-tuple-element.28.dgt_ref, bf16[1376,1024]{1,0:T(8,128)(2,1)} %get-tuple-element.29.dut_ref, bf16[1024,4096]{1,0:T(8,128)(2,1)} %bitcast.12, ...), custom_call_target="tpu_custom_call" | custom-call | flops 34628173824 | bytes 67633152 | tf_op jit(solution)/shard_map/weight_grads/pallas_call | solution.py:506
  123.6 0.0 collective-permute-done.2
  123.6 0.0 collective-permute-done
  123.6 0.0 collective-permute-done.1
  123.6 0.0 copy-done
  123.6 1.5 %add_convert_fusion = bf16[128,4096]{1,0:T(8,128)(2,1)} fusion(bf16[128,4096]{1,0:T(8,128)(2,1)S(1)} %collective-permute-done.1, bf16[128,4096]{1,0:T(8,128)(2,1)S(1)} %collective-permute-done, bf16[128,4096]{1,0:T(8,128)(2,1)S(1)} %copy-done, bf16[128,2048]{1,0:T(8,128)(2,1)S(1)} %collective-permute-done.2), kind=kLoop, calls=%fused_computation | loop fusion | flops 4194304 | bytes 4718592 | tf_op jit(solution)/shard_map/convert_element_type | solution.py:570
Async XLA Ops:
  83.5 40.1 %collective-permute-start.2 = (bf16[128,2048]{1,0:T(8,128)(2,1)}, bf16[128,2048]{1,0:T(8,128)(2,1)S(1)}, u32[]{:S(2)}, u32[]{:S(2)}) collective-permute-start(bf16[128,2048]{1,0:T(8,128)(2,1)} %get-tuple-element.26), channel_id=1, source_target_pairs={{0,6},{1,7},{2,4},{3,5},{4,2},{5,3},{6,0},{7,1},{8,14},{9,15},{10,... | collective-permute-start | bytes 1572872 | tf_op jit(solution)/shard_map/ppermute | solution.py:563
  85.0 38.6 %collective-permute-start = (bf16[128,4096]{1,0:T(8,128)(2,1)}, bf16[128,4096]{1,0:T(8,128)(2,1)S(1)}, u32[]{:S(2)}, u32[]{:S(2)}) collective-permute-start(bf16[128,4096]{1,0:T(8,128)(2,1)} %get-tuple-element.24), channel_id=1, source_target_pairs={{0,2},{1,3},{2,0},{3,1},{4,6},{5,7},{6,4},{7,5},{8,10},{9,11},{10,... | collective-permute-start | bytes 3145736 | tf_op jit(solution)/shard_map/ppermute | solution.py:563
  86.5 37.1 %collective-permute-start.1 = (bf16[128,4096]{1,0:T(8,128)(2,1)}, bf16[128,4096]{1,0:T(8,128)(2,1)S(1)}, u32[]{:S(2)}, u32[]{:S(2)}) collective-permute-start(bf16[128,4096]{1,0:T(8,128)(2,1)} %get-tuple-element.25), channel_id=1, source_target_pairs={{0,4},{1,5},{2,6},{3,7},{4,0},{5,1},{6,2},{7,3},{8,12},{9,13},{10,... | collective-permute-start | bytes 3145736 | tf_op jit(solution)/shard_map/ppermute | solution.py:563
  87.0 36.6 %copy-start = (bf16[128,4096]{1,0:T(8,128)(2,1)S(1)}, bf16[128,4096]{1,0:T(8,128)(2,1)}, u32[]{:S(2)}) copy-start(bf16[128,4096]{1,0:T(8,128)(2,1)} %get-tuple-element.23) | copy-start | bytes 3145732

commit v8 on v7

--- a/solution.py
+++ b/solution.py
@@ -11,6 +11,7 @@
 BF16 = jnp.bfloat16
 F32 = jnp.float32
 NH = 8
+HOPS = 2
 DOWN = 2
 NY = 16
 AHEAD, LAG, TAKE = 4, 4, 6
@@ -31,7 +32,6 @@
     nfull, rest = ff // 128, ff % 128
     hc = hid // NH
     tall = 8 * tok
-    half = NH // 2
 
     t = lax.axis_index("tp")
     ty, tx, tc = t // 4, (t // 2) % 2, t % 2
@@ -259,7 +259,7 @@
         return rcopy(blk(dyv, dg, k), r1v.at[k], rs.at[1], r1r.at[k], n1(k))
 
     def sums_out(k, diagonal):
-        outs = [(so_ref, t, k), (sx_ref, xn, k), (sy_ref, yn, k)] + ([(sd_ref, dg, k - half)] if diagonal else [])
+        outs = [(so_ref, t, k), (sx_ref, xn, k), (sy_ref, yn, k)] + ([(sd_ref, dg, k - HOPS)] if diagonal else [])
         return [pltpu.make_async_copy(blk(dyv, owner, k), ref.at[:, cols(c)], po.at[i])
                 for i, (ref, owner, c) in enumerate(outs)]
 
@@ -267,16 +267,20 @@
         b = blk(dyv, owner, k)
         b[...] = (b[...].astype(F32) + other.astype(F32)).astype(BF16)
 
-    def t_block(r0):
-        rows = pl.ds(r0, 128)
-        ugv[rows, :] = duv[:, rows].T
-        uuv[rows, :] = duv[:, pl.ds(fp + r0, 128)].T
+    def t_block(b):
+        src = pl.multiple_of(jnp.minimum(b, blocks - 1) * 128, 128)
+        rows = pl.ds(pl.multiple_of(jnp.minimum(b, blocks) * 128, 128), 128)
+        ugv[rows, :] = duv[:, pl.ds(src, 128)].T
+        uuv[rows, :] = duv[:, pl.ds(fp + src, 128)].T
 
     blocks = fp // 128
     per = -(-blocks // NH)
 
+    outs = [pltpu.make_async_copy(v.at[pl.ds(0, ff), :], ref, ol.at[i])
+            for i, (v, ref) in enumerate(((ugv, dgt_ref), (uuv, dut_ref)))]
+
     def phase2(i, carry):
-        for first, ks in ((NH - 1, range(0, 3)), (NH, range(3, NH))):
+        for first, ks in ((NH - 1, range(0, 3)),):
             @pl.when(i == first)
             def _():
                 for k in ks:
@@ -292,7 +296,7 @@
             w_load(i, 1).wait()
             slot = (i + 1) % 2
             for b in range(per):
-                t_block(pl.multiple_of(jnp.minimum(per * i + b, blocks - 1) * 128, 128))
+                t_block(per * i + b)
             p = jnp.dot(duv[...], wbuf[slot], preferred_element_type=F32)
             dyv[:, :, :, cols(i)] = p.astype(BF16).reshape(4, 2, tok, hc)
 
@@ -300,6 +304,11 @@
             def _():
                 w_load(i + 2, 0).start()
                 w_load(i + 2, 1).start()
+
+        @pl.when(i == -(-blocks // per))
+        def _():
+            for o in outs:
+                o.start()
 
         @pl.when(i < NH)
         def _():
@@ -312,18 +321,18 @@
             for q in range(4):
                 add(2 * q + tc, k, r0v[k, q])
 
-            @pl.when(k < half)
+            @pl.when(k < HOPS)
             def _():
                 rs1(k).start()
 
-            @pl.when(k >= half)
+            @pl.when(k >= HOPS)
             def _():
                 for o in sums_out(k, True):
                     o.start()
 
-        @pl.when(i >= NH + 1 - half)
-        def _():
-            k = i - (NH + 1 - half)
+        @pl.when((i >= 5) & (i < 5 + HOPS))
+        def _():
+            k = i - 5
             rs1(k).wait_recv()
             add(n2(k), k, r1v[k])
             for o in sums_out(k, False):
@@ -333,10 +342,8 @@
 
     ag_mid(xa_ref, xs, xr, 0)
     lax.fori_loop(0, NH + 1, phase2, 0)
-    outs = [pltpu.make_async_copy(v.at[pl.ds(0, ff), :], ref, ol.at[i])
-            for i, (v, ref) in enumerate(((ugv, dgt_ref), (uuv, dut_ref)))]
-    for o in outs:
-        o.start()
+    for k in range(3, NH):
+        ag_last(xa_ref, xs, xr, k)
 
     def drain(k, carry):
         ag_end(xa_ref, xs, xr, k)
@@ -346,7 +353,7 @@
     for n in range(7):
         left(xa_ref.at[0, 0], xs.at[n])
     left(dyv.at[:, 0], rs.at[0])
-    left(dyv.at[0, 0, :, pl.ds(0, hid // 2)], rs.at[1])
+    left(dyv.at[0, 0, :, pl.ds(0, HOPS * hc)], rs.at[1])
     x_put.wait()
     for n, ref in enumerate((so_ref, sx_ref, sy_ref, sd_ref)):
         pltpu.make_async_copy(ref, ref, po.at[n]).wait()
@@ -529,10 +536,10 @@
         full = jax.ShapeDtypeStruct((4, 2, tok, hid), BF16)
         act = jax.ShapeDtypeStruct((ff, tall), BF16)
         own = jax.ShapeDtypeStruct((tok, hid), BF16)
-        half = jax.ShapeDtypeStruct((tok, hid // 2), BF16)
+        rest = jax.ShapeDtypeStruct((tok, hid - HOPS * hc), BF16)
         so, sx, sy, sd, zt, dgt, dut, dya, xa, ddp = pl.pallas_call(
             _comm_kernel,
-            out_shape=(own, own, own, half, act, act, act, full, full,
+            out_shape=(own, own, own, rest, act, act, act, full, full,
                        jax.ShapeDtypeStruct((ff, DOWN * hc), F32)),
             in_specs=[any_] * 7,
             out_specs=(any_,) * 10,
@@ -544,13 +551,13 @@
                 pltpu.VMEM((tall, fp), BF16),
                 pltpu.VMEM((tall, 2 * fp), BF16),
                 pltpu.VMEM((2, 2 * fp, hc), BF16),
-                pltpu.VMEM((fp, tall), BF16),
-                pltpu.VMEM((fp, tall), BF16),
+                pltpu.VMEM((fp + 128, tall), BF16),
+                pltpu.VMEM((fp + 128, tall), BF16),
                 pltpu.VMEM((NH, 4, tok, hc), BF16),
-                pltpu.VMEM((NH // 2, tok, hc), BF16),
+                pltpu.VMEM((HOPS, tok, hc), BF16),
                 pltpu.VMEM((tok, hid), BF16),
                 pltpu.VMEM((2, ff, hc), F32),
-                sem((7,)), sem((NY, 3)), sem((7,)), sem((NH, 3)), sem((2,)), sem((NH,)), sem((NH // 2,)),
+                sem((7,)), sem((NY, 3)), sem((7,)), sem((NH, 3)), sem((2,)), sem((NH,)), sem((HOPS,)),
                 sem((NY // AHEAD,)), sem((2,)), sem((2, 2)), sem((2,)), sem((2,)), sem((1,)), sem((4,)), sem((2,)),
             ],
             compiler_params=pltpu.CompilerParams(collective_id=0, has_side_effects=True, vmem_limit_bytes=67043328),
@@ -566,7 +573,7 @@
         zt, dgt, dut, ddp = (pltpu.with_memory_space_constraint(v, pltpu.HBM) for v in (zt, dgt, dut, ddp))
         dwd, dwg, dwu = _weight_grads(zt, dgt, dut, dya, xa, ddp)
         fx, fy, fd, dwd, dwg, dwu = lax.optimization_barrier((fx, fy, fd, dwd, dwg, dwu))
-        right = jnp.pad(fd, ((0, 0), (hid // 2, 0)))
+        right = jnp.pad(fd, ((0, 0), (HOPS * hc, 0)))
         dx = sum(v.astype(F32) for v in (so, fx, fy, right)).astype(BF16)
         return dx, dwg.T, dwu.T, dwd
 

time: 125 us -> 127 us (1.016)
  waiting for transfers between devices: 0.01 us -> 3.05 us
    ppermute x3, waiting for transfers between devices: 0.01 us -> 3.05 us  [to(): return lax.ppermute(v, 'tp', [(i, i ^ flip) for i in range(8)])]
    pallas_call x1, Pallas kernels: 82.9 us -> 81.4 us  [local_backward(): pl.pallas_call(_comm_kernel, out_shape=(own, own, own, rest, act, act, ac...]
  transfers between devices with their start and end apart: 3 -> 3, of which waited for: 0 -> 1; matrix products, arithmetic and copies ran while one was open for 0% -> 0% of each run, Pallas kernels for 29% -> 29%
where the time goes in v8:
time: 127 us
  Pallas kernels  118 us (93%)
  starting transfers between devices  3.52 us (3%)
  waiting for transfers between devices  3.05 us (2%)
  other arithmetic  1.58 us (1%)
    pallas_call x1, Pallas kernels, local_backward(): pl.pallas_call(_comm_kernel, out_shape=(own, own, own, rest, act, act, ac...  81.4 us
    pallas_call x1, Pallas kernels, _weight_grads(): pl.pallas_call(_weight_kernel, out_shape=(jax.ShapeDtypeStruct((ff, hid),...  36.5 us
    ppermute x3, starting transfers between devices, to(): return lax.ppermute(v, 'tp', [(i, i ^ flip) for i in range(8)])  3.52 us
    ppermute x3, waiting for transfers between devices, to(): return lax.ppermute(v, 'tp', [(i, i ^ flip) for i in range(8)])  3.05 us
  transfers between devices with their start and end apart: 3, of which 1 were waited for; matrix products, arithmetic and copies ran while one was open for 0% of the time, Pallas kernels for 29%

profile of v8, /device:TPU:0, one launch (start us, length us, event | category | flops | bytes accessed | tf_op | source)
XLA Modules:
  0.0 126.7 jit_solution(1195043416480647140)
XLA Ops:
  0.6 81.4 %gather_partial.1 = (bf16[128,4096]{1,0:T(8,128)(2,1)}, bf16[128,4096]{1,0:T(8,128)(2,1)}, bf16[128,4096]{1,0:T(8,128)(2,1)}, bf16[128,3072]{1,0:T(8,128)(2,1)},...) custom-call(bf16[128,4096]{1,0:T(8,128)(2,1)} %x_ref.1, ...), custom_call_target="tpu_custom_call" | custom-call | tf_op jit(solution)/shard_map/gather_partial/pallas_call | solution.py:540
  82.0 1.5 %collective-permute-start.2 = (bf16[128,3072]{1,0:T(8,128)(2,1)}, bf16[128,3072]{1,0:T(8,128)(2,1)S(1)}, u32[]{:S(2)}, u32[]{:S(2)}) collective-permute-start(bf16[128,3072]{1,0:T(8,128)(2,1)} %get-tuple-element.26), channel_id=1, source_target_pairs={{0,6},{1,7},{2,4},{3,5},{4,2},{5,3},{6,0},{7,1},{8,14},{9,15},{10,... | collective-permute-start | bytes 2359304 | tf_op jit(solution)/shard_map/ppermute | solution.py:570
  83.5 1.5 %collective-permute-start = (bf16[128,4096]{1,0:T(8,128)(2,1)}, bf16[128,4096]{1,0:T(8,128)(2,1)S(1)}, u32[]{:S(2)}, u32[]{:S(2)}) collective-permute-start(bf16[128,4096]{1,0:T(8,128)(2,1)} %get-tuple-element.24), channel_id=1, source_target_pairs={{0,2},{1,3},{2,0},{3,1},{4,6},{5,7},{6,4},{7,5},{8,10},{9,11},{10,... | collective-permute-start | bytes 3145736 | tf_op jit(solution)/shard_map/ppermute | solution.py:570
  85.0 0.5 collective-permute-start.1
  85.5 0.0 copy-start
  85.5 36.5 %weight_grads.1 = (f32[1376,4096]{1,0:T(8,128)}, f32[1376,4096]{1,0:T(8,128)}, f32[1376,4096]{1,0:T(8,128)}) custom-call(bf16[1376,1024]{1,0:T(8,128)(2,1)} %get-tuple-element.27.zt_ref, bf16[1376,1024]{1,0:T(8,128)(2,1)} %get-tuple-element.28.dgt_ref, bf16[1376,1024]{1,0:T(8,128)(2,1)} %get-tuple-element.29.dut_ref, bf16[1024,4096]{1,0:T(8,128)(2,1)} %bitcast.12, ...), custom_call_target="tpu_custom_call" | custom-call | flops 34628173824 | bytes 67633152 | tf_op jit(solution)/shard_map/weight_grads/pallas_call | solution.py:513
  122.1 0.0 collective-permute-done.2
  122.1 3.0 %collective-permute-done = bf16[128,4096]{1,0:T(8,128)(2,1)S(1)} collective-permute-done((bf16[128,4096]{1,0:T(8,128)(2,1)}, bf16[128,4096]{1,0:T(8,128)(2,1)S(1)}, u32[]{:S(2)}, u32[]{:S(2)}) %collective-permute-start) | collective-permute-done | bytes 1048608 | tf_op jit(solution)/shard_map/ppermute | solution.py:570
  125.1 0.0 collective-permute-done.1
  125.1 0.0 copy-done
  125.1 1.6 %add_convert_fusion = bf16[128,4096]{1,0:T(8,128)(2,1)} fusion(bf16[128,4096]{1,0:T(8,128)(2,1)S(1)} %collective-permute-done.1, bf16[128,4096]{1,0:T(8,128)(2,1)S(1)} %collective-permute-done, bf16[128,4096]{1,0:T(8,128)(2,1)S(1)} %copy-done, bf16[128,3072]{1,0:T(8,128)(2,1)S(1)} %collective-permute-done.2), kind=kLoop, calls=%fused_computation | loop fusion | flops 4194304 | bytes 4980736 | tf_op jit(solution)/shard_map/convert_element_type | solution.py:577
Async XLA Ops:
  82.0 40.1 %collective-permute-start.2 = (bf16[128,3072]{1,0:T(8,128)(2,1)}, bf16[128,3072]{1,0:T(8,128)(2,1)S(1)}, u32[]{:S(2)}, u32[]{:S(2)}) collective-permute-start(bf16[128,3072]{1,0:T(8,128)(2,1)} %get-tuple-element.26), channel_id=1, source_target_pairs={{0,6},{1,7},{2,4},{3,5},{4,2},{5,3},{6,0},{7,1},{8,14},{9,15},{10,... | collective-permute-start | bytes 2359304 | tf_op jit(solution)/shard_map/ppermute | solution.py:570
  83.5 41.6 %collective-permute-start = (bf16[128,4096]{1,0:T(8,128)(2,1)}, bf16[128,4096]{1,0:T(8,128)(2,1)S(1)}, u32[]{:S(2)}, u32[]{:S(2)}) collective-permute-start(bf16[128,4096]{1,0:T(8,128)(2,1)} %get-tuple-element.24), channel_id=1, source_target_pairs={{0,2},{1,3},{2,0},{3,1},{4,6},{5,7},{6,4},{7,5},{8,10},{9,11},{10,... | collective-permute-start | bytes 3145736 | tf_op jit(solution)/shard_map/ppermute | solution.py:570
  85.0 40.1 %collective-permute-start.1 = (bf16[128,4096]{1,0:T(8,128)(2,1)}, bf16[128,4096]{1,0:T(8,128)(2,1)S(1)}, u32[]{:S(2)}, u32[]{:S(2)}) collective-permute-start(bf16[128,4096]{1,0:T(8,128)(2,1)} %get-tuple-element.25), channel_id=1, source_target_pairs={{0,4},{1,5},{2,6},{3,7},{4,0},{5,1},{6,2},{7,3},{8,12},{9,13},{10,... | collective-permute-start | bytes 3145736 | tf_op jit(solution)/shard_map/ppermute | solution.py:570
  85.5 39.6 %copy-start = (bf16[128,4096]{1,0:T(8,128)(2,1)S(1)}, bf16[128,4096]{1,0:T(8,128)(2,1)}, u32[]{:S(2)}) copy-start(bf16[128,4096]{1,0:T(8,128)(2,1)} %get-tuple-element.23) | copy-start | bytes 3145732

commit v9 on v8

--- a/solution.py
+++ b/solution.py
@@ -11,7 +11,7 @@
 BF16 = jnp.bfloat16
 F32 = jnp.float32
 NH = 8
-HOPS = 2
+HOPS = 4
 DOWN = 2
 NY = 16
 AHEAD, LAG, TAKE = 4, 4, 6
@@ -422,11 +422,11 @@
 
         late = None
         for s, (pair, c, row, size, kt) in enumerate(steps):
-            if s == 0 or (c == 0 and kt == 0 and waits):
-                for w in waits[pair] if waits else ():
+            if s == 0 or (kt == 0 and (pair, c) in waits):
+                for w in waits.get((pair, c), ()):
                     w.wait()
                 push(s)
-            if s + 1 < len(steps) and not (waits and steps[s + 1][1] == 0 and steps[s + 1][4] == 0):
+            if s + 1 < len(steps) and not (steps[s + 1][4] == 0 and steps[s + 1][:2] in waits):
                 push(s + 1)
             block = a[row:row + size, kt * 256:kt * 256 + 256]
             for q in range(2):
@@ -443,14 +443,13 @@
     def give(p):
         return pltpu.make_async_copy(cv.at[p], dd_ref.at[:, p * 512:p * 512 + 512], co.at[p])
 
-    zl, gl, ul = (pltpu.make_async_copy(src, dst, ls.at[i])
-                  for i, (src, dst) in enumerate(((zt_ref, zv), (dgt_ref, dgv), (dut_ref, duv))))
+    zl, ul = (pltpu.make_async_copy(src, dst, ls.at[i]) for i, (src, dst) in enumerate(((zt_ref, zv), (dut_ref, duv))))
+    gl = [pltpu.make_async_copy(dgt_ref.at[rows, :], dgv.at[rows, :], ls.at[2 + i])
+          for i, rows in enumerate((pl.ds(0, sizes[0]), pl.ds(sizes[0], ff - sizes[0])))]
     parts = range(nb // 512)
     first = x_loads(0)
-    gl.start()
-    for c in first:
+    for c in (gl[0], first[0], gl[1], *first[1:], ul):
         c.start()
-    ul.start()
     zl.start()
     for c in y_loads(1) + x_loads(1):
         c.start()
@@ -459,8 +458,8 @@
         h = len(flat) // 2
         accs = [[part[2] if i == len(sizes) - 1 else part[i % 2] for i in range(len(sizes))]
                 for part in (flat[:h], flat[h:])]
-        product(1, 0, accs, [[gl, first[0]], first[1:]])
-        product(2, 0, accs, [[ul], []])
+        product(1, 0, accs, {(0, 0): [gl[0], first[0]], (0, 1): gl[1:], (1, 0): first[1:]})
+        product(2, 0, accs, {(0, 0): [ul]})
         zl.wait()
 
         def rest(j, carry):
@@ -490,7 +489,7 @@
 
             put_all(1, j - 1).wait()
             for i in range(3):
-                product(i, j, accs, None)
+                product(i, j, accs, {})
             return carry
 
         lax.fori_loop(1, n, rest, 0)
@@ -517,7 +516,7 @@
         out_specs=(any_,) * 3,
         scratch_shapes=[pltpu.VMEM((ff, tall), BF16)] * 3 + [pltpu.VMEM((2, tall, nb), BF16)] * 2
         + [pltpu.VMEM((k, ff, nb), F32) for k in (1, 1, 2)] + [pltpu.VMEM((nb // 512, ff, 512), F32)]
-        + [sem((3,)), sem((2, 2)), sem((2, 2)), sem((3, 2)), sem((2,)), sem((2,))],
+        + [sem((4,)), sem((2, 2)), sem((2, 2)), sem((3, 2)), sem((2,)), sem((2,))],
         compiler_params=pltpu.CompilerParams(vmem_limit_bytes=54 * 2 ** 20),
         cost_estimate=pl.CostEstimate(flops=6 * ff * tall * hid, bytes_accessed=12 * ff * hid, transcendentals=0),
         name="weight_grads",

time: 127 us -> 124 us (0.976)
  waiting for transfers between devices: 3.05 us -> 0.01 us
    ppermute x3, waiting for transfers between devices: 3.05 us -> 0.01 us  [to(): return lax.ppermute(v, 'tp', [(i, i ^ flip) for i in range(8)])]
  transfers between devices with their start and end apart: 3 -> 3, of which waited for: 1 -> 0; matrix products, arithmetic and copies ran while one was open for 0% -> 0% of each run, Pallas kernels for 29% -> 30%
where the time goes in v9:
time: 124 us
  Pallas kernels  118 us (95%)
  starting transfers between devices  3.52 us (3%)
  other arithmetic  1.54 us (1%)
    pallas_call x1, Pallas kernels, local_backward(): pl.pallas_call(_comm_kernel, out_shape=(own, own, own, rest, act, act, ac...  81.4 us
    pallas_call x1, Pallas kernels, _weight_grads(): pl.pallas_call(_weight_kernel, out_shape=(jax.ShapeDtypeStruct((ff, hid),...  36.7 us
    ppermute x3, starting transfers between devices, to(): return lax.ppermute(v, 'tp', [(i, i ^ flip) for i in range(8)])  3.52 us
  transfers between devices with their start and end apart: 3, of which 0 were waited for; matrix products, arithmetic and copies ran while one was open for 0% of the time, Pallas kernels for 30%

profile of v9, /device:TPU:0, one launch (start us, length us, event | category | flops | bytes accessed | tf_op | source)
XLA Modules:
  0.0 123.9 jit_solution(8125666942792610310)
XLA Ops:
  0.6 81.4 %gather_partial.1 = (bf16[128,4096]{1,0:T(8,128)(2,1)}, bf16[128,4096]{1,0:T(8,128)(2,1)}, bf16[128,4096]{1,0:T(8,128)(2,1)}, bf16[128,2048]{1,0:T(8,128)(2,1)},...) custom-call(bf16[128,4096]{1,0:T(8,128)(2,1)} %x_ref.1, ...), custom_call_target="tpu_custom_call" | custom-call | tf_op jit(solution)/shard_map/gather_partial/pallas_call | solution.py:539
  82.1 1.5 %collective-permute-start.2 = (bf16[128,2048]{1,0:T(8,128)(2,1)}, bf16[128,2048]{1,0:T(8,128)(2,1)S(1)}, u32[]{:S(2)}, u32[]{:S(2)}) collective-permute-start(bf16[128,2048]{1,0:T(8,128)(2,1)} %get-tuple-element.26), channel_id=1, source_target_pairs={{0,6},{1,7},{2,4},{3,5},{4,2},{5,3},{6,0},{7,1},{8,14},{9,15},{10,... | collective-permute-start | bytes 1572872 | tf_op jit(solution)/shard_map/ppermute | solution.py:569
  83.6 1.5 %collective-permute-start = (bf16[128,4096]{1,0:T(8,128)(2,1)}, bf16[128,4096]{1,0:T(8,128)(2,1)S(1)}, u32[]{:S(2)}, u32[]{:S(2)}) collective-permute-start(bf16[128,4096]{1,0:T(8,128)(2,1)} %get-tuple-element.24), channel_id=1, source_target_pairs={{0,2},{1,3},{2,0},{3,1},{4,6},{5,7},{6,4},{7,5},{8,10},{9,11},{10,... | collective-permute-start | bytes 3145736 | tf_op jit(solution)/shard_map/ppermute | solution.py:569
  85.1 0.5 collective-permute-start.1
  85.6 0.0 copy-start
  85.6 36.7 %weight_grads.1 = (f32[1376,4096]{1,0:T(8,128)}, f32[1376,4096]{1,0:T(8,128)}, f32[1376,4096]{1,0:T(8,128)}) custom-call(bf16[1376,1024]{1,0:T(8,128)(2,1)} %get-tuple-element.27.zt_ref, bf16[1376,1024]{1,0:T(8,128)(2,1)} %get-tuple-element.28.dgt_ref, bf16[1376,1024]{1,0:T(8,128)(2,1)} %get-tuple-element.29.dut_ref, bf16[1024,4096]{1,0:T(8,128)(2,1)} %bitcast.12, ...), custom_call_target="tpu_custom_call" | custom-call | flops 34628173824 | bytes 67633152 | tf_op jit(solution)/shard_map/weight_grads/pallas_call | solution.py:512
  122.3 0.0 collective-permute-done.2
  122.3 0.0 collective-permute-done
  122.4 0.0 collective-permute-done.1
  122.4 0.0 copy-done
  122.4 1.5 %add_convert_fusion = bf16[128,4096]{1,0:T(8,128)(2,1)} fusion(bf16[128,4096]{1,0:T(8,128)(2,1)S(1)} %collective-permute-done.1, bf16[128,4096]{1,0:T(8,128)(2,1)S(1)} %collective-permute-done, bf16[128,4096]{1,0:T(8,128)(2,1)S(1)} %copy-done, bf16[128,2048]{1,0:T(8,128)(2,1)S(1)} %collective-permute-done.2), kind=kLoop, calls=%fused_computation | loop fusion | flops 4194304 | bytes 4718592 | tf_op jit(solution)/shard_map/convert_element_type | solution.py:576
Async XLA Ops:
  82.1 40.3 %collective-permute-start.2 = (bf16[128,2048]{1,0:T(8,128)(2,1)}, bf16[128,2048]{1,0:T(8,128)(2,1)S(1)}, u32[]{:S(2)}, u32[]{:S(2)}) collective-permute-start(bf16[128,2048]{1,0:T(8,128)(2,1)} %get-tuple-element.26), channel_id=1, source_target_pairs={{0,6},{1,7},{2,4},{3,5},{4,2},{5,3},{6,0},{7,1},{8,14},{9,15},{10,... | collective-permute-start | bytes 1572872 | tf_op jit(solution)/shard_map/ppermute | solution.py:569
  83.6 38.8 %collective-permute-start = (bf16[128,4096]{1,0:T(8,128)(2,1)}, bf16[128,4096]{1,0:T(8,128)(2,1)S(1)}, u32[]{:S(2)}, u32[]{:S(2)}) collective-permute-start(bf16[128,4096]{1,0:T(8,128)(2,1)} %get-tuple-element.24), channel_id=1, source_target_pairs={{0,2},{1,3},{2,0},{3,1},{4,6},{5,7},{6,4},{7,5},{8,10},{9,11},{10,... | collective-permute-start | bytes 3145736 | tf_op jit(solution)/shard_map/ppermute | solution.py:569
  85.1 37.3 %collective-permute-start.1 = (bf16[128,4096]{1,0:T(8,128)(2,1)}, bf16[128,4096]{1,0:T(8,128)(2,1)S(1)}, u32[]{:S(2)}, u32[]{:S(2)}) collective-permute-start(bf16[128,4096]{1,0:T(8,128)(2,1)} %get-tuple-element.25), channel_id=1, source_target_pairs={{0,4},{1,5},{2,6},{3,7},{4,0},{5,1},{6,2},{7,3},{8,12},{9,13},{10,... | collective-permute-start | bytes 3145736 | tf_op jit(solution)/shard_map/ppermute | solution.py:569
  85.6 36.8 %copy-start = (bf16[128,4096]{1,0:T(8,128)(2,1)S(1)}, bf16[128,4096]{1,0:T(8,128)(2,1)}, u32[]{:S(2)}) copy-start(bf16[128,4096]{1,0:T(8,128)(2,1)} %get-tuple-element.23) | copy-start | bytes 3145732

commit v10 on v9

--- a/solution.py
+++ b/solution.py
@@ -11,8 +11,8 @@
 BF16 = jnp.bfloat16
 F32 = jnp.float32
 NH = 8
-HOPS = 4
-DOWN = 2
+HOPS = 6
+DOWN = 4
 NY = 16
 AHEAD, LAG, TAKE = 4, 4, 6
 NT = (((1,), (1,)), ((), ()))
@@ -163,7 +163,7 @@
         spv[:, lanes] = sp.T
         utv[:, lanes] = uu.T.astype(BF16)
 
-    down0 = -(-(fp // 128) // per_h) * per_h
+    down0 = fp // 128
 
     def phase1(i, carry):
         @pl.when((i < NY - AHEAD) & (i % AHEAD == 0))
@@ -213,9 +213,9 @@
             def _():
                 wd_load(k + 2).start()
 
-        @pl.when((i >= down0) & ((i - down0) % per_h == 0) & (i < down0 + DOWN * per_h))
-        def _():
-            k = (i - down0) // per_h
+        @pl.when((i >= down0) & (i < down0 + DOWN))
+        def _():
+            k = i - down0
 
             @pl.when(k >= 2)
             def _():
@@ -279,6 +279,12 @@
     outs = [pltpu.make_async_copy(v.at[pl.ds(0, ff), :], ref, ol.at[i])
             for i, (v, ref) in enumerate(((ugv, dgt_ref), (uuv, dut_ref)))]
 
+    def hop_end(k):
+        rs1(k).wait_recv()
+        add(n2(k), k, r1v[k])
+        for o in sums_out(k, False):
+            o.start()
+
     def phase2(i, carry):
         for first, ks in ((NH - 1, range(0, 3)),):
             @pl.when(i == first)
@@ -332,16 +338,14 @@
 
         @pl.when((i >= 5) & (i < 5 + HOPS))
         def _():
-            k = i - 5
-            rs1(k).wait_recv()
-            add(n2(k), k, r1v[k])
-            for o in sums_out(k, False):
-                o.start()
+            hop_end(i - 5)
 
         return carry
 
     ag_mid(xa_ref, xs, xr, 0)
     lax.fori_loop(0, NH + 1, phase2, 0)
+    for k in range(NH - 4, HOPS):
+        hop_end(k)
     for k in range(3, NH):
         ag_last(xa_ref, xs, xr, k)
 
@@ -446,12 +450,11 @@
     zl, ul = (pltpu.make_async_copy(src, dst, ls.at[i]) for i, (src, dst) in enumerate(((zt_ref, zv), (dut_ref, duv))))
     gl = [pltpu.make_async_copy(dgt_ref.at[rows, :], dgv.at[rows, :], ls.at[2 + i])
           for i, rows in enumerate((pl.ds(0, sizes[0]), pl.ds(sizes[0], ff - sizes[0])))]
-    parts = range(nb // 512)
+    parts = range(part_ref.shape[1] // 512)
+    early, late = parts[:len(parts) // 2], parts[len(parts) // 2:]
+    start = part_ref.shape[1] // nb
     first = x_loads(0)
-    for c in (gl[0], first[0], gl[1], *first[1:], ul):
-        c.start()
-    zl.start()
-    for c in y_loads(1) + x_loads(1):
+    for c in (gl[0], first[0], gl[1], *first[1:], ul, *x_loads(1), zl, *y_loads(start)):
         c.start()
 
     def body(*flat):
@@ -460,6 +463,15 @@
                 for part in (flat[:h], flat[h:])]
         product(1, 0, accs, {(0, 0): [gl[0], first[0]], (0, 1): gl[1:], (1, 0): first[1:]})
         product(2, 0, accs, {(0, 0): [ul]})
+        for c in x_loads(1):
+            c.wait()
+        for c in x_loads(2):
+            c.start()
+        for p in early:
+            take(p).start()
+        put_all(1, 0).wait()
+        product(1, 1, accs, {})
+        product(2, 1, accs, {})
         zl.wait()
 
         def rest(j, carry):
@@ -471,28 +483,33 @@
                 for c in y_loads(j + 1) + x_loads(j + 1):
                     c.start()
 
-            @pl.when(j == 1)
-            def _():
-                for p in parts:
-                    take(p).start()
-
-            @pl.when(j == 2)
-            def _():
-                for p in parts:
+            @pl.when(j > start)
+            def _():
+                put_all(0, j - 1).wait()
+
+            put_all(1, j - 1).wait()
+            put_all(2, j - 2).wait()
+            product(0, j, accs, {})
+
+            @pl.when(j == start)
+            def _():
+                for p in early:
                     take(p).wait()
                     give(p).start()
-
-            @pl.when(j >= 2)
-            def _():
-                put_all(0, j - 1).wait()
-                put_all(2, j - 2).wait()
-
-            put_all(1, j - 1).wait()
-            for i in range(3):
-                product(i, j, accs, {})
+                for p in late:
+                    take(p).start()
+
+            @pl.when(j == start + 1)
+            def _():
+                for p in late:
+                    take(p).wait()
+                    give(p).start()
+
+            product(1, j, accs, {})
+            product(2, j, accs, {})
             return carry
 
-        lax.fori_loop(1, n, rest, 0)
+        lax.fori_loop(start, n, rest, 0)
 
     pl.run_scoped(body, *[pltpu.ACC(q)((size, 256), F32) for q in range(2) for size in (sizes[0], sizes[0], sizes[-1])])
     put_all(0, n - 1).wait()
@@ -515,8 +532,8 @@
         in_specs=[any_] * 6,
         out_specs=(any_,) * 3,
         scratch_shapes=[pltpu.VMEM((ff, tall), BF16)] * 3 + [pltpu.VMEM((2, tall, nb), BF16)] * 2
-        + [pltpu.VMEM((k, ff, nb), F32) for k in (1, 1, 2)] + [pltpu.VMEM((nb // 512, ff, 512), F32)]
-        + [sem((4,)), sem((2, 2)), sem((2, 2)), sem((3, 2)), sem((2,)), sem((2,))],
+        + [pltpu.VMEM((k, ff, nb), F32) for k in (1, 1, 2)] + [pltpu.VMEM((DOWN, ff, 512), F32)]
+        + [sem((4,)), sem((2, 2)), sem((2, 2)), sem((3, 2)), sem((DOWN,)), sem((DOWN,))],
         compiler_params=pltpu.CompilerParams(vmem_limit_bytes=54 * 2 ** 20),
         cost_estimate=pl.CostEstimate(flops=6 * ff * tall * hid, bytes_accessed=12 * ff * hid, transcendentals=0),
         name="weight_grads",

time: 124 us -> 126 us (1.016)
  Pallas kernels: 118 us -> 120 us
    pallas_call x1, Pallas kernels: 81.4 us -> 86.1 us  [local_backward(): pl.pallas_call(_comm_kernel, out_shape=(own, own, own, rest, act, act, ac...]
    pallas_call x1, Pallas kernels: 36.7 us -> 33.9 us  [_weight_grads(): pl.pallas_call(_weight_kernel, out_shape=(jax.ShapeDtypeStruct((ff, hid),...]
  transfers between devices with their start and end apart: 3 -> 3, of which waited for: 0 -> 0; matrix products, arithmetic and copies ran while one was open for 0% -> 0% of each run, Pallas kernels for 30% -> 27%
where the time goes in v10:
time: 126 us
  Pallas kernels  120 us (95%)
  starting transfers between devices  3.52 us (3%)
  other arithmetic  1.49 us (1%)
    pallas_call x1, Pallas kernels, local_backward(): pl.pallas_call(_comm_kernel, out_shape=(own, own, own, rest, act, act, ac...  86.1 us
    pallas_call x1, Pallas kernels, _weight_grads(): pl.pallas_call(_weight_kernel, out_shape=(jax.ShapeDtypeStruct((ff, hid),...  33.9 us
    ppermute x3, starting transfers between devices, to(): return lax.ppermute(v, 'tp', [(i, i ^ flip) for i in range(8)])  3.52 us
  transfers between devices with their start and end apart: 3, of which 0 were waited for; matrix products, arithmetic and copies ran while one was open for 0% of the time, Pallas kernels for 27%

profile of v10, /device:TPU:0, one launch (start us, length us, event | category | flops | bytes accessed | tf_op | source)
XLA Modules:
  0.0 125.7 jit_solution(11746524518997294899)
XLA Ops:
  0.6 86.1 %gather_partial.1 = (bf16[128,4096]{1,0:T(8,128)(2,1)}, bf16[128,4096]{1,0:T(8,128)(2,1)}, bf16[128,4096]{1,0:T(8,128)(2,1)}, bf16[128,1024]{1,0:T(8,128)(2,1)},...) custom-call(bf16[128,4096]{1,0:T(8,128)(2,1)} %x_ref.1, ...), custom_call_target="tpu_custom_call" | custom-call | tf_op jit(solution)/shard_map/gather_partial/pallas_call | solution.py:556
  86.7 1.5 %collective-permute-start.2 = (bf16[128,1024]{1,0:T(8,128)(2,1)}, bf16[128,1024]{1,0:T(8,128)(2,1)S(1)}, u32[]{:S(2)}, u32[]{:S(2)}) collective-permute-start(bf16[128,1024]{1,0:T(8,128)(2,1)} %get-tuple-element.26), channel_id=1, source_target_pairs={{0,6},{1,7},{2,4},{3,5},{4,2},{5,3},{6,0},{7,1},{8,14},{9,15},{10,... | collective-permute-start | bytes 786440 | tf_op jit(solution)/shard_map/ppermute | solution.py:586
  88.2 0.5 collective-permute-start
  88.8 1.5 %collective-permute-start.1 = (bf16[128,4096]{1,0:T(8,128)(2,1)}, bf16[128,4096]{1,0:T(8,128)(2,1)S(1)}, u32[]{:S(2)}, u32[]{:S(2)}) collective-permute-start(bf16[128,4096]{1,0:T(8,128)(2,1)} %get-tuple-element.25), channel_id=1, source_target_pairs={{0,4},{1,5},{2,6},{3,7},{4,0},{5,1},{6,2},{7,3},{8,12},{9,13},{10,... | collective-permute-start | bytes 3145736 | tf_op jit(solution)/shard_map/ppermute | solution.py:586
  90.2 0.0 copy-start
  90.2 33.9 %weight_grads.1 = (f32[1376,4096]{1,0:T(8,128)}, f32[1376,4096]{1,0:T(8,128)}, f32[1376,4096]{1,0:T(8,128)}) custom-call(bf16[1376,1024]{1,0:T(8,128)(2,1)} %get-tuple-element.27.zt_ref, bf16[1376,1024]{1,0:T(8,128)(2,1)} %get-tuple-element.28.dgt_ref, bf16[1376,1024]{1,0:T(8,128)(2,1)} %get-tuple-element.29.dut_ref, bf16[1024,4096]{1,0:T(8,128)(2,1)} %bitcast.12, ...), custom_call_target="tpu_custom_call" | custom-call | flops 34628173824 | bytes 67633152 | tf_op jit(solution)/shard_map/weight_grads/pallas_call | solution.py:529
  124.2 0.0 collective-permute-done.2
  124.2 0.0 collective-permute-done
  124.2 0.0 collective-permute-done.1
  124.2 0.0 copy-done
  124.2 1.5 %add_convert_fusion = bf16[128,4096]{1,0:T(8,128)(2,1)} fusion(bf16[128,4096]{1,0:T(8,128)(2,1)S(1)} %collective-permute-done.1, bf16[128,4096]{1,0:T(8,128)(2,1)S(1)} %collective-permute-done, bf16[128,4096]{1,0:T(8,128)(2,1)S(1)} %copy-done, bf16[128,1024]{1,0:T(8,128)(2,1)S(1)} %collective-permute-done.2), kind=kLoop, calls=%fused_computation | loop fusion | flops 4194304 | bytes 4456448 | tf_op jit(solution)/shard_map/convert_element_type | solution.py:593
Async XLA Ops:
  86.7 37.5 %collective-permute-start.2 = (bf16[128,1024]{1,0:T(8,128)(2,1)}, bf16[128,1024]{1,0:T(8,128)(2,1)S(1)}, u32[]{:S(2)}, u32[]{:S(2)}) collective-permute-start(bf16[128,1024]{1,0:T(8,128)(2,1)} %get-tuple-element.26), channel_id=1, source_target_pairs={{0,6},{1,7},{2,4},{3,5},{4,2},{5,3},{6,0},{7,1},{8,14},{9,15},{10,... | collective-permute-start | bytes 786440 | tf_op jit(solution)/shard_map/ppermute | solution.py:586
  88.2 36.0 %collective-permute-start = (bf16[128,4096]{1,0:T(8,128)(2,1)}, bf16[128,4096]{1,0:T(8,128)(2,1)S(1)}, u32[]{:S(2)}, u32[]{:S(2)}) collective-permute-start(bf16[128,4096]{1,0:T(8,128)(2,1)} %get-tuple-element.24), channel_id=1, source_target_pairs={{0,2},{1,3},{2,0},{3,1},{4,6},{5,7},{6,4},{7,5},{8,10},{9,11},{10,... | collective-permute-start | bytes 3145736 | tf_op jit(solution)/shard_map/ppermute | solution.py:586
  88.8 35.4 %collective-permute-start.1 = (bf16[128,4096]{1,0:T(8,128)(2,1)}, bf16[128,4096]{1,0:T(8,128)(2,1)S(1)}, u32[]{:S(2)}, u32[]{:S(2)}) collective-permute-start(bf16[128,4096]{1,0:T(8,128)(2,1)} %get-tuple-element.25), channel_id=1, source_target_pairs={{0,4},{1,5},{2,6},{3,7},{4,0},{5,1},{6,2},{7,3},{8,12},{9,13},{10,... | collective-permute-start | bytes 3145736 | tf_op jit(solution)/shard_map/ppermute | solution.py:586
  90.2 34.0 %copy-start = (bf16[128,4096]{1,0:T(8,128)(2,1)S(1)}, bf16[128,4096]{1,0:T(8,128)(2,1)}, u32[]{:S(2)}) copy-start(bf16[128,4096]{1,0:T(8,128)(2,1)} %get-tuple-element.23) | copy-start | bytes 3145732

commit v11 on v9

--- a/solution.py
+++ b/solution.py
@@ -163,7 +163,7 @@
         spv[:, lanes] = sp.T
         utv[:, lanes] = uu.T.astype(BF16)
 
-    down0 = -(-(fp // 128) // per_h) * per_h
+    down0 = fp // 128
 
     def phase1(i, carry):
         @pl.when((i < NY - AHEAD) & (i % AHEAD == 0))
@@ -213,9 +213,9 @@
             def _():
                 wd_load(k + 2).start()
 
-        @pl.when((i >= down0) & ((i - down0) % per_h == 0) & (i < down0 + DOWN * per_h))
-        def _():
-            k = (i - down0) // per_h
+        @pl.when((i >= down0) & (i < down0 + DOWN))
+        def _():
+            k = i - down0
 
             @pl.when(k >= 2)
             def _():
@@ -458,7 +458,7 @@
         h = len(flat) // 2
         accs = [[part[2] if i == len(sizes) - 1 else part[i % 2] for i in range(len(sizes))]
                 for part in (flat[:h], flat[h:])]
-        product(1, 0, accs, {(0, 0): [gl[0], first[0]], (0, 1): gl[1:], (1, 0): first[1:]})
+        product(1, 0, accs, {(0, 0): [*gl, first[0]], (1, 0): first[1:]})
         product(2, 0, accs, {(0, 0): [ul]})
         zl.wait()
 

time: 124 us -> 124 us (level)
  transfers between devices with their start and end apart: 3 -> 3, of which waited for: 0 -> 0; matrix products, arithmetic and copies ran while one was open for 0% -> 0% of each run, Pallas kernels for 30% -> 29%
where the time goes in v11:
time: 124 us
  Pallas kernels  118 us (95%)
  starting transfers between devices  3.52 us (3%)
  other arithmetic  1.54 us (1%)
    pallas_call x1, Pallas kernels, local_backward(): pl.pallas_call(_comm_kernel, out_shape=(own, own, own, rest, act, act, ac...  81.9 us
    pallas_call x1, Pallas kernels, _weight_grads(): pl.pallas_call(_weight_kernel, out_shape=(jax.ShapeDtypeStruct((ff, hid),...  36.6 us
    ppermute x3, starting transfers between devices, to(): return lax.ppermute(v, 'tp', [(i, i ^ flip) for i in range(8)])  3.52 us
  transfers between devices with their start and end apart: 3, of which 0 were waited for; matrix products, arithmetic and copies ran while one was open for 0% of the time, Pallas kernels for 29%

profile of v11, /device:TPU:0, one launch (start us, length us, event | category | flops | bytes accessed | tf_op | source)
XLA Modules:
  0.0 124.2 jit_solution(2177314806097801381)
XLA Ops:
  0.6 81.9 %gather_partial.1 = (bf16[128,4096]{1,0:T(8,128)(2,1)}, bf16[128,4096]{1,0:T(8,128)(2,1)}, bf16[128,4096]{1,0:T(8,128)(2,1)}, bf16[128,2048]{1,0:T(8,128)(2,1)},...) custom-call(bf16[128,4096]{1,0:T(8,128)(2,1)} %x_ref.1, ...), custom_call_target="tpu_custom_call" | custom-call | tf_op jit(solution)/shard_map/gather_partial/pallas_call | solution.py:539
  82.6 1.5 %collective-permute-start.2 = (bf16[128,2048]{1,0:T(8,128)(2,1)}, bf16[128,2048]{1,0:T(8,128)(2,1)S(1)}, u32[]{:S(2)}, u32[]{:S(2)}) collective-permute-start(bf16[128,2048]{1,0:T(8,128)(2,1)} %get-tuple-element.26), channel_id=1, source_target_pairs={{0,6},{1,7},{2,4},{3,5},{4,2},{5,3},{6,0},{7,1},{8,14},{9,15},{10,... | collective-permute-start | bytes 1572872 | tf_op jit(solution)/shard_map/ppermute | solution.py:569
  84.1 1.0 collective-permute-start
  85.1 1.0 collective-permute-start.1
  86.1 0.0 copy-start
  86.1 36.6 %weight_grads.1 = (f32[1376,4096]{1,0:T(8,128)}, f32[1376,4096]{1,0:T(8,128)}, f32[1376,4096]{1,0:T(8,128)}) custom-call(bf16[1376,1024]{1,0:T(8,128)(2,1)} %get-tuple-element.27.zt_ref, bf16[1376,1024]{1,0:T(8,128)(2,1)} %get-tuple-element.28.dgt_ref, bf16[1376,1024]{1,0:T(8,128)(2,1)} %get-tuple-element.29.dut_ref, bf16[1024,4096]{1,0:T(8,128)(2,1)} %bitcast.12, ...), custom_call_target="tpu_custom_call" | custom-call | flops 34628173824 | bytes 67633152 | tf_op jit(solution)/shard_map/weight_grads/pallas_call | solution.py:512
  122.6 0.0 collective-permute-done.2
  122.7 0.0 collective-permute-done
  122.7 0.0 collective-permute-done.1
  122.7 0.0 copy-done
  122.7 1.5 %add_convert_fusion = bf16[128,4096]{1,0:T(8,128)(2,1)} fusion(bf16[128,4096]{1,0:T(8,128)(2,1)S(1)} %collective-permute-done.1, bf16[128,4096]{1,0:T(8,128)(2,1)S(1)} %collective-permute-done, bf16[128,4096]{1,0:T(8,128)(2,1)S(1)} %copy-done, bf16[128,2048]{1,0:T(8,128)(2,1)S(1)} %collective-permute-done.2), kind=kLoop, calls=%fused_computation | loop fusion | flops 4194304 | bytes 4718592 | tf_op jit(solution)/shard_map/convert_element_type | solution.py:576
Async XLA Ops:
  82.6 40.1 %collective-permute-start.2 = (bf16[128,2048]{1,0:T(8,128)(2,1)}, bf16[128,2048]{1,0:T(8,128)(2,1)S(1)}, u32[]{:S(2)}, u32[]{:S(2)}) collective-permute-start(bf16[128,2048]{1,0:T(8,128)(2,1)} %get-tuple-element.26), channel_id=1, source_target_pairs={{0,6},{1,7},{2,4},{3,5},{4,2},{5,3},{6,0},{7,1},{8,14},{9,15},{10,... | collective-permute-start | bytes 1572872 | tf_op jit(solution)/shard_map/ppermute | solution.py:569
  84.1 38.6 %collective-permute-start = (bf16[128,4096]{1,0:T(8,128)(2,1)}, bf16[128,4096]{1,0:T(8,128)(2,1)S(1)}, u32[]{:S(2)}, u32[]{:S(2)}) collective-permute-start(bf16[128,4096]{1,0:T(8,128)(2,1)} %get-tuple-element.24), channel_id=1, source_target_pairs={{0,2},{1,3},{2,0},{3,1},{4,6},{5,7},{6,4},{7,5},{8,10},{9,11},{10,... | collective-permute-start | bytes 3145736 | tf_op jit(solution)/shard_map/ppermute | solution.py:569
  85.1 37.6 %collective-permute-start.1 = (bf16[128,4096]{1,0:T(8,128)(2,1)}, bf16[128,4096]{1,0:T(8,128)(2,1)S(1)}, u32[]{:S(2)}, u32[]{:S(2)}) collective-permute-start(bf16[128,4096]{1,0:T(8,128)(2,1)} %get-tuple-element.25), channel_id=1, source_target_pairs={{0,4},{1,5},{2,6},{3,7},{4,0},{5,1},{6,2},{7,3},{8,12},{9,13},{10,... | collective-permute-start | bytes 3145736 | tf_op jit(solution)/shard_map/ppermute | solution.py:569
  86.1 36.6 %copy-start = (bf16[128,4096]{1,0:T(8,128)(2,1)S(1)}, bf16[128,4096]{1,0:T(8,128)(2,1)}, u32[]{:S(2)}) copy-start(bf16[128,4096]{1,0:T(8,128)(2,1)} %get-tuple-element.23) | copy-start | bytes 3145732
